TPU v7x, 128 devices: a whole 4x4x4 slice. The times are simulated.
128 devices in a mesh: rep: 1, ep: 16 (over z, y), fsdp: 8 (over x, core).
Axes of the slice: x: 4, y: 4, z: 4, core: 2. Of those that a mesh axis runs over, the one named last changes fastest.
Arguments:
- x: bfloat16 [32768, 4096], P(('rep', 'ep', 'fsdp'))
- norm_w: float32 [2, 4096], replicated
- router_w: bfloat16 [2, 4096, 16], replicated
- w_gate: bfloat16 [2, 16, 4096, 688], P(None, 'ep', None, 'fsdp')
- w_up: bfloat16 [2, 16, 4096, 688], P(None, 'ep', None, 'fsdp')
- w_down: bfloat16 [2, 16, 688, 4096], P(None, 'ep', 'fsdp')
- expert_idx: int32 [2, 32768, 4], P(None, ('rep', 'ep', 'fsdp'))
Outputs:
- output: bfloat16 [32768, 4096], P(('rep', 'ep', 'fsdp'))
All inputs are finite; a program needn't handle non-finite values.
Results may differ from a plain program's by a relative error of at most 0.0054561.
Values are sent between devices in bfloat16 or wider.
A program may use at most 1 GiB of HBM per device.

v0:
```python
import jax
import jax.numpy as jnp
from jax import lax
from jax.sharding import PartitionSpec as P

NORM_EPS = 1e-5


def rms_norm(x, norm_w):
    x_f32 = x.astype(jnp.float32)
    return (x_f32 * lax.rsqrt(jnp.mean(x_f32 * x_f32, axis=-1, keepdims=True) + NORM_EPS) * norm_w).astype(jnp.bfloat16)


def route_gates(normed, router_w, expert_idx):
    logits = jnp.dot(normed, router_w, preferred_element_type=jnp.float32)
    return jax.nn.softmax(jnp.take_along_axis(logits, expert_idx, axis=-1), axis=-1)


def routed_ffn(normed, gate_wts, expert_idx, w_gate, w_up, w_down):
    tok_count, top_k = expert_idx.shape
    experts = w_gate.shape[0]
    flat_ids = expert_idx.reshape(-1)
    sort_order = jnp.argsort(flat_ids, stable=True)
    tok_rows = jnp.take(normed, sort_order // top_k, axis=0)
    group_sizes = jnp.bincount(flat_ids, length=experts).astype(jnp.int32)
    gate_proj = lax.ragged_dot(tok_rows, w_gate, group_sizes, preferred_element_type=jnp.float32)
    up_proj = lax.ragged_dot(tok_rows, w_up, group_sizes, preferred_element_type=jnp.float32)
    hidden_act = (jax.nn.silu(gate_proj) * up_proj).astype(jnp.bfloat16)
    sorted_out = lax.ragged_dot(hidden_act, w_down, group_sizes, preferred_element_type=jnp.float32)
    slot_pos = jnp.zeros_like(sort_order).at[sort_order].set(jnp.arange(sort_order.shape[0], dtype=sort_order.dtype))
    slot_out = jnp.take(sorted_out, slot_pos, axis=0).reshape(tok_count, top_k, -1)
    return jnp.sum(gate_wts[:, :, None] * slot_out, axis=1)


def solution(mesh):
    tok_spec = P(("rep", "ep", "fsdp"), None)
    idx_spec = P(None, ("rep", "ep", "fsdp"), None)
    in_specs = (tok_spec, P(None, None), P(None, None, None), P(None, "ep", None, "fsdp"), P(None, "ep", None, "fsdp"), P(None, "ep", "fsdp", None), idx_spec)

    def local_program(x, norm_w, router_w, w_gate, w_up, w_down, expert_idx):
        for layer_num in range(norm_w.shape[0]):
            full_gate = lax.all_gather(lax.all_gather(w_gate[layer_num], "fsdp", axis=2, tiled=True), "ep", axis=0, tiled=True)
            full_up = lax.all_gather(lax.all_gather(w_up[layer_num], "fsdp", axis=2, tiled=True), "ep", axis=0, tiled=True)
            full_down = lax.all_gather(lax.all_gather(w_down[layer_num], "fsdp", axis=1, tiled=True), "ep", axis=0, tiled=True)
            normed = rms_norm(x, norm_w[layer_num])
            gate_wts = route_gates(normed, router_w[layer_num], expert_idx[layer_num])
            mixed = routed_ffn(normed, gate_wts, expert_idx[layer_num], full_gate, full_up, full_down)
            x = (x.astype(jnp.float32) + mixed).astype(jnp.bfloat16)
        return x

    return jax.shard_map(local_program, mesh=mesh, in_specs=in_specs, out_specs=tok_spec, check_vma=False)
```

profile of v0, /device:TPU:1, one launch (start us, length us, event | category | flops | bytes accessed | tf_op | source)
XLA Modules:
  0.0 3452.8 jit_solution(7536059839814226082)
XLA Ops:
  6.5 7.5 slice_bitcast_fusion.2
  14.2 4.9 slice_bitcast_fusion.1
  19.2 4.9 slice_bitcast_fusion
  26.2 53.4 %all-gather.25.cloned.1.call-done = bf16[1,1,4096,688]{2,1,0,3:T(2,128)(2,1)} async-done(((bf16[1,1,4096,86]{2,1,0,3:T(2,128)(2,1)}), bf16[1,1,4096,688]{2,1,0,3:T(2,128)(2,1)}) %all-gather.25.cloned.1.call-update) | async-done | bytes 5636112 | tf_op jit(solution)/shard_map/all_gather | solution.py:42
  79.6 13.0 copy.26
  93.2 50.2 %all-gather.29.cloned.1.call-done = bf16[1,1,4096,688]{2,1,0,3:T(2,128)(2,1)} async-done(((bf16[1,1,4096,86]{2,1,0,3:T(2,128)(2,1)}), bf16[1,1,4096,688]{2,1,0,3:T(2,128)(2,1)}) %all-gather.29.cloned.1.call-update) | async-done | bytes 5636112 | tf_op jit(solution)/shard_map/all_gather | solution.py:43
  143.4 13.0 copy.29
  156.7 50.6 %all-gather.33.cloned.1.call-done = bf16[1,1,688,4096]{3,1,0,2:T(2,128)(2,1)} async-done(((bf16[1,1,86,4096]{3,1,0,2:T(2,128)(2,1)}), bf16[1,1,688,4096]{3,1,0,2:T(2,128)(2,1)}) %all-gather.33.cloned.1.call-update) | async-done | bytes 5636112 | tf_op jit(solution)/shard_map/all_gather | solution.py:44
  207.2 13.1 copy.32
  220.6 50.3 %all-gather.37.cloned.1.call-done = bf16[1,1,4096,688]{2,1,0,3:T(2,128)(2,1)} async-done(((bf16[1,1,4096,86]{2,1,0,3:T(2,128)(2,1)}), bf16[1,1,4096,688]{2,1,0,3:T(2,128)(2,1)}) %all-gather.37.cloned.1.call-update) | async-done | bytes 5636112 | tf_op jit(solution)/shard_map/all_gather | solution.py:42
  270.9 13.1 copy.35
  284.3 50.3 %all-gather.41.cloned.1.call-done = bf16[1,1,4096,688]{2,1,0,3:T(2,128)(2,1)} async-done(((bf16[1,1,4096,86]{2,1,0,3:T(2,128)(2,1)}), bf16[1,1,4096,688]{2,1,0,3:T(2,128)(2,1)}) %all-gather.41.cloned.1.call-update) | async-done | bytes 5636112 | tf_op jit(solution)/shard_map/all_gather | solution.py:43
  334.6 13.0 copy.38
  348.1 50.1 %all-gather.45.cloned.1.call-done = bf16[1,1,688,4096]{3,1,0,2:T(2,128)(2,1)} async-done(((bf16[1,1,86,4096]{3,1,0,2:T(2,128)(2,1)}), bf16[1,1,688,4096]{3,1,0,2:T(2,128)(2,1)}) %all-gather.45.cloned.1.call-update) | async-done | bytes 5636112 | tf_op jit(solution)/shard_map/all_gather | solution.py:44
  398.2 13.0 copy.41
  411.2 0.7 copy-done.20
  412.3 8.1 scatter_custom_fusion
  420.5 2.0 ragged-dot-metadata.1
  422.6 4.4 sort.31
  428.1 2.2 fusion.2
  430.4 7.6 gather_fusion.1
  438.7 8.7 gather_fusion
  447.8 0.7 reshape.189
  448.6 8.1 scatter_custom_fusion.2
  456.8 1.8 ragged-dot-metadata
  458.6 4.3 scatter_custom_fusion.1
  462.9 4.4 sort.32
  467.9 4.3 scatter_custom_fusion.3
  475.4 0.8 fusion.14
  476.3 7.4 broadcast_select_fusion.3
  483.7 402.6 %all-gather.27.cloned.1.call-done = bf16[16,1,4096,688]{2,3,1,0:T(8,128)(2,1)} async-done(((bf16[1,1,4096,688]{2,3,1,0:T(8,128)(2,1)}), bf16[16,1,4096,688]{2,3,1,0:T(8,128)(2,1)}) %all-gather.27.cloned.1.call-update) | async-done | bytes 90177552 | tf_op jit(solution)/shard_map/all_gather | solution.py:42
  886.3 116.4 %copy.27 = bf16[16,1,4096,688]{3,2,0,1:T(8,128)(2,1)} copy(bf16[16,1,4096,688]{2,3,1,0:T(8,128)(2,1)} %all-gather.27.cloned.1.call-done) | data formatting | bytes 180355072 | tf_op jit(solution)/shard_map/all_gather | solution.py:42
  1002.7 371.5 %all-gather.31.cloned.1.call-done = bf16[16,1,4096,688]{2,3,1,0:T(8,128)(2,1)} async-done(((bf16[1,1,4096,688]{2,3,1,0:T(8,128)(2,1)}), bf16[16,1,4096,688]{2,3,1,0:T(8,128)(2,1)}) %all-gather.31.cloned.1.call-update) | async-done | bytes 90177552 | tf_op jit(solution)/shard_map/all_gather | solution.py:43
  1374.2 112.8 %copy.30 = bf16[16,1,4096,688]{3,2,0,1:T(8,128)(2,1)} copy(bf16[16,1,4096,688]{2,3,1,0:T(8,128)(2,1)} %all-gather.31.cloned.1.call-done) | data formatting | bytes 180355072 | tf_op jit(solution)/shard_map/all_gather | solution.py:43
  1486.9 50.2 %ragged-dot-none.5 = f32[1024,688]{1,0:T(8,128)} custom-call(s32[1]{0:T(128)} %get-tuple-element.24, s32[17]{0:T(128)} %get-tuple-element.25, s32[19]{0:T(128)} %get-tuple-element.26, s32[19]{0:T(128)} %get-tuple-element.27, s32[1]{0:T(128)} %get-tuple-element.24, bf16[1024,4096]{1,0:T(8,128)(2,1)} %broadcast_select_fusion.3, bf16[16,4096,688]{2,1,0:T(8,128)(2,1)} %bitcast.4), custom_call_target="tpu_custom_call" | custom-call | flops 5771362304 | bytes 101384256 | tf_op jit(solution)/shard_map/ragged_dot_general/ragged-dot-none
  1537.2 50.8 %ragged-dot-none.4 = f32[1024,688]{1,0:T(8,128)} custom-call(s32[1]{0:T(128)} %get-tuple-element.24, s32[17]{0:T(128)} %get-tuple-element.25, s32[19]{0:T(128)} %get-tuple-element.26, s32[19]{0:T(128)} %get-tuple-element.27, s32[1]{0:T(128)} %get-tuple-element.24, bf16[1024,4096]{1,0:T(8,128)(2,1)} %broadcast_select_fusion.3, bf16[16,4096,688]{2,1,0:T(8,128)(2,1)} %bitcast.5), custom_call_target="tpu_custom_call" | custom-call | flops 5771362304 | bytes 101384256 | tf_op jit(solution)/shard_map/ragged_dot_general/ragged-dot-none
  1588.0 3.9 multiply_convert_fusion.1
  1591.9 270.2 %all-gather.35.cloned.1.call-done = bf16[16,1,688,4096]{3,2,1,0:T(8,128)(2,1)} async-done(((bf16[1,1,688,4096]{3,2,1,0:T(8,128)(2,1)}), bf16[16,1,688,4096]{3,2,1,0:T(8,128)(2,1)}) %all-gather.35.cloned.1.call-update) | async-done | bytes 90177552 | tf_op jit(solution)/shard_map/all_gather | solution.py:44
  1862.1 52.3 %ragged-dot-none.3 = f32[1024,4096]{1,0:T(8,128)} custom-call(s32[1]{0:T(128)} %get-tuple-element.24, s32[17]{0:T(128)} %get-tuple-element.25, s32[19]{0:T(128)} %get-tuple-element.26, s32[19]{0:T(128)} %get-tuple-element.27, s32[1]{0:T(128)} %get-tuple-element.24, bf16[1024,688]{1,0:T(8,128)(2,1)} %multiply_convert_fusion.1, bf16[16,688,4096]{2,1,0:T(8,128)(2,1)} %bitcast.6), custom_call_target="tpu_custom_call" | custom-call | flops 5771362304 | bytes 108363840 | tf_op jit(solution)/shard_map/ragged_dot_general/ragged-dot-none
  1914.4 20.4 gather_fusion.2
  1934.8 12.0 broadcast_select_fusion.1
  1946.8 19.0 reshape.70
  1965.8 14.3 multiply_reduce_fusion.1
  1980.1 0.8 fusion.4
  1981.0 1.3 copy-done.3
  1983.0 0.6 fusion.8
  1983.6 8.6 gather_fusion.3
  1992.4 7.7 gather_fusion.4
  2000.1 349.7 %all-gather.39.cloned.1.call-done = bf16[16,1,4096,688]{2,3,1,0:T(8,128)(2,1)} async-done(((bf16[1,1,4096,688]{2,3,1,0:T(8,128)(2,1)}), bf16[16,1,4096,688]{2,3,1,0:T(8,128)(2,1)}) %all-gather.39.cloned.1.call-update) | async-done | bytes 90177552 | tf_op jit(solution)/shard_map/all_gather | solution.py:42
  2349.8 112.8 %copy.36 = bf16[16,1,4096,688]{3,2,0,1:T(8,128)(2,1)} copy(bf16[16,1,4096,688]{2,3,1,0:T(8,128)(2,1)} %all-gather.39.cloned.1.call-done) | data formatting | bytes 180355072 | tf_op jit(solution)/shard_map/all_gather | solution.py:42
  2462.6 375.1 %all-gather.43.cloned.1.call-done = bf16[16,1,4096,688]{2,3,1,0:T(8,128)(2,1)} async-done(((bf16[1,1,4096,688]{2,3,1,0:T(8,128)(2,1)}), bf16[16,1,4096,688]{2,3,1,0:T(8,128)(2,1)}) %all-gather.43.cloned.1.call-update) | async-done | bytes 90177552 | tf_op jit(solution)/shard_map/all_gather | solution.py:43
  2837.7 116.4 %copy.39 = bf16[16,1,4096,688]{3,2,0,1:T(8,128)(2,1)} copy(bf16[16,1,4096,688]{2,3,1,0:T(8,128)(2,1)} %all-gather.43.cloned.1.call-done) | data formatting | bytes 180355072 | tf_op jit(solution)/shard_map/all_gather | solution.py:43
  2954.5 0.8 fusion.16
  2955.3 7.5 broadcast_select_fusion.2
  2962.8 50.5 %ragged-dot-none.2 = f32[1024,688]{1,0:T(8,128)} custom-call(s32[1]{0:T(128)} %get-tuple-element.12, s32[17]{0:T(128)} %get-tuple-element.13, s32[19]{0:T(128)} %get-tuple-element.14, s32[19]{0:T(128)} %get-tuple-element.15, s32[1]{0:T(128)} %get-tuple-element.12, bf16[1024,4096]{1,0:T(8,128)(2,1)} %broadcast_select_fusion.2, bf16[16,4096,688]{2,1,0:T(8,128)(2,1)} %bitcast.11), custom_call_target="tpu_custom_call" | custom-call | flops 5771362304 | bytes 101384256 | tf_op jit(solution)/shard_map/ragged_dot_general/ragged-dot-none
  3013.3 50.5 %ragged-dot-none.1 = f32[1024,688]{1,0:T(8,128)} custom-call(s32[1]{0:T(128)} %get-tuple-element.12, s32[17]{0:T(128)} %get-tuple-element.13, s32[19]{0:T(128)} %get-tuple-element.14, s32[19]{0:T(128)} %get-tuple-element.15, s32[1]{0:T(128)} %get-tuple-element.12, bf16[1024,4096]{1,0:T(8,128)(2,1)} %broadcast_select_fusion.2, bf16[16,4096,688]{2,1,0:T(8,128)(2,1)} %bitcast.12), custom_call_target="tpu_custom_call" | custom-call | flops 5771362304 | bytes 101384256 | tf_op jit(solution)/shard_map/ragged_dot_general/ragged-dot-none
  3063.7 3.9 multiply_convert_fusion
  3067.7 257.8 %all-gather.47.cloned.1.call-done = bf16[16,1,688,4096]{3,2,1,0:T(8,128)(2,1)} async-done(((bf16[1,1,688,4096]{3,2,1,0:T(8,128)(2,1)}), bf16[16,1,688,4096]{3,2,1,0:T(8,128)(2,1)}) %all-gather.47.cloned.1.call-update) | async-done | bytes 90177552 | tf_op jit(solution)/shard_map/all_gather | solution.py:44
  3325.5 52.3 %ragged-dot-none = f32[1024,4096]{1,0:T(8,128)} custom-call(s32[1]{0:T(128)} %get-tuple-element.12, s32[17]{0:T(128)} %get-tuple-element.13, s32[19]{0:T(128)} %get-tuple-element.14, s32[19]{0:T(128)} %get-tuple-element.15, s32[1]{0:T(128)} %get-tuple-element.12, bf16[1024,688]{1,0:T(8,128)(2,1)} %multiply_convert_fusion, bf16[16,688,4096]{2,1,0:T(8,128)(2,1)} %bitcast.13), custom_call_target="tpu_custom_call" | custom-call | flops 5771362304 | bytes 108363840 | tf_op jit(solution)/shard_map/ragged_dot_general/ragged-dot-none
  3377.8 20.4 gather_fusion.5
  3398.2 12.0 broadcast_select_fusion
  3410.2 19.0 reshape.71
  3429.3 14.3 multiply_reduce_fusion
  3443.5 2.0 fusion.7
  (107 shorter events, 12.0 us)
Async XLA Ops:
  6.5 7.6 copy-start.9
  6.5 73.1 %all-gather.25.cloned.1.call-start = ((), (), s32[]{:S(2)}) async-start(), calls=%async_computation | async-start | bytes 12681216 | tf_op jit(solution)/shard_map/all_gather | solution.py:42
  14.1 5.1 copy-start.10
  14.1 129.3 %all-gather.29.cloned.1.call-start = ((), (), s32[]{:S(2)}) async-start(), calls=%async_computation.2 | async-start | bytes 12681216 | tf_op jit(solution)/shard_map/all_gather | solution.py:43
  19.1 188.1 %all-gather.33.cloned.1.call-start = ((), (), s32[]{:S(2)}) async-start(), calls=%async_computation.4 | async-start | bytes 12681216 | tf_op jit(solution)/shard_map/all_gather | solution.py:44
  24.1 246.8 %all-gather.37.cloned.1.call-start = ((), (), s32[]{:S(2)}) async-start(), calls=%async_computation.6 | async-start | bytes 12681216 | tf_op jit(solution)/shard_map/all_gather | solution.py:42
  24.7 309.8 %all-gather.41.cloned.1.call-start = ((), (), s32[]{:S(2)}) async-start(), calls=%async_computation.8 | async-start | bytes 12681216 | tf_op jit(solution)/shard_map/all_gather | solution.py:43
  25.3 372.9 %all-gather.45.cloned.1.call-start = ((), (), s32[]{:S(2)}) async-start(), calls=%async_computation.10 | async-start | bytes 12681216 | tf_op jit(solution)/shard_map/all_gather | solution.py:44
  25.9 860.4 %all-gather.27.cloned.1.call-start = ((), (), s32[]{:S(2)}) async-start(), calls=%async_computation.1 | async-start | bytes 95813632 | tf_op jit(solution)/shard_map/all_gather | solution.py:42
  92.6 1281.5 %all-gather.31.cloned.1.call-start = ((), (), s32[]{:S(2)}) async-start(), calls=%async_computation.3 | async-start | bytes 95813632 | tf_op jit(solution)/shard_map/all_gather | solution.py:43
  156.4 1705.6 %all-gather.35.cloned.1.call-start = ((), (), s32[]{:S(2)}) async-start(), calls=%async_computation.5 | async-start | bytes 95813632 | tf_op jit(solution)/shard_map/all_gather | solution.py:44
  220.3 2129.5 %all-gather.39.cloned.1.call-start = ((), (), s32[]{:S(2)}) async-start(), calls=%async_computation.7 | async-start | bytes 95813632 | tf_op jit(solution)/shard_map/all_gather | solution.py:42
  284.0 2553.8 %all-gather.43.cloned.1.call-start = ((), (), s32[]{:S(2)}) async-start(), calls=%async_computation.9 | async-start | bytes 95813632 | tf_op jit(solution)/shard_map/all_gather | solution.py:43
  347.6 2977.9 %all-gather.47.cloned.1.call-start = ((), (), s32[]{:S(2)}) async-start(), calls=%async_computation.11 | async-start | bytes 95813632 | tf_op jit(solution)/shard_map/all_gather | solution.py:44
  411.2 0.7 copy-start.20
  411.2 15.8 copy-start.1
  411.2 16.3 copy-start.16
  430.4 7.7 copy-start.13
  447.6 36.1 %copy-start.7 = (s32[1,256,4]{2,1,0:T(8,128)}, s32[1,256,4]{2,1,0:T(8,128)S(1)}, u32[]{:S(2)}) copy-start(s32[1,256,4]{2,1,0:T(8,128)S(1)} %copy.46) | copy-start | bytes 12292
  1537.2 50.8 %copy-start.5 = (f32[1024,688]{1,0:T(8,128)S(1)}, f32[1024,688]{1,0:T(8,128)}, u32[]{:S(2)}) copy-start(f32[1024,688]{1,0:T(8,128)} %ragged-dot-none.5) | copy-start | bytes 8454148
  1862.1 52.3 %copy-start.19 = (s32[1024]{0:T(1024)S(1)}, s32[1024]{0:T(1024)}, u32[]{:S(2)}) copy-start(s32[1024]{0:T(1024)} %fusion.22) | copy-start | bytes 12292
  1914.4 20.4 copy-start.22
  1946.8 19.0 copy-start.11
  1965.8 14.3 copy-start.2
  1980.1 2.2 copy-start.15
  1981.0 1.3 copy-start.3
  1981.0 2.0 copy-start.14
  1981.0 2.6 copy-start
  1983.6 8.8 copy-start.17
  2462.6 491.6 %copy-start.8 = (s32[1,256,4]{2,1,0:T(8,128)S(1)}, s32[1,256,4]{2,1,0:T(8,128)}, u32[]{:S(2)}) copy-start(s32[1,256,4]{2,1,0:T(8,128)} %copy-done.7) | copy-start | bytes 12292
  2462.6 492.7 %copy-start.23 = (pred[1024]{0:T(1024)(128)(4,1)S(1)}, pred[1024]{0:T(1024)(128)(4,1)}, u32[]{:S(2)}) copy-start(pred[1024]{0:T(1024)(128)(4,1)} %compare_and_fusion.1) | copy-start | bytes 3076
  3013.3 50.5 %copy-start.6 = (f32[1024,688]{1,0:T(8,128)S(1)}, f32[1024,688]{1,0:T(8,128)}, u32[]{:S(2)}) copy-start(f32[1024,688]{1,0:T(8,128)} %ragged-dot-none.2) | copy-start | bytes 8454148
  3325.5 52.3 %copy-start.18 = (s32[1024]{0:T(1024)S(1)}, s32[1024]{0:T(1024)}, u32[]{:S(2)}) copy-start(s32[1024]{0:T(1024)} %fusion.23) | copy-start | bytes 12292
  3377.8 20.4 copy-start.21
  3410.2 19.0 copy-start.12
  3429.3 14.3 copy-start.4
Sparse Core Ops, SparseCore 0:
  14.2 65.3 all-gather.24
  81.3 62.0 all-gather.28
  145.1 62.0 all-gather.32
  208.8 62.0 all-gather.36
  272.4 62.0 all-gather.40
  336.1 62.0 all-gather.44
  400.4 485.8 all-gather.26
  888.4 485.6 all-gather.30
  1376.3 485.6 all-gather.34
  1864.1 485.6 all-gather.38
  2352.0 485.6 all-gather.42
  2839.8 485.6 all-gather.46
where the time goes:
time: 3470 us; the launch traced here: 3450 us
  waiting for transfers between devices  2330 us (67%)
  local copies, waits for them, and re-layouts  679 us (20%)
  Pallas kernels  310 us (9%)
  other arithmetic  112 us (3%)
    all_gather x2, waiting for transfers between devices, local_program(): lax.all_gather(lax.all_gather(w_gate[layer_num], 'fsdp', axis=2, tiled=Tr...  752 us
    all_gather x2, waiting for transfers between devices, local_program(): lax.all_gather(lax.all_gather(w_up[layer_num], 'fsdp', axis=2, tiled=True...  747 us
    all_gather x2, waiting for transfers between devices, local_program(): lax.all_gather(lax.all_gather(w_down[layer_num], 'fsdp', axis=1, tiled=Tr...  528 us
    another operation x6, Pallas kernels  307 us
    all_gather x2, local copies, waits for them, and re-layouts, local_program(): lax.all_gather(lax.all_gather(w_up[layer_num], 'fsdp', axis=2, tiled=True...  229 us
    all_gather x2, local copies, waits for them, and re-layouts, local_program(): lax.all_gather(lax.all_gather(w_gate[layer_num], 'fsdp', axis=2, tiled=Tr...  229 us
    all_gather x2, waiting for transfers between devices, local_program(): lax.all_gather(w_gate[layer_num], 'fsdp', axis=2, tiled=True)  104 us
    all_gather x2, waiting for transfers between devices, local_program(): lax.all_gather(w_down[layer_num], 'fsdp', axis=1, tiled=True)  101 us
  transfers between devices with their start and end apart: 12, of which 12 were waited for; matrix products, arithmetic and copies ran while one was open for 21% of the time, Pallas kernels for 7%

commit v1 on v0

v1 whole, which is shorter than its diff:
```python
import functools

import jax
import jax.numpy as jnp
from jax import lax
from jax.experimental import pallas as pl
from jax.experimental.pallas import tpu as pltpu
from jax.sharding import PartitionSpec as P

NORM_EPS = 1e-5
TB = 256
D = 4096
FP = 88
E = 16
K = 4
GROUPS = 4
GROWS = E // GROUPS * 2 * FP
BF = jnp.bfloat16
F32 = jnp.float32


def up_kernel(x_ref, nw_ref, idx_ref, w_hbm, rt_hbm, a_ref, g_ref, wv, h, slots, logits, sems):
    step = pl.program_id(0)

    @pl.when(step == 0)
    def _():
        copies = []
        for g in range(GROUPS):
            copies.append(pltpu.make_async_copy(w_hbm.at[pl.ds(g * GROWS, GROWS)], wv.at[g, pl.ds(0, GROWS)], sems.at[2 * g]))
            copies.append(pltpu.make_async_copy(rt_hbm, wv.at[g, pl.ds(GROWS, E)], sems.at[2 * g + 1]))
        for c in copies:
            c.start()
        for c in copies:
            c.wait()

    for tb in range(2):
        def rows(c, tb=tb):
            if x_ref.shape[0] == 2:
                return x_ref[tb, c]
            return x_ref[c, tb]

        def ssq_body(c, acc):
            xf = rows(c).astype(F32)
            return acc + jnp.sum(xf * xf, axis=0, keepdims=True)

        ssq = lax.fori_loop(0, 8, ssq_body, jnp.zeros((1, TB), F32))
        rstd = lax.rsqrt(ssq * (1.0 / D) + NORM_EPS)

        def h_body(c, carry, tb=tb, rstd=rstd):
            xf = rows(c).astype(F32)
            nw = nw_ref[c]
            nw2 = jnp.concatenate([nw, nw], axis=1)
            h[pl.ds(pl.multiple_of(c * 512, 512), 512), tb * TB:(tb + 1) * TB] = (xf * rstd * nw2).astype(BF)
            return carry

        lax.fori_loop(0, 8, h_body, 0)

    slots[...] = jnp.zeros_like(slots)
    idx = jnp.concatenate([idx_ref[0], idx_ref[1]], axis=1)

    def group(g, carry):
        res = jnp.dot(wv[g], h[...], preferred_element_type=F32)
        logits[...] = res[GROWS:]
        for k in range(E // GROUPS):
            u = res[k * 2 * FP:k * 2 * FP + FP]
            v = res[k * 2 * FP + FP:(k + 1) * 2 * FP]
            act = jax.nn.silu(u) * v
            e = g * (E // GROUPS) + k
            for j in range(K):
                slots[j] = jnp.where(idx[j:j + 1] == e, act, slots[j])
        return carry

    lax.fori_loop(0, GROUPS, group, 0)
    for tb in range(2):
        a_ref[tb] = slots[:, :, tb * TB:(tb + 1) * TB].astype(BF)
    eids = lax.broadcasted_iota(jnp.int32, (E, 2 * TB), 0)
    chosen = idx[0:1] == eids
    for j in range(1, K):
        chosen = jnp.logical_or(chosen, idx[j:j + 1] == eids)
    lg = jnp.where(chosen, logits[...], -jnp.inf)
    ex = jnp.where(chosen, jnp.exp(lg - jnp.max(lg, axis=0, keepdims=True)), 0.0)
    gates = ex / jnp.sum(ex, axis=0, keepdims=True)
    for tb in range(2):
        g_ref[tb] = gates[:, tb * TB:(tb + 1) * TB]


def up_proj(x, nw, idx, w, rt, tok_major):
    if tok_major:
        x_spec = pl.BlockSpec((2, 8, 512, TB), lambda i: (i, 0, 0, 0))
    else:
        x_spec = pl.BlockSpec((8, 2, 512, TB), lambda i: (0, i, 0, 0))
    return pl.pallas_call(
        up_kernel,
        grid=(4,),
        out_shape=(jax.ShapeDtypeStruct((8, K, FP, TB), BF), jax.ShapeDtypeStruct((8, E, TB), F32)),
        in_specs=[
            x_spec,
            pl.BlockSpec((8, 512, 128), lambda i: (0, 0, 0)),
            pl.BlockSpec((2, K, TB), lambda i: (i, 0, 0)),
            pl.BlockSpec(memory_space=pl.ANY),
            pl.BlockSpec(memory_space=pl.ANY),
        ],
        out_specs=(pl.BlockSpec((2, K, FP, TB), lambda i: (i, 0, 0, 0)), pl.BlockSpec((2, E, TB), lambda i: (i, 0, 0))),
        scratch_shapes=[
            pltpu.VMEM((GROUPS, GROWS + E, D), BF),
            pltpu.VMEM((D, 2 * TB), BF),
            pltpu.VMEM((K, FP, 2 * TB), F32),
            pltpu.VMEM((E, 2 * TB), F32),
            pltpu.SemaphoreType.DMA((2 * GROUPS,)),
        ],
        compiler_params=pltpu.CompilerParams(vmem_limit_bytes=60 * 1024 * 1024),
        cost_estimate=pl.CostEstimate(flops=2 * 2832 * D * 2048, bytes_accessed=45_000_000, transcendentals=3_000_000),
        name="up_proj",
    )(x, nw, idx, w, rt)


def down_kernel(a_ref, idx_ref, g_ref, x_ref, wd_ref, o_ref, acc):
    idx = jnp.concatenate([idx_ref[0], idx_ref[1]], axis=1).astype(F32).astype(BF)
    gates = jnp.concatenate([g_ref[0], g_ref[1]], axis=1)
    acc[...] = jnp.zeros_like(acc)
    for e in range(E):
        parts = []
        for tb in range(2):
            sel = jnp.zeros((8 * FP, TB), BF)
            for j in range(K):
                row = idx[j:j + 1, tb * TB:(tb + 1) * TB]
                sel = jnp.where(row == jnp.asarray(e, BF), a_ref[tb, j], sel)
            parts.append(sel)
        out = jnp.dot(wd_ref[e], jnp.concatenate(parts, axis=1), preferred_element_type=F32)
        acc[...] += gates[e:e + 1] * out
    for tb in range(2):
        o_ref[tb] = (x_ref[tb].astype(F32) + acc[:, tb * TB:(tb + 1) * TB]).astype(BF)


def down_proj(a, idx, gates, xs, wd):
    return pl.pallas_call(
        down_kernel,
        grid=(4,),
        out_shape=jax.ShapeDtypeStruct((8, 512, TB), BF),
        in_specs=[
            pl.BlockSpec((2, K, 8 * FP, TB), lambda i: (i, 0, 0, 0)),
            pl.BlockSpec((2, K, TB), lambda i: (i, 0, 0)),
            pl.BlockSpec((2, E, TB), lambda i: (i, 0, 0)),
            pl.BlockSpec((2, 512, TB), lambda i: (i, 0, 0)),
            pl.BlockSpec((E, 512, 8 * FP), lambda i: (0, 0, 0)),
        ],
        out_specs=pl.BlockSpec((2, 512, TB), lambda i: (i, 0, 0)),
        scratch_shapes=[pltpu.VMEM((512, 2 * TB), F32)],
        compiler_params=pltpu.CompilerParams(vmem_limit_bytes=60 * 1024 * 1024),
        cost_estimate=pl.CostEstimate(flops=2 * 704 * 16 * 512 * 2048, bytes_accessed=30_000_000, transcendentals=0),
        name="down_proj",
    )(a, idx, gates, xs, wd)


def solution(mesh):
    tok_spec = P(("rep", "ep", "fsdp"), None)
    idx_spec = P(None, ("rep", "ep", "fsdp"), None)
    in_specs = (tok_spec, P(None, None), P(None, None, None), P(None, "ep", None, "fsdp"), P(None, "ep", None, "fsdp"), P(None, "ep", "fsdp", None), idx_spec)

    def local_program(x, norm_w, router_w, w_gate, w_up, w_down, expert_idx):
        layers = norm_w.shape[0]
        me = lax.axis_index("fsdp")
        ups = []
        for l in range(layers):
            pad = jnp.zeros((FP - 86, D), BF)
            rows = jnp.concatenate([w_gate[l, 0].T, pad, w_up[l, 0].T, pad], axis=0)
            ups.append(lax.all_gather(rows, "ep", axis=0, tiled=True))
        wd = jnp.pad(w_down[:, 0], ((0, 0), (0, FP - 86), (0, 0)))
        wd = lax.all_to_all(wd, "fsdp", split_axis=2, concat_axis=1, tiled=True)
        wd = jnp.swapaxes(wd, 1, 2)
        downs = [lax.all_gather(wd[l], "ep", axis=0, tiled=False) for l in range(layers)]
        xt = x.T.reshape(8, 512, TB)
        xs_all = lax.all_gather(xt, "fsdp", axis=0, tiled=False)
        idx_all = lax.all_gather(jnp.swapaxes(expert_idx, 1, 2), "fsdp", axis=0, tiled=False)
        xs = lax.dynamic_index_in_dim(xs_all, me, axis=1, keepdims=False)
        for l in range(layers):
            nw = jnp.broadcast_to(norm_w[l].reshape(8, 512, 1), (8, 512, 128))
            a, gates = up_proj(xs_all, nw, idx_all[:, l], ups[l], router_w[l].T, l == 0)
            a_all = lax.all_gather(a, "fsdp", axis=2, tiled=True)
            xs = down_proj(a_all, idx_all[:, l], gates, xs, downs[l])
            if l + 1 < layers:
                xs_all = lax.all_gather(xs, "fsdp", axis=0, tiled=False)
        y = lax.all_to_all(xs, "fsdp", split_axis=0, concat_axis=0, tiled=True)
        return y.reshape(D, TB).T

    return jax.shard_map(local_program, mesh=mesh, in_specs=in_specs, out_specs=tok_spec, check_vma=False)
```

time: 3470 us -> 879 us (0.25)
  waiting for transfers between devices: 2330 us -> 479 us
  local copies, waits for them, and re-layouts: 679 us -> 69.3 us
  other arithmetic: 112 us -> 1.84 us
  blocking collectives: 0 us -> 98.2 us
  Pallas kernels: 310 us -> 215 us
    all_gather x12 -> x8, waiting for transfers between devices: 2330 us -> 477 us  [the longest x2 255 us: local_program(): ups.append(lax.all_gather(rows, 'ep', axis=0, tiled=True))]
    all_gather x10 -> x2, local copies, waits for them, and re-layouts: 537 us -> 31.2 us  [local_program(): lax.all_gather(wd[l], 'ep', axis=0, tiled=False)]
    another operation x6 -> x0, Pallas kernels: 307 us -> none
    pallas_call x0 -> x4, Pallas kernels: none -> 215 us  [the longest x2 145 us: up_proj(): pl.pallas_call(up_kernel, grid=(4,), out_shape=(jax.ShapeDtypeStruct((8,...]
    all_to_all x0 -> x2, blocking collectives: none -> 84.4 us  [the longest x1 54.7 us: local_program(): wd = lax.all_to_all(wd, 'fsdp', split_axis=2, concat_axis=1, tiled=True)]
    gather x10 -> x0, local copies, waits for them, and re-layouts: 74.5 us -> none  [the longest x2 40.8 us: routed_ffn(): jnp.take(sorted_out, slot_pos, axis=0).reshape(tok_count, top_k, -1)]
    select_n x6 -> x0, other arithmetic: 39.6 us -> none  [the longest x2 24 us: routed_ffn(): jnp.take(sorted_out, slot_pos, axis=0).reshape(tok_count, top_k, -1)]
    reshape x2 -> x1, local copies, waits for them, and re-layouts: 38 us -> 2.85 us  [local_program(): return y.reshape(D, TB).T]
  transfers between devices with their start and end apart: 12 -> 8, of which waited for: 12 -> 8; matrix products, arithmetic and copies ran while one was open for 21% -> 7% of each run, Pallas kernels for 7% -> 21%
where the time goes in v1:
time: 879 us; the launch traced here: 877 us
  waiting for transfers between devices  479 us (54%)
  Pallas kernels  215 us (24%)
  blocking collectives  98.2 us (11%)
  local copies, waits for them, and re-layouts  69.3 us (8%)
  between operations  13.7 us (2%)
    all_gather x2, waiting for transfers between devices, local_program(): ups.append(lax.all_gather(rows, 'ep', axis=0, tiled=True))  255 us
    pallas_call x2, Pallas kernels, up_proj(): pl.pallas_call(up_kernel, grid=(4,), out_shape=(jax.ShapeDtypeStruct((8,...  145 us
    all_gather x2, waiting for transfers between devices, local_program(): a_all = lax.all_gather(a, 'fsdp', axis=2, tiled=True)  95.2 us
    all_gather x1, waiting for transfers between devices, local_program(): xs_all = lax.all_gather(xs, 'fsdp', axis=0, tiled=False)  86.9 us
    pallas_call x2, Pallas kernels, down_proj(): pl.pallas_call(down_kernel, grid=(4,), out_shape=jax.ShapeDtypeStruct((8,...  69.8 us
    all_to_all x1, blocking collectives, local_program(): wd = lax.all_to_all(wd, 'fsdp', split_axis=2, concat_axis=1, tiled=True)  54.7 us
    all_gather x2, local copies, waits for them, and re-layouts, local_program(): lax.all_gather(wd[l], 'ep', axis=0, tiled=False)  31.2 us
    all_to_all x1, blocking collectives, local_program(): y = lax.all_to_all(xs, 'fsdp', split_axis=0, concat_axis=0, tiled=True)  29.7 us
  transfers between devices with their start and end apart: 8, of which 8 were waited for; matrix products, arithmetic and copies ran while one was open for 7% of the time, Pallas kernels for 21%

profile of v1, /device:TPU:1, one launch (start us, length us, event | category | flops | bytes accessed | tf_op | source)
XLA Modules:
  0.0 877.4 jit_solution(8892046163565235005)
XLA Ops:
  6.5 0.0 all-gather.11.cloned.1.call-start
  6.5 4.1 copy.48
  10.6 0.0 copy-start
  10.6 0.0 all-gather.11.cloned.1.call-update
  10.6 0.0 all-gather.13.cloned.1.call-start
  10.7 1.3 copy-done
  12.0 3.1 fusion.4
  15.1 0.0 copy-start.1
  15.1 1.6 copy_bitcast_fusion
  16.7 0.0 copy-done.1
  16.7 3.4 fusion.3
  20.1 1.5 copy_bitcast_fusion.1
  21.7 1.8 pad_maximum_fusion
  23.5 0.0 copy-start.2
  23.5 0.0 all-gather.13.cloned.1.call-update
  23.6 0.0 all-gather.17.cloned.1.call-start
  23.6 1.3 copy-done.2
  24.9 5.7 copy.52
  30.6 2.2 pad.4
  32.8 54.7 %all_to_all.23 = bf16[2,88,4096]{1,0,2:T(2,128)(2,1)S(1)} all-to-all(bf16[2,88,4096]{1,0,2:T(2,128)(2,1)S(1)} %pad.4), channel_id=1, replica_groups=mesh['rep'=1,'ep'=16,'fsdp'=8] {'fsdp'}, dimensions={2} | all-to-all | bytes 2883584 | tf_op jit(solution)/shard_map/all_to_all | solution.py:169
  87.5 1.5 copy.62
  89.0 0.0 copy-start.4
  89.0 0.0 copy-start.5
  89.0 0.0 copy-start.3
  89.0 1.2 fusion.2
  90.2 0.0 all-gather.17.cloned.1.call-update
  90.3 0.0 all-gather.15.cloned.1.call-start
  90.3 0.0 copy-done.4
  90.3 0.1 slice_reduce_fusion
  90.4 0.0 copy-done.5
  90.4 13.8 %all-gather = s32[16,4,256]{2,1,0:T(4,128)S(1)} all-gather(s32[2,4,256]{2,1,0:T(4,128)S(1)} %bitcast.56), channel_id=2, replica_groups=mesh['rep'=1,'ep'=16,'fsdp'=8] {'fsdp'}, dimensions={0}, use_global_device_ids=true | all-gather | bytes 73728 | tf_op jit(solution)/shard_map/all_gather | solution.py:174
  104.2 0.6 slice_bitcast_fusion.2
  104.9 0.0 copy-done.3
  104.9 0.7 slice_bitcast_fusion
  105.6 16.7 %all-gather.11.cloned.1.call-done.x_ref = bf16[8,8,512,256]{3,2,1,0:T(8,128)(2,1)} async-done(((bf16[1,8,512,256]{3,2,1,0:T(8,128)(2,1)}), bf16[8,8,512,256]{3,2,1,0:T(8,128)(2,1)}) %all-gather.11.cloned.1.call-update) | async-done | bytes 16777232 | tf_op jit(solution)/shard_map/all_gather | solution.py:173
  122.3 145.6 %all-gather.13.cloned.1.call-done.w_hbm = bf16[2816,4096]{1,0:T(8,128)(2,1)} async-done(((bf16[176,4096]{1,0:T(8,128)(2,1)}), bf16[2816,4096]{1,0:T(8,128)(2,1)}) %all-gather.13.cloned.1.call-update) | async-done | bytes 23068688 | tf_op jit(solution)/shard_map/all_gather | solution.py:167
  267.9 1.9 broadcast_in_dim.15.nw_ref
  269.8 72.7 %up_proj.2 = (bf16[8,4,88,256]{3,2,1,0:T(8,128)(2,1)}, f32[8,16,256]{2,1,0:T(8,128)}) custom-call(bf16[8,8,512,256]{3,2,1,0:T(8,128)(2,1)} %all-gather.11.cloned.1.call-done.x_ref, f32[8,512,128]{2,1,0:T(8,128)} %broadcast_in_dim.15.nw_ref, s32[8,4,256]{2,1,0:T(4,128)} %get-tuple-element.24.idx_ref, bf16[2816,4096]{1,0:T(8,128)(2,1)} %all-gather.13.cloned.1.call-done.w_hbm, ...), custom_call_target="tpu_custom_call" | custom-call | flops 47513075712 | bytes 45000000 | tf_op jit(solution)/shard_map/up_proj/pallas_call | solution.py:92
  342.5 0.0 all-gather.15.cloned.1.call-update
  342.5 0.0 all-gather.19.cloned.1.call-start
  342.6 0.5 all-gather.19.cloned.1.call-update
  343.1 0.0 all-gather.25.cloned.1.call-start
  343.2 11.4 %all-gather.17.cloned.1.call-done = bf16[16,512,704]{1,2,0:T(8,128)(2,1)} async-done(((bf16[1,512,704]{1,2,0:T(8,128)(2,1)}), bf16[16,512,704]{1,2,0:T(8,128)(2,1)}) %all-gather.17.cloned.1.call-update) | async-done | bytes 11534352 | tf_op jit(solution)/shard_map/all_gather | solution.py:171
  354.5 15.7 %copy.55.wd_ref = bf16[16,512,704]{2,1,0:T(8,128)(2,1)} copy(bf16[16,512,704]{1,2,0:T(8,128)(2,1)} %all-gather.17.cloned.1.call-done) | data formatting | bytes 23068672 | tf_op jit(solution)/shard_map/all_gather | solution.py:171
  370.3 3.0 dynamic-slice_bitcast_fusion.x_ref
  373.3 45.9 %all-gather.15.cloned.1.call-done.a_ref = bf16[8,4,704,256]{3,2,1,0:T(8,128)(2,1)} async-done(((bf16[8,4,88,256]{3,2,1,0:T(8,128)(2,1)}), bf16[8,4,704,256]{3,2,1,0:T(8,128)(2,1)}) %all-gather.15.cloned.1.call-update) | async-done | bytes 11534352 | tf_op jit(solution)/shard_map/all_gather | solution.py:179
  419.2 34.9 %down_proj.2.x_ref = bf16[8,512,256]{2,1,0:T(8,128)(2,1)} custom-call(bf16[8,4,704,256]{3,2,1,0:T(8,128)(2,1)} %all-gather.15.cloned.1.call-done.a_ref, s32[8,4,256]{2,1,0:T(4,128)} %get-tuple-element.24.idx_ref, f32[8,16,256]{2,1,0:T(8,128)} %get-tuple-element.10.g_ref, bf16[8,512,256]{2,1,0:T(8,128)(2,1)} %dynamic-slice_bitcast_fusion.x_ref, ...), custom_call_target="tpu_custom_call" | custom-call | flops 23622320128 | bytes 30000000 | tf_op jit(solution)/shard_map/down_proj/pallas_call | solution.py:136
  454.1 0.0 all-gather.25.cloned.1.call-update
  454.1 0.0 all-gather.23.cloned.1.call-start
  454.2 0.7 all-gather.23.cloned.1.call-update
  454.9 0.3 all-gather.21.cloned.1.call-start
  455.1 109.3 %all-gather.19.cloned.1.call-done.w_hbm = bf16[2816,4096]{1,0:T(8,128)(2,1)} async-done(((bf16[176,4096]{1,0:T(8,128)(2,1)}), bf16[2816,4096]{1,0:T(8,128)(2,1)}) %all-gather.19.cloned.1.call-update) | async-done | bytes 23068688 | tf_op jit(solution)/shard_map/all_gather | solution.py:167
  564.4 86.9 %all-gather.25.cloned.1.call-done = bf16[64,512,256]{2,1,0:T(8,128)(2,1)} async-done(((bf16[8,512,256]{2,1,0:T(8,128)(2,1)}), bf16[64,512,256]{2,1,0:T(8,128)(2,1)}) %all-gather.25.cloned.1.call-update) | async-done | bytes 16777232 | tf_op jit(solution)/shard_map/all_gather | solution.py:182
  651.4 1.9 broadcast_in_dim.17.nw_ref
  653.3 72.7 %up_proj.3 = (bf16[8,4,88,256]{3,2,1,0:T(8,128)(2,1)}, f32[8,16,256]{2,1,0:T(8,128)}) custom-call(bf16[8,8,512,256]{3,2,1,0:T(8,128)(2,1)} %bitcast.57, f32[8,512,128]{2,1,0:T(8,128)} %broadcast_in_dim.17.nw_ref, s32[8,4,256]{2,1,0:T(4,128)} %get-tuple-element.23.idx_ref, bf16[2816,4096]{1,0:T(8,128)(2,1)} %all-gather.19.cloned.1.call-done.w_hbm, ...), custom_call_target="tpu_custom_call" | custom-call | flops 47513075712 | bytes 45000000 | tf_op jit(solution)/shard_map/up_proj/pallas_call | solution.py:92
  726.0 0.0 all-gather.21.cloned.1.call-update
  726.0 12.4 %all-gather.23.cloned.1.call-done = bf16[16,512,704]{1,2,0:T(8,128)(2,1)} async-done(((bf16[1,512,704]{1,2,0:T(8,128)(2,1)}), bf16[16,512,704]{1,2,0:T(8,128)(2,1)}) %all-gather.23.cloned.1.call-update) | async-done | bytes 11534352 | tf_op jit(solution)/shard_map/all_gather | solution.py:171
  738.4 15.5 %copy.59.wd_ref = bf16[16,512,704]{2,1,0:T(8,128)(2,1)} copy(bf16[16,512,704]{1,2,0:T(8,128)(2,1)} %all-gather.23.cloned.1.call-done) | data formatting | bytes 23068672 | tf_op jit(solution)/shard_map/all_gather | solution.py:171
  753.8 49.3 %all-gather.21.cloned.1.call-done.a_ref = bf16[8,4,704,256]{3,2,1,0:T(8,128)(2,1)} async-done(((bf16[8,4,88,256]{3,2,1,0:T(8,128)(2,1)}), bf16[8,4,704,256]{3,2,1,0:T(8,128)(2,1)}) %all-gather.21.cloned.1.call-update) | async-done | bytes 11534352 | tf_op jit(solution)/shard_map/all_gather | solution.py:179
  803.1 34.9 %down_proj.3 = bf16[8,512,256]{2,1,0:T(8,128)(2,1)} custom-call(bf16[8,4,704,256]{3,2,1,0:T(8,128)(2,1)} %all-gather.21.cloned.1.call-done.a_ref, s32[8,4,256]{2,1,0:T(4,128)} %get-tuple-element.23.idx_ref, f32[8,16,256]{2,1,0:T(8,128)} %get-tuple-element.12.g_ref, bf16[8,512,256]{2,1,0:T(8,128)(2,1)} %down_proj.2.x_ref, bf16[16,512,704]{2,1,0:T(8,128)(2,1)} %copy.59.wd_ref), custom_call_target="tpu_custom_call" | custom-call | flops 23622320128 | bytes 30000000 | tf_op jit(solution)/shard_map/down_proj/pallas_call | solution.py:136
  838.0 29.7 %all_to_all.24 = bf16[8,512,256]{2,1,0:T(8,128)(2,1)S(1)} all-to-all(bf16[8,512,256]{2,1,0:T(8,128)(2,1)} %down_proj.3), channel_id=1, replica_groups=mesh['rep'=1,'ep'=16,'fsdp'=8] {'fsdp'}, dimensions={0} | all-to-all | bytes 4194304 | tf_op jit(solution)/shard_map/all_to_all | solution.py:183
  867.8 2.8 copy.60
  (3 shorter events, 0.0 us)
Async XLA Ops:
  6.5 115.8 %all-gather.11.cloned.1.call-start = ((), (), s32[]{:S(2)}) async-start(), calls=%async_computation.2 | async-start | bytes 18874368 | tf_op jit(solution)/shard_map/all_gather | solution.py:173
  10.6 1.4 copy-start
  10.6 257.3 %all-gather.13.cloned.1.call-start = ((), (), s32[]{:S(2)}) async-start(), calls=%async_computation.3 | async-start | bytes 24510464 | tf_op jit(solution)/shard_map/all_gather | solution.py:167
  15.1 1.6 copy-start.1
  23.5 1.4 copy-start.2
  23.6 331.0 %all-gather.17.cloned.1.call-start = ((), (), s32[]{:S(2)}) async-start(), calls=%async_computation.5 | async-start | bytes 12255232 | tf_op jit(solution)/shard_map/all_gather | solution.py:171
  89.0 1.3 copy-start.4
  89.0 1.4 copy-start.5
  89.0 15.9 %copy-start.3 = (bf16[2,4096,16]{1,2,0:T(8,128)(2,1)S(1)}, bf16[2,4096,16]{1,2,0:T(8,128)(2,1)}, u32[]{:S(2)}) copy-start(bf16[2,4096,16]{1,2,0:T(8,128)(2,1)} %param.9) | copy-start | bytes 786436
  90.3 328.9 %all-gather.15.cloned.1.call-start = ((), (), s32[]{:S(2)}) async-start(), calls=%async_computation.4 | async-start | bytes 12976128 | tf_op jit(solution)/shard_map/all_gather | solution.py:179
  342.5 221.9 %all-gather.19.cloned.1.call-start = ((), (), s32[]{:S(2)}) async-start(), calls=%async_computation.6 | async-start | bytes 24510464 | tf_op jit(solution)/shard_map/all_gather | solution.py:167
  343.1 308.2 %all-gather.25.cloned.1.call-start = ((), (), s32[]{:S(2)}) async-start(), calls=%async_computation.9 | async-start | bytes 18874368 | tf_op jit(solution)/shard_map/all_gather | solution.py:182
  454.1 284.2 %all-gather.23.cloned.1.call-start = ((), (), s32[]{:S(2)}) async-start(), calls=%async_computation.8 | async-start | bytes 12255232 | tf_op jit(solution)/shard_map/all_gather | solution.py:171
  454.9 348.3 %all-gather.21.cloned.1.call-start = ((), (), s32[]{:S(2)}) async-start(), calls=%async_computation.7 | async-start | bytes 12976128 | tf_op jit(solution)/shard_map/all_gather | solution.py:179
Sparse Core Ops, SparseCore 0:
  10.8 111.5 all-gather.10
  124.5 143.3 all-gather.12
  270.0 84.4 all-gather.16
  356.1 63.0 all-gather.14
  421.2 143.1 all-gather.18
  566.0 85.3 all-gather.24
  653.5 84.8 all-gather.22
  740.0 63.0 all-gather.20

commit v2 on v1

--- a/solution.py
+++ b/solution.py
@@ -11,6 +11,7 @@
 TB = 256
 D = 4096
 FP = 88
+KP = 768
 E = 16
 K = 4
 GROUPS = 4
@@ -30,8 +31,6 @@
             copies.append(pltpu.make_async_copy(rt_hbm, wv.at[g, pl.ds(GROWS, E)], sems.at[2 * g + 1]))
         for c in copies:
             c.start()
-        for c in copies:
-            c.wait()
 
     for tb in range(2):
         def rows(c, tb=tb):
@@ -59,6 +58,11 @@
     idx = jnp.concatenate([idx_ref[0], idx_ref[1]], axis=1)
 
     def group(g, carry):
+        @pl.when(step == 0)
+        def _():
+            pltpu.make_async_copy(w_hbm.at[pl.ds(g * GROWS, GROWS)], wv.at[g, pl.ds(0, GROWS)], sems.at[2 * g]).wait()
+            pltpu.make_async_copy(rt_hbm, wv.at[g, pl.ds(GROWS, E)], sems.at[2 * g + 1]).wait()
+
         res = jnp.dot(wv[g], h[...], preferred_element_type=F32)
         logits[...] = res[GROWS:]
         for k in range(E // GROUPS):
@@ -116,18 +120,25 @@
 
 def down_kernel(a_ref, idx_ref, g_ref, x_ref, wd_ref, o_ref, acc):
     idx = jnp.concatenate([idx_ref[0], idx_ref[1]], axis=1).astype(F32).astype(BF)
-    gates = jnp.concatenate([g_ref[0], g_ref[1]], axis=1)
     acc[...] = jnp.zeros_like(acc)
-    for e in range(E):
-        parts = []
-        for tb in range(2):
-            sel = jnp.zeros((8 * FP, TB), BF)
-            for j in range(K):
-                row = idx[j:j + 1, tb * TB:(tb + 1) * TB]
-                sel = jnp.where(row == jnp.asarray(e, BF), a_ref[tb, j], sel)
-            parts.append(sel)
-        out = jnp.dot(wd_ref[e], jnp.concatenate(parts, axis=1), preferred_element_type=F32)
-        acc[...] += gates[e:e + 1] * out
+
+    def group(g, carry):
+        for k in range(E // GROUPS):
+            e = g * (E // GROUPS) + k
+            ef = e.astype(F32).astype(BF)
+            parts = []
+            for tb in range(2):
+                sel = jnp.zeros((8 * FP, TB), BF)
+                for j in range(K):
+                    row = idx[j:j + 1, tb * TB:(tb + 1) * TB]
+                    sel = jnp.where(row == ef, a_ref[tb, j], sel)
+                parts.append(sel)
+            out = jnp.dot(wd_ref[e, :, :8 * FP], jnp.concatenate(parts, axis=1), preferred_element_type=F32)
+            gate = jnp.concatenate([g_ref[0, pl.ds(e, 1)], g_ref[1, pl.ds(e, 1)]], axis=1)
+            acc[...] += gate * out
+        return carry
+
+    lax.fori_loop(0, GROUPS, group, 0)
     for tb in range(2):
         o_ref[tb] = (x_ref[tb].astype(F32) + acc[:, tb * TB:(tb + 1) * TB]).astype(BF)
 
@@ -142,7 +153,7 @@
             pl.BlockSpec((2, K, TB), lambda i: (i, 0, 0)),
             pl.BlockSpec((2, E, TB), lambda i: (i, 0, 0)),
             pl.BlockSpec((2, 512, TB), lambda i: (i, 0, 0)),
-            pl.BlockSpec((E, 512, 8 * FP), lambda i: (0, 0, 0)),
+            pl.BlockSpec((E, 512, KP), lambda i: (0, 0, 0)),
         ],
         out_specs=pl.BlockSpec((2, 512, TB), lambda i: (i, 0, 0)),
         scratch_shapes=[pltpu.VMEM((512, 2 * TB), F32)],
@@ -152,6 +163,223 @@
     )(a, idx, gates, xs, wd)
 
 
+MESH = pl.DeviceIdType.MESH
+CH = 4
+
+
+def ring_position():
+    f = lax.axis_index("fsdp")
+    ring, core = f // 2, f % 2
+
+    def at(step, other=0):
+        c = core if other == 0 else 1 - core
+        return lax.rem(ring + step, 4) * 2 + c
+
+    return f, at
+
+
+def greet(peers):
+    barrier = pltpu.get_barrier_semaphore()
+    for p in peers:
+        pl.semaphore_signal(barrier, inc=1, device_id={"fsdp": p}, device_id_type=MESH)
+    pl.semaphore_wait(barrier, len(peers))
+
+
+def ring_gather(own, place, send_sem, recv_sem):
+    f, at = ring_position()
+    left, right, partner = at(3), at(1), at(0, 1)
+
+    def copy(kind, k, src, owner, target):
+        return pltpu.make_async_remote_copy(
+            src_ref=src, dst_ref=place(owner, k), send_sem=send_sem.at[kind, k], recv_sem=recv_sem.at[kind, k],
+            device_id={"fsdp": target}, device_id_type=MESH)
+
+    sent = []
+
+    def send(kind, k, src, owner, target):
+        c = copy(kind, k, src, owner, target)
+        c.start()
+        sent.append(c)
+
+    def arrived(kind, k, owner):
+        copy(kind, k, place(owner, k), owner, left).wait_recv()
+
+    def start():
+        for k in range(CH):
+            send(0, k, own(k), f, right)
+            send(1, k, own(k), f, left)
+            send(2, k, own(k), f, partner)
+
+    def finish():
+        for k in range(CH):
+            arrived(0, k, at(3))
+            if k < CH // 2:
+                send(3, k, place(at(3), k), at(3), right)
+            send(4, k, place(at(3), k), at(3), partner)
+            arrived(1, k, at(1))
+            if k >= CH // 2:
+                send(3, k, place(at(1), k), at(1), left)
+            send(5, k, place(at(1), k), at(1), partner)
+        for i in range(CH // 2):
+            for k in (i, i + CH // 2):
+                arrived(3, k, at(2))
+                send(6, k, place(at(2), k), at(2), partner)
+        for kind, owner in ((2, at(0, 1)), (4, at(3, 1)), (5, at(1, 1)), (6, at(2, 1))):
+            for k in range(CH):
+                arrived(kind, k, owner)
+        for c in sent:
+            c.wait_send()
+
+    return start, finish
+
+
+RING_SEMS = [pltpu.SemaphoreType.DMA((7, CH)), pltpu.SemaphoreType.DMA((7, CH))]
+
+
+def others(at):
+    return [at(s, o) for s in range(4) for o in range(2) if (s, o) != (0, 0)]
+
+
+def first_kernel(x_ref, idx_ref, wd_ref, x_all, idx_all, wd_all, send_sem, recv_sem, local_sem, psend, precv):
+    f, at = ring_position()
+    peers = [(s, o) for s in range(4) for o in range(2) if (s, o) != (0, 0)]
+    greet(others(at))
+    n = 8 // CH
+    start, finish = ring_gather(lambda k: x_ref.at[pl.ds(k * n, n)], lambda owner, k: x_all.at[owner, pl.ds(k * n, n)], send_sem, recv_sem)
+    locals_ = [
+        pltpu.make_async_copy(x_ref, x_all.at[f], local_sem.at[0]),
+        pltpu.make_async_copy(idx_ref, idx_all.at[f], local_sem.at[1]),
+        pltpu.make_async_copy(wd_ref.at[:, f], wd_all.at[:, f], local_sem.at[2]),
+    ]
+    for c in locals_:
+        c.start()
+    small = []
+    for p, (s, o) in enumerate(peers):
+        small.append(pltpu.make_async_remote_copy(
+            src_ref=idx_ref, dst_ref=idx_all.at[f], send_sem=psend.at[0, p], recv_sem=precv.at[0, p],
+            device_id={"fsdp": at(s, o)}, device_id_type=MESH))
+        small.append(pltpu.make_async_remote_copy(
+            src_ref=wd_ref.at[:, at(s, o)], dst_ref=wd_all.at[:, f], send_sem=psend.at[1, p], recv_sem=precv.at[1, p],
+            device_id={"fsdp": at(s, o)}, device_id_type=MESH))
+    for c in small:
+        c.start()
+    start()
+    finish()
+    for p, (s, o) in enumerate(peers):
+        source = at((4 - s) % 4, o)
+        for kind, (src, dst) in enumerate(((idx_ref, idx_all.at[source]), (wd_ref.at[:, 0], wd_all.at[:, source]))):
+            pltpu.make_async_remote_copy(
+                src_ref=src, dst_ref=dst, send_sem=psend.at[kind, p], recv_sem=precv.at[kind, p],
+                device_id={"fsdp": source}, device_id_type=MESH).wait_recv()
+    for c in small:
+        c.wait_send()
+    for c in locals_:
+        c.wait()
+
+
+def first_exchange(xt, idx, wd):
+    return pl.pallas_call(
+        first_kernel,
+        out_shape=(jax.ShapeDtypeStruct((8, 8, 512, TB), BF), jax.ShapeDtypeStruct((8, 2, K, TB), jnp.int32), jax.ShapeDtypeStruct((2, 8, FP, 512), BF)),
+        in_specs=[pl.BlockSpec(memory_space=pltpu.VMEM)] * 3,
+        out_specs=[pl.BlockSpec(memory_space=pl.ANY)] * 3,
+        scratch_shapes=RING_SEMS + [pltpu.SemaphoreType.DMA((3,)), pltpu.SemaphoreType.DMA((2, 7)), pltpu.SemaphoreType.DMA((2, 7))],
+        compiler_params=pltpu.CompilerParams(collective_id=0, has_side_effects=True),
+        cost_estimate=pl.CostEstimate(flops=70_000_000_000, bytes_accessed=16_000_000, transcendentals=0),
+        name="first_exchange",
+    )(xt, idx, wd)
+
+
+def x_gather_kernel(x_ref, x_all, send_sem, recv_sem, local_sem):
+    f, at = ring_position()
+    greet([at(3), at(1), at(0, 1)])
+    n = 8 // CH
+    start, finish = ring_gather(lambda k: x_ref.at[pl.ds(k * n, n)], lambda owner, k: x_all.at[owner, pl.ds(k * n, n)], send_sem, recv_sem)
+    mine = pltpu.make_async_copy(x_ref, x_all.at[f], local_sem)
+    mine.start()
+    start()
+    finish()
+    mine.wait()
+
+
+def x_gather(xs):
+    return pl.pallas_call(
+        x_gather_kernel,
+        out_shape=jax.ShapeDtypeStruct((8, 8, 512, TB), BF),
+        in_specs=[pl.BlockSpec(memory_space=pltpu.VMEM)],
+        out_specs=pl.BlockSpec(memory_space=pl.ANY),
+        scratch_shapes=RING_SEMS + [pltpu.SemaphoreType.DMA],
+        compiler_params=pltpu.CompilerParams(collective_id=1, has_side_effects=True),
+        cost_estimate=pl.CostEstimate(flops=70_000_000_000, bytes_accessed=16_000_000, transcendentals=0),
+        name="x_gather",
+    )(xs)
+
+
+def a_gather_kernel(a_ref, a_all, send_sem, recv_sem, local_sem):
+    f, at = ring_position()
+    greet([at(3), at(1), at(0, 1)])
+    n = 8 // CH
+
+    def place(owner, k):
+        return a_all.at[pl.ds(k * n, n), :, pl.ds(pl.multiple_of(owner * FP, 8), FP)]
+
+    start, finish = ring_gather(lambda k: a_ref.at[pl.ds(k * n, n)], place, send_sem, recv_sem)
+    mine = pltpu.make_async_copy(a_ref, a_all.at[:, :, pl.ds(pl.multiple_of(f * FP, 8), FP)], local_sem)
+    mine.start()
+    start()
+    finish()
+    mine.wait()
+
+
+def a_gather(a):
+    return pl.pallas_call(
+        a_gather_kernel,
+        out_shape=jax.ShapeDtypeStruct((8, K, 8 * FP, TB), BF),
+        in_specs=[pl.BlockSpec(memory_space=pltpu.VMEM)],
+        out_specs=pl.BlockSpec(memory_space=pl.ANY),
+        scratch_shapes=RING_SEMS + [pltpu.SemaphoreType.DMA],
+        compiler_params=pltpu.CompilerParams(collective_id=2, has_side_effects=True),
+        cost_estimate=pl.CostEstimate(flops=50_000_000_000, bytes_accessed=12_000_000, transcendentals=0),
+        name="a_gather",
+    )(a)
+
+
+def last_kernel(y_ref, o_ref, local_sem, psend, precv):
+    f, at = ring_position()
+    peers = [(s, o) for s in range(4) for o in range(2) if (s, o) != (0, 0)]
+    greet(others(at))
+    mine = pltpu.make_async_copy(y_ref.at[f], o_ref.at[f], local_sem)
+    mine.start()
+    copies = []
+    for p, (s, o) in enumerate(peers):
+        c = pltpu.make_async_remote_copy(
+            src_ref=y_ref.at[at(s, o)], dst_ref=o_ref.at[f], send_sem=psend.at[p], recv_sem=precv.at[p],
+            device_id={"fsdp": at(s, o)}, device_id_type=MESH)
+        c.start()
+        copies.append(c)
+    for p, (s, o) in enumerate(peers):
+        source = at((4 - s) % 4, o)
+        pltpu.make_async_remote_copy(
+            src_ref=y_ref.at[0], dst_ref=o_ref.at[source], send_sem=psend.at[p], recv_sem=precv.at[p],
+            device_id={"fsdp": source}, device_id_type=MESH).wait_recv()
+    for c in copies:
+        c.wait_send()
+    mine.wait()
+
+
+def last_exchange(y):
+    return pl.pallas_call(
+        last_kernel,
+        out_shape=jax.ShapeDtypeStruct((8, 512, TB), BF),
+        in_specs=[pl.BlockSpec(memory_space=pltpu.VMEM)],
+        out_specs=pl.BlockSpec(memory_space=pl.ANY),
+        scratch_shapes=[pltpu.SemaphoreType.DMA, pltpu.SemaphoreType.DMA((7,)), pltpu.SemaphoreType.DMA((7,))],
+        compiler_params=pltpu.CompilerParams(collective_id=3, has_side_effects=True),
+        cost_estimate=pl.CostEstimate(flops=20_000_000_000, bytes_accessed=4_000_000, transcendentals=0),
+        name="last_exchange",
+    )(y)
+
+
 def solution(mesh):
     tok_spec = P(("rep", "ep", "fsdp"), None)
     idx_spec = P(None, ("rep", "ep", "fsdp"), None)
@@ -160,27 +388,31 @@
     def local_program(x, norm_w, router_w, w_gate, w_up, w_down, expert_idx):
         layers = norm_w.shape[0]
         me = lax.axis_index("fsdp")
-        ups = []
-        for l in range(layers):
-            pad = jnp.zeros((FP - 86, D), BF)
-            rows = jnp.concatenate([w_gate[l, 0].T, pad, w_up[l, 0].T, pad], axis=0)
-            ups.append(lax.all_gather(rows, "ep", axis=0, tiled=True))
-        wd = jnp.pad(w_down[:, 0], ((0, 0), (0, FP - 86), (0, 0)))
-        wd = lax.all_to_all(wd, "fsdp", split_axis=2, concat_axis=1, tiled=True)
-        wd = jnp.swapaxes(wd, 1, 2)
-        downs = [lax.all_gather(wd[l], "ep", axis=0, tiled=False) for l in range(layers)]
+        pad = jnp.zeros((FP - 86, D), BF)
+        rows = [jnp.concatenate([w_gate[l, 0].T, pad, w_up[l, 0].T, pad], axis=0) for l in range(layers)]
+        ups = [lax.all_gather(rows[0], "ep", axis=0, tiled=True)]
         xt = x.T.reshape(8, 512, TB)
-        xs_all = lax.all_gather(xt, "fsdp", axis=0, tiled=False)
-        idx_all = lax.all_gather(jnp.swapaxes(expert_idx, 1, 2), "fsdp", axis=0, tiled=False)
+        wd = jnp.pad(w_down[:, 0], ((0, 0), (0, FP - 86), (0, 0))).reshape(layers, FP, 8, 512).swapaxes(1, 2)
+        xt, idx, wd, _ = lax.optimization_barrier((xt, jnp.swapaxes(expert_idx, 1, 2), wd, rows[0]))
+        xs_all, idx_all, wd = first_exchange(xt, idx, wd)
+
+        def gather_down(block):
+            block = jnp.swapaxes(block.reshape(8 * FP, 512), 0, 1)
+            return lax.all_gather(jnp.pad(block, ((0, 0), (0, KP - 8 * FP))), "ep", axis=0, tiled=False)
+
+        downs = [gather_down(wd[0])]
         xs = lax.dynamic_index_in_dim(xs_all, me, axis=1, keepdims=False)
         for l in range(layers):
             nw = jnp.broadcast_to(norm_w[l].reshape(8, 512, 1), (8, 512, 128))
             a, gates = up_proj(xs_all, nw, idx_all[:, l], ups[l], router_w[l].T, l == 0)
-            a_all = lax.all_gather(a, "fsdp", axis=2, tiled=True)
-            xs = down_proj(a_all, idx_all[:, l], gates, xs, downs[l])
             if l + 1 < layers:
-                xs_all = lax.all_gather(xs, "fsdp", axis=0, tiled=False)
-        y = lax.all_to_all(xs, "fsdp", split_axis=0, concat_axis=0, tiled=True)
-        return y.reshape(D, TB).T
+                nxt, _ = lax.optimization_barrier((rows[l + 1], a))
+                ups.append(lax.all_gather(nxt, "ep", axis=0, tiled=True))
+            xs = down_proj(a_gather(a), idx_all[:, l], gates, xs, downs[l])
+            if l + 1 < layers:
+                nxt, _ = lax.optimization_barrier((wd[l + 1], xs))
+                downs.append(gather_down(nxt))
+                xs_all = x_gather(xs)
+        return last_exchange(xs).reshape(D, TB).T
 
     return jax.shard_map(local_program, mesh=mesh, in_specs=in_specs, out_specs=tok_spec, check_vma=False)

time: 879 us -> 610 us (0.69)
  waiting for transfers between devices: 479 us -> 38.5 us
  Pallas kernels: 215 us -> 519 us
  blocking collectives: 98.2 us -> 0 us
  local copies, waits for them, and re-layouts: 69.3 us -> 36.2 us
    all_gather x8 -> x4, waiting for transfers between devices: 477 us -> 38.4 us  [the longest x1 38.3 us: local_program(): ups = [lax.all_gather(rows[0], 'ep', axis=0, tiled=True)]]
    pallas_call x0 -> x5, Pallas kernels: none -> 309 us  [the longest x2 109 us: a_gather(): pl.pallas_call(a_gather_kernel, out_shape=jax.ShapeDtypeStruct((8, K, 8 *...]
    all_to_all x2 -> x0, blocking collectives: 84.4 us -> none  [the longest x1 54.7 us: local_program(): wd = lax.all_to_all(wd, 'fsdp', split_axis=2, concat_axis=1, tiled=True)]
    all_gather x2 -> x0, local copies, waits for them, and re-layouts: 31.2 us -> none  [local_program(): lax.all_gather(wd[l], 'ep', axis=0, tiled=False)]
    all_gather x1 -> x0, blocking collectives: 13.8 us -> none  [local_program(): lax.all_gather(jnp.swapaxes(expert_idx, 1, 2), 'fsdp', axis=0, tiled=False)]
    pallas_call x2, Pallas kernels: 145 us -> 134 us  [up_proj(): pl.pallas_call(up_kernel, grid=(4,), out_shape=(jax.ShapeDtypeStruct((8,...]
  transfers between devices with their start and end apart: 8 -> 4, of which waited for: 8 -> 1; matrix products, arithmetic and copies ran while one was open for 7% -> 3% of each run, Pallas kernels for 21% -> 74%
where the time goes in v2:
time: 610 us; the launch traced here: 609 us
  Pallas kernels  519 us (85%)
  waiting for transfers between devices  38.5 us (6%)
  local copies, waits for them, and re-layouts  36.2 us (6%)
  between operations  13.4 us (2%)
    pallas_call x2, Pallas kernels, up_proj(): pl.pallas_call(up_kernel, grid=(4,), out_shape=(jax.ShapeDtypeStruct((8,...  134 us
    pallas_call x2, Pallas kernels, a_gather(): pl.pallas_call(a_gather_kernel, out_shape=jax.ShapeDtypeStruct((8, K, 8 *...  109 us
    pallas_call x1, Pallas kernels, first_exchange(): pl.pallas_call(first_kernel, out_shape=(jax.ShapeDtypeStruct((8, 8, 512,...  95.2 us
    pallas_call x2, Pallas kernels, down_proj(): pl.pallas_call(down_kernel, grid=(4,), out_shape=jax.ShapeDtypeStruct((8,...  76.2 us
    pallas_call x1, Pallas kernels, x_gather(): pl.pallas_call(x_gather_kernel, out_shape=jax.ShapeDtypeStruct((8, 8, 512...  76 us
    all_gather x1, waiting for transfers between devices, local_program(): ups = [lax.all_gather(rows[0], 'ep', axis=0, tiled=True)]  38.3 us
    pallas_call x1, Pallas kernels, last_exchange(): pl.pallas_call(last_kernel, out_shape=jax.ShapeDtypeStruct((8, 512, TB),...  28.4 us
  transfers between devices with their start and end apart: 4, of which 1 were waited for; matrix products, arithmetic and copies ran while one was open for 3% of the time, Pallas kernels for 74%

profile of v2, /device:TPU:1, one launch (start us, length us, event | category | flops | bytes accessed | tf_op | source)
XLA Modules:
  0.0 609.4 jit_solution(4184151825662982559)
XLA Ops:
  6.5 0.0 copy-start
  6.5 0.0 all-gather.7.cloned.1.call-start
  6.5 5.1 fusion.3
  11.6 0.0 copy-done
  11.6 3.2 fusion.2
  14.8 1.5 copy_bitcast_fusion.1
  16.3 1.5 copy_bitcast_fusion.2
  17.9 0.0 copy-start.1
  17.9 1.9 pad_maximum_fusion
  19.8 0.0 all-gather.7.cloned.1.call-update
  19.8 0.2 all-gather.11.cloned.1.call-start
  20.1 0.3 copy-done.1
  20.3 2.4 copy.18
  22.7 2.9 pad.11
  25.7 1.1 reshape.20
  26.7 1.9 copy.43
  28.6 95.2 %first_exchange.1 = (bf16[8,8,512,256]{3,2,1,0:T(8,128)(2,1)}, s32[8,2,4,256]{3,2,1,0:T(4,128)}, bf16[2,8,88,512]{3,2,1,0:T(8,128)(2,1)}) custom-call(bf16[8,512,256]{2,1,0:T(8,128)(2,1)} %bitcast.54, s32[2,4,256]{2,1,0:T(4,128)} %bitcast.60, bf16[2,8,88,512]{3,2,1,0:T(8,128)(2,1)} %bitcast.56), custom_call_target="tpu_custom_call" | custom-call | flops 70000001024 | bytes 16000000 | tf_op jit(solution)/shard_map/first_exchange/pallas_call | solution.py:281
  123.8 1.4 slice_bitcast_fusion
  125.2 0.3 copy.24
  125.5 0.0 copy-start.4
  125.5 0.0 copy-start.3
  125.5 0.0 copy-start.2
  125.6 1.0 pad.12
  126.5 0.0 all-gather.11.cloned.1.call-update
  126.5 0.0 all-gather.9.cloned.1.call-start
  126.6 0.0 copy-done.4
  126.6 0.1 slice_reduce_fusion
  126.7 0.0 copy-done.3
  126.7 0.6 slice_bitcast_fusion.3
  127.3 0.0 copy-done.2
  127.3 0.7 slice_bitcast_fusion.1
  128.1 38.3 %all-gather.7.cloned.1.call-done.w_hbm = bf16[2816,4096]{1,0:T(8,128)(2,1)} async-done(((bf16[176,4096]{1,0:T(8,128)(2,1)}), bf16[2816,4096]{1,0:T(8,128)(2,1)}) %all-gather.7.cloned.1.call-update) | async-done | bytes 23068688 | tf_op jit(solution)/shard_map/all_gather | solution.py:393
  166.4 1.9 broadcast_in_dim.19.nw_ref
  168.3 67.0 %up_proj.2 = (bf16[8,4,88,256]{3,2,1,0:T(8,128)(2,1)}, f32[8,16,256]{2,1,0:T(8,128)}) custom-call(bf16[8,8,512,256]{3,2,1,0:T(8,128)(2,1)} %get-tuple-element.20.x_ref, f32[8,512,128]{2,1,0:T(8,128)} %broadcast_in_dim.19.nw_ref, s32[8,4,256]{2,1,0:T(4,128)} %get-tuple-element.40.idx_ref, bf16[2816,4096]{1,0:T(8,128)(2,1)} %all-gather.7.cloned.1.call-done.w_hbm, ...), custom_call_target="tpu_custom_call" | custom-call | flops 47513075712 | bytes 45000000 | tf_op jit(solution)/shard_map/up_proj/pallas_call | solution.py:96
  235.4 0.0 all-gather.9.cloned.1.call-update
  235.4 0.3 all-gather.13.cloned.1.call-start
  235.7 3.1 dynamic-slice_bitcast_fusion.x_ref
  238.7 54.9 %a_gather.2.a_ref = bf16[8,4,704,256]{3,2,1,0:T(8,128)(2,1)} custom-call(bf16[8,4,88,256]{3,2,1,0:T(8,128)(2,1)} %get-tuple-element.22.a_ref), custom_call_target="tpu_custom_call" | custom-call | flops 49999998976 | bytes 12000000 | tf_op jit(solution)/shard_map/a_gather/pallas_call | solution.py:335
  293.6 0.0 all-gather.11.cloned.1.call-done
  293.6 38.1 %down_proj.2.x_ref = bf16[8,512,256]{2,1,0:T(8,128)(2,1)} custom-call(bf16[8,4,704,256]{3,2,1,0:T(8,128)(2,1)} %a_gather.2.a_ref, s32[8,4,256]{2,1,0:T(4,128)} %get-tuple-element.40.idx_ref, f32[8,16,256]{2,1,0:T(8,128)} %get-tuple-element.23.g_ref, bf16[8,512,256]{2,1,0:T(8,128)(2,1)} %dynamic-slice_bitcast_fusion.x_ref, bf16[16,512,768]{2,1,0:T(8,128)(2,1)} %bitcast.58), custom_call_target="tpu_custom_call" | custom-call | flops 23622320128 | bytes 30000000 | tf_op jit(solution)/shard_map/down_proj/pallas_call | solution.py:147
  331.8 0.3 copy.28
  332.0 1.0 pad.13
  333.0 0.0 all-gather.13.cloned.1.call-update
  333.0 76.0 %x_gather.1.x_ref = bf16[8,8,512,256]{3,2,1,0:T(8,128)(2,1)} custom-call(bf16[8,512,256]{2,1,0:T(8,128)(2,1)} %down_proj.2.x_ref), custom_call_target="tpu_custom_call" | custom-call | flops 70000001024 | bytes 16000000 | tf_op jit(solution)/shard_map/x_gather/pallas_call | solution.py:306
  409.0 0.0 all-gather.9.cloned.1.call-done.w_hbm
  409.1 1.9 broadcast_in_dim.21.nw_ref
  411.0 67.0 %up_proj.3 = (bf16[8,4,88,256]{3,2,1,0:T(8,128)(2,1)}, f32[8,16,256]{2,1,0:T(8,128)}) custom-call(bf16[8,8,512,256]{3,2,1,0:T(8,128)(2,1)} %x_gather.1.x_ref, f32[8,512,128]{2,1,0:T(8,128)} %broadcast_in_dim.21.nw_ref, s32[8,4,256]{2,1,0:T(4,128)} %get-tuple-element.39.idx_ref, bf16[2816,4096]{1,0:T(8,128)(2,1)} %all-gather.9.cloned.1.call-done.w_hbm, ...), custom_call_target="tpu_custom_call" | custom-call | flops 47513075712 | bytes 45000000 | tf_op jit(solution)/shard_map/up_proj/pallas_call | solution.py:96
  478.0 54.2 %a_gather.3.a_ref = bf16[8,4,704,256]{3,2,1,0:T(8,128)(2,1)} custom-call(bf16[8,4,88,256]{3,2,1,0:T(8,128)(2,1)} %get-tuple-element.26.a_ref), custom_call_target="tpu_custom_call" | custom-call | flops 49999998976 | bytes 12000000 | tf_op jit(solution)/shard_map/a_gather/pallas_call | solution.py:335
  532.2 0.0 all-gather.13.cloned.1.call-done
  532.3 38.1 %down_proj.3.y_ref = bf16[8,512,256]{2,1,0:T(8,128)(2,1)} custom-call(bf16[8,4,704,256]{3,2,1,0:T(8,128)(2,1)} %a_gather.3.a_ref, s32[8,4,256]{2,1,0:T(4,128)} %get-tuple-element.39.idx_ref, f32[8,16,256]{2,1,0:T(8,128)} %get-tuple-element.27.g_ref, bf16[8,512,256]{2,1,0:T(8,128)(2,1)} %down_proj.2.x_ref, bf16[16,512,768]{2,1,0:T(8,128)(2,1)} %bitcast.59), custom_call_target="tpu_custom_call" | custom-call | flops 23622320128 | bytes 30000000 | tf_op jit(solution)/shard_map/down_proj/pallas_call | solution.py:147
  570.4 28.4 %last_exchange.1 = bf16[8,512,256]{2,1,0:T(8,128)(2,1)} custom-call(bf16[8,512,256]{2,1,0:T(8,128)(2,1)} %down_proj.3.y_ref), custom_call_target="tpu_custom_call" | custom-call | flops 20000000000 | bytes 4000000 | tf_op jit(solution)/shard_map/last_exchange/pallas_call | solution.py:371
  598.8 4.1 copy.29
  (3 shorter events, 0.0 us)
Async XLA Ops:
  6.5 5.1 copy-start
  6.5 159.9 %all-gather.7.cloned.1.call-start = ((), (), s32[]{:S(2)}) async-start(), calls=%async_computation | async-start | bytes 24510464 | tf_op jit(solution)/shard_map/all_gather | solution.py:393
  17.9 2.4 copy-start.1
  19.8 273.8 %all-gather.11.cloned.1.call-start = ((), (), s32[]{:S(2)}) async-start(), calls=%async_computation.2 | async-start | bytes 13369344 | tf_op jit(solution)/shard_map/all_gather | solution.py:401
  125.5 1.1 copy-start.4
  125.5 1.2 copy-start.3
  125.5 1.8 copy-start.2
  126.5 282.5 %all-gather.9.cloned.1.call-start = ((), (), s32[]{:S(2)}) async-start(), calls=%async_computation.1 | async-start | bytes 24510464 | tf_op jit(solution)/shard_map/all_gather | solution.py:410
  235.4 296.9 %all-gather.13.cloned.1.call-start = ((), (), s32[]{:S(2)}) async-start(), calls=%async_computation.3 | async-start | bytes 13369344 | tf_op jit(solution)/shard_map/all_gather | solution.py:401
Sparse Core Ops, SparseCore 0:
  19.9 146.4 all-gather.6
  168.5 89.3 all-gather.10
  260.1 143.0 all-gather.8
  405.2 89.3 all-gather.12

commit v3 on v1

v3 whole, which is shorter than its diff:
```python
import functools

import jax
import jax.numpy as jnp
from jax import lax
from jax.experimental import pallas as pl
from jax.experimental.pallas import tpu as pltpu
from jax.sharding import PartitionSpec as P

NORM_EPS = 1e-5
TB = 256
D = 4096
FP = 88
KP = 768
E = 16
K = 4
GROUPS = 4
GROWS = E // GROUPS * 2 * FP
HALF = 256
BF = jnp.bfloat16
F32 = jnp.float32
MESH = pl.DeviceIdType.MESH
PEERS = [(s, o) for s in range(4) for o in range(2) if (s, o) != (0, 0)]


def fsdp_at(step, other=0):
    f = lax.axis_index("fsdp")
    core = f % 2
    return lax.rem(f // 2 + step, 4) * 2 + (1 - core if other else core)


def greet(devices):
    barrier = pltpu.get_barrier_semaphore()
    for d in devices:
        pl.semaphore_signal(barrier, inc=1, device_id=d, device_id_type=MESH)
    pl.semaphore_wait(barrier, len(devices))


class Ring:
    def __init__(self, pos, dev, own, place, chunks, send_sem, recv_sem, partner=None):
        self.pos, self.dev, self.own, self.place, self.chunks = pos, dev, own, place, chunks
        self.send_sem, self.recv_sem, self.partner = send_sem, recv_sem, partner

    def at(self, step):
        return lax.rem(self.pos + step, 4)

    def copy(self, kind, k, src, dst, device):
        return pltpu.make_async_remote_copy(
            src_ref=src, dst_ref=dst, send_sem=self.send_sem.at[kind, k], recv_sem=self.recv_sem.at[kind, k],
            device_id=device, device_id_type=MESH)

    def own_copies(self, k):
        mine = self.place(self.pos, k)
        out = [self.copy(0, k, self.own(k), mine, self.dev(self.at(1))), self.copy(1, k, self.own(k), mine, self.dev(self.at(3)))]
        if self.partner is not None:
            out.append(self.copy(3, k, self.own(k), mine, self.partner))
        return out

    def onward(self, k, odd):
        source, target = (self.at(1), self.at(3)) if odd else (self.at(3), self.at(1))
        ref = self.place(source, k)
        return self.copy(2, k, ref, ref, self.dev(target))

    def across(self, kind, k):
        ref = self.place(self.at({4: 3, 5: 1, 6: 2}[kind]), k)
        return self.copy(kind, k, ref, ref, self.partner)

    def arrived(self, kind, k, step, other=0):
        ref = self.place(self.at(step), k, 1) if other else self.place(self.at(step), k)
        self.copy(kind, k, ref, ref, self.dev(self.at(1))).wait_recv()

    def start(self, k):
        for c in self.own_copies(k):
            c.start()

    def relay(self, k, odd):
        self.arrived(0, k, 3)
        if not odd:
            self.onward(k, odd).start()
        if self.partner is not None:
            self.across(4, k).start()
        self.arrived(1, k, 1)
        if odd:
            self.onward(k, odd).start()
        if self.partner is not None:
            self.across(5, k).start()

    def last(self, k):
        self.arrived(2, k, 2)
        if self.partner is not None:
            self.across(6, k).start()

    def drain(self):
        for k in range(self.chunks):
            if self.partner is not None:
                for kind, step in ((3, 0), (4, 3), (5, 1), (6, 2)):
                    self.arrived(kind, k, step, 1)
            for c in self.own_copies(k):
                c.wait_send()
            self.onward(k, k % 2 == 1).wait_send()
            if self.partner is not None:
                for kind in (4, 5, 6):
                    self.across(kind, k).wait_send()


def x_ring(own, place, send_sem, recv_sem):
    f = lax.axis_index("fsdp")
    core = f % 2

    def where(p, k, other=0):
        return place(p * 2 + (1 - core if other else core), k)

    return Ring(f // 2, lambda p: {"fsdp": p * 2 + core}, own, where, 8, send_sem, recv_sem, {"fsdp": fsdp_at(0, 1)})


X_SEMS = [pltpu.SemaphoreType.DMA((7, 8)), pltpu.SemaphoreType.DMA((7, 8))]


def x_neighbours():
    return [{"fsdp": fsdp_at(1)}, {"fsdp": fsdp_at(3)}, {"fsdp": fsdp_at(0, 1)}]


def first_kernel(x_ref, idx_ref, wd_ref, x_all, idx_all, wd_all, send_sem, recv_sem, local_sem, psend, precv):
    f = lax.axis_index("fsdp")
    greet([{"fsdp": fsdp_at(s, o)} for s, o in PEERS])
    ring = x_ring(lambda k: x_ref.at[k], lambda owner, k: x_all.at[owner, k], send_sem, recv_sem)
    locals_ = [
        pltpu.make_async_copy(x_ref, x_all.at[f], local_sem.at[0]),
        pltpu.make_async_copy(idx_ref, idx_all.at[f], local_sem.at[1]),
        pltpu.make_async_copy(wd_ref.at[:, f], wd_all.at[:, f], local_sem.at[2]),
    ]
    for c in locals_:
        c.start()
    small = []
    for p, (s, o) in enumerate(PEERS):
        peer = fsdp_at(s, o)
        small.append(pltpu.make_async_remote_copy(
            src_ref=idx_ref, dst_ref=idx_all.at[f], send_sem=psend.at[0, p], recv_sem=precv.at[0, p],
            device_id={"fsdp": peer}, device_id_type=MESH))
        small.append(pltpu.make_async_remote_copy(
            src_ref=wd_ref.at[:, peer], dst_ref=wd_all.at[:, f], send_sem=psend.at[1, p], recv_sem=precv.at[1, p],
            device_id={"fsdp": peer}, device_id_type=MESH))
    for c in small:
        c.start()
    for k in range(8):
        ring.start(k)
    for k in range(8):
        ring.relay(k, k % 2 == 1)
    for k in range(8):
        ring.last(k)
    ring.drain()
    for p, (s, o) in enumerate(PEERS):
        source = fsdp_at((4 - s) % 4, o)
        for kind, (src, dst) in enumerate(((idx_ref, idx_all.at[source]), (wd_ref.at[:, 0], wd_all.at[:, source]))):
            pltpu.make_async_remote_copy(
                src_ref=src, dst_ref=dst, send_sem=psend.at[kind, p], recv_sem=precv.at[kind, p],
                device_id={"fsdp": source}, device_id_type=MESH).wait_recv()
    for c in small:
        c.wait_send()
    for c in locals_:
        c.wait()


def first_exchange(xt, idx, wd):
    return pl.pallas_call(
        first_kernel,
        out_shape=(jax.ShapeDtypeStruct((8, 8, 512, TB), BF), jax.ShapeDtypeStruct((8, 2, K, TB), jnp.int32), jax.ShapeDtypeStruct((2, 8, FP, 512), BF)),
        in_specs=[pl.BlockSpec(memory_space=pltpu.VMEM)] * 3,
        out_specs=[pl.BlockSpec(memory_space=pl.ANY)] * 3,
        scratch_shapes=X_SEMS + [pltpu.SemaphoreType.DMA((3,)), pltpu.SemaphoreType.DMA((2, 7)), pltpu.SemaphoreType.DMA((2, 7))],
        compiler_params=pltpu.CompilerParams(collective_id=0, has_side_effects=True),
        cost_estimate=pl.CostEstimate(flops=70_000_000_000, bytes_accessed=16_000_000, transcendentals=0),
        name="first_exchange",
    )(xt, idx, wd)


def wd_rings(wd_ref, wd_all, send1, recv1, send2, recv2):
    e = lax.axis_index("ep")
    z, y = e // 4, e % 4
    on_y = lambda p: {"ep": z * 4 + p}
    on_z = lambda p: {"ep": p * 4 + y}
    rows = lambda b, k: pl.ds(b * HALF + k * (HALF // 2), HALF // 2)
    first = [
        Ring(y, on_y, lambda k: wd_ref.at[rows(0, k)], lambda p, k: wd_all.at[z * 4 + p, rows(0, k)], 2, send1.at[0], recv1.at[0]),
        Ring(z, on_z, lambda k: wd_ref.at[rows(1, k)], lambda p, k: wd_all.at[p * 4 + y, rows(1, k)], 2, send1.at[1], recv1.at[1]),
    ]
    by_z = lambda p, k: wd_all.at[p * 4 + k, pl.ds(0, HALF)]
    by_y = lambda p, k: wd_all.at[k * 4 + p, pl.ds(HALF, HALF)]
    second = [
        Ring(z, on_z, lambda k: by_z(z, k), by_z, 4, send2.at[0], recv2.at[0]),
        Ring(y, on_y, lambda k: by_y(y, k), by_y, 4, send2.at[1], recv2.at[1]),
    ]
    near = [on_y(lax.rem(y + 1, 4)), on_y(lax.rem(y + 3, 4)), on_z(lax.rem(z + 1, 4)), on_z(lax.rem(z + 3, 4))]
    return first, second, near


def up_kernel(
    x_ref, nw_ref, idx_ref, wd_ref, w_hbm, rt_hbm, a_all, g_ref, wd_all,
    wv, h, slots, logits, a_buf, sems, send_sem, recv_sem, send1, recv1, send2, recv2, local_sem,
):
    step = pl.program_id(0)
    f = lax.axis_index("fsdp")
    mine = lambda owner: pl.ds(pl.multiple_of(owner * FP, 8), FP)
    ring = x_ring(lambda k: a_buf.at[k], lambda owner, k: a_all.at[k, :, mine(owner)], send_sem, recv_sem)
    first, second, near = wd_rings(wd_ref, wd_all, send1, recv1, send2, recv2)
    own_wd = pltpu.make_async_copy(wd_ref, wd_all.at[lax.axis_index("ep")], local_sem.at[8])

    def own_a(k):
        return pltpu.make_async_copy(a_buf.at[k], a_all.at[k, :, mine(f)], local_sem.at[k])

    @pl.when(step == 0)
    def _():
        for g in range(GROUPS):
            pltpu.make_async_copy(w_hbm.at[pl.ds(g * GROWS, GROWS)], wv.at[g, pl.ds(0, GROWS)], sems.at[2 * g]).start()
            pltpu.make_async_copy(rt_hbm, wv.at[g, pl.ds(GROWS, E)], sems.at[2 * g + 1]).start()
        greet(x_neighbours() + near)
        own_wd.start()
        for r in first:
            for k in range(2):
                r.start(k)

    @pl.when(step == 1)
    def _():
        for r in first:
            for k in range(2):
                r.last(k)
            r.drain()
        own_wd.wait()
        for r in second:
            for k in range(4):
                r.start(k)

    for tb in range(2):
        def rows(c, tb=tb):
            if x_ref.shape[0] == 2:
                return x_ref[tb, c]
            return x_ref[c, tb]

        def ssq_body(c, acc):
            xf = rows(c).astype(F32)
            return acc + jnp.sum(xf * xf, axis=0, keepdims=True)

        ssq = lax.fori_loop(0, 8, ssq_body, jnp.zeros((1, TB), F32))
        rstd = lax.rsqrt(ssq * (1.0 / D) + NORM_EPS)

        def h_body(c, carry, tb=tb, rstd=rstd):
            xf = rows(c).astype(F32)
            nw = nw_ref[c]
            nw2 = jnp.concatenate([nw, nw], axis=1)
            h[pl.ds(pl.multiple_of(c * 512, 512), 512), tb * TB:(tb + 1) * TB] = (xf * rstd * nw2).astype(BF)
            return carry

        lax.fori_loop(0, 8, h_body, 0)

    slots[...] = jnp.zeros_like(slots)
    idx = jnp.concatenate([idx_ref[0], idx_ref[1]], axis=1)

    def group(g, carry):
        @pl.when(step == 0)
        def _():
            pltpu.make_async_copy(w_hbm.at[pl.ds(g * GROWS, GROWS)], wv.at[g, pl.ds(0, GROWS)], sems.at[2 * g]).wait()
            pltpu.make_async_copy(rt_hbm, wv.at[g, pl.ds(GROWS, E)], sems.at[2 * g + 1]).wait()

        @pl.when(jnp.logical_and(step == 0, g == 3))
        def _():
            for r in first:
                for k in range(2):
                    r.relay(k, k % 2 == 1)

        @pl.when(jnp.logical_and(step >= 1, g == 2))
        def _():
            for tb in range(2):
                ring.relay(2 * step - 2 + tb, tb == 1)

        @pl.when(jnp.logical_and(step == 3, g == 1))
        def _():
            for r in second:
                for k in range(2):
                    r.relay(k, k % 2 == 1)

        @pl.when(jnp.logical_and(step == 3, g == 3))
        def _():
            for r in second:
                for k in range(2, 4):
                    r.relay(k, k % 2 == 1)

        res = jnp.dot(wv[g], h[...], preferred_element_type=F32)
        logits[...] = res[GROWS:]
        for k in range(E // GROUPS):
            u = res[k * 2 * FP:k * 2 * FP + FP]
            v = res[k * 2 * FP + FP:(k + 1) * 2 * FP]
            act = jax.nn.silu(u) * v
            e = g * (E // GROUPS) + k
            for j in range(K):
                slots[j] = jnp.where(idx[j:j + 1] == e, act, slots[j])
        return carry

    lax.fori_loop(0, GROUPS, group, 0)
    for tb in range(2):
        k = 2 * step + tb
        a_buf[k] = slots[:, :, tb * TB:(tb + 1) * TB].astype(BF)
    eids = lax.broadcasted_iota(jnp.int32, (E, 2 * TB), 0)
    chosen = idx[0:1] == eids
    for j in range(1, K):
        chosen = jnp.logical_or(chosen, idx[j:j + 1] == eids)
    lg = jnp.where(chosen, logits[...], -jnp.inf)
    ex = jnp.where(chosen, jnp.exp(lg - jnp.max(lg, axis=0, keepdims=True)), 0.0)
    gates = ex / jnp.sum(ex, axis=0, keepdims=True)
    for tb in range(2):
        g_ref[tb] = gates[:, tb * TB:(tb + 1) * TB]
    for tb in range(2):
        k = 2 * step + tb
        ring.start(k)
        own_a(k).start()

    @pl.when(step == 3)
    def _():
        for k in (6, 7):
            ring.relay(k, k % 2 == 1)
        for k in range(8):
            ring.last(k)
        ring.drain()
        for k in range(8):
            own_a(k).wait()
        for r in second:
            for k in range(4):
                r.last(k)
            r.drain()


def up_proj(x, nw, idx, wd, w, rt, tok_major):
    if tok_major:
        x_spec = pl.BlockSpec((2, 8, 512, TB), lambda i: (i, 0, 0, 0))
    else:
        x_spec = pl.BlockSpec((8, 2, 512, TB), lambda i: (0, i, 0, 0))
    return pl.pallas_call(
        up_kernel,
        grid=(4,),
        out_shape=(jax.ShapeDtypeStruct((8, K, 8 * FP, TB), BF), jax.ShapeDtypeStruct((8, E, TB), F32), jax.ShapeDtypeStruct((E, 512, KP), BF)),
        in_specs=[
            x_spec,
            pl.BlockSpec((8, 512, 128), lambda i: (0, 0, 0)),
            pl.BlockSpec((2, K, TB), lambda i: (i, 0, 0)),
            pl.BlockSpec((512, KP), lambda i: (0, 0)),
            pl.BlockSpec(memory_space=pl.ANY),
            pl.BlockSpec(memory_space=pl.ANY),
        ],
        out_specs=(pl.BlockSpec(memory_space=pl.ANY), pl.BlockSpec((2, E, TB), lambda i: (i, 0, 0)), pl.BlockSpec(memory_space=pl.ANY)),
        scratch_shapes=[
            pltpu.VMEM((GROUPS, GROWS + E, D), BF),
            pltpu.VMEM((D, 2 * TB), BF),
            pltpu.VMEM((K, FP, 2 * TB), F32),
            pltpu.VMEM((E, 2 * TB), F32),
            pltpu.VMEM((8, K, FP, TB), BF),
            pltpu.SemaphoreType.DMA((2 * GROUPS,)),
        ] + X_SEMS + [
            pltpu.SemaphoreType.DMA((2, 3, 2)), pltpu.SemaphoreType.DMA((2, 3, 2)),
            pltpu.SemaphoreType.DMA((2, 3, 4)), pltpu.SemaphoreType.DMA((2, 3, 4)),
            pltpu.SemaphoreType.DMA((9,)),
        ],
        compiler_params=pltpu.CompilerParams(
            vmem_limit_bytes=60 * 1024 * 1024, collective_id=1 if tok_major else 2, has_side_effects=True),
        cost_estimate=pl.CostEstimate(flops=2 * 2832 * D * 2048, bytes_accessed=45_000_000, transcendentals=3_000_000),
        name="up_proj",
    )(x, nw, idx, wd, w, rt)


def down_block(a_ref, idx_ref, g_ref, x_ref, wd_ref, acc, hook):
    idx = jnp.concatenate([idx_ref[0], idx_ref[1]], axis=1).astype(F32).astype(BF)
    acc[...] = jnp.zeros_like(acc)

    def group(g, carry):
        if hook is not None:
            hook(g)
        for k in range(E // GROUPS):
            e = g * (E // GROUPS) + k
            ef = e.astype(F32).astype(BF)
            parts = []
            for tb in range(2):
                sel = jnp.zeros((8 * FP, TB), BF)
                for j in range(K):
                    row = idx[j:j + 1, tb * TB:(tb + 1) * TB]
                    sel = jnp.where(row == ef, a_ref[tb, j], sel)
                parts.append(sel)
            out = jnp.dot(wd_ref[e, :, :8 * FP], jnp.concatenate(parts, axis=1), preferred_element_type=F32)
            gate = jnp.concatenate([g_ref[0, pl.ds(e, 1)], g_ref[1, pl.ds(e, 1)]], axis=1)
            acc[...] += gate * out
        return carry

    lax.fori_loop(0, GROUPS, group, 0)
    xf = lambda tb: x_ref[tb].reshape(512, TB) if len(x_ref.shape) == 4 and x_ref.shape[0] == 2 else x_ref[0, tb]
    return [(xf(tb).astype(F32) + acc[:, tb * TB:(tb + 1) * TB]).astype(BF) for tb in range(2)]


def down_mid_kernel(a_ref, idx_ref, g_ref, x_ref, wd_ref, x_all, acc, o_buf, send_sem, recv_sem, local_sem):
    step = pl.program_id(0)
    f = lax.axis_index("fsdp")
    ring = x_ring(lambda k: o_buf.at[k], lambda owner, k: x_all.at[owner, k], send_sem, recv_sem)

    def own_x(k):
        return pltpu.make_async_copy(o_buf.at[k], x_all.at[f, k], local_sem.at[k])

    @pl.when(step == 0)
    def _():
        greet(x_neighbours())

    def hook(g):
        @pl.when(jnp.logical_and(step >= 2, g == 2))
        def _():
            for tb in range(2):
                ring.relay(2 * step - 4 + tb, tb == 1)

    blocks = down_block(a_ref, idx_ref, g_ref, x_ref, wd_ref, acc, hook)
    for tb in range(2):
        o_buf[2 * step + tb] = blocks[tb]
    for tb in range(2):
        ring.start(2 * step + tb)
        own_x(2 * step + tb).start()

    @pl.when(step == 3)
    def _():
        for k in range(4, 8):
            ring.relay(k, k % 2 == 1)
        for k in range(8):
            ring.last(k)
        ring.drain()
        for k in range(8):
            own_x(k).wait()


def down_last_kernel(a_ref, idx_ref, g_ref, x_ref, wd_ref, o_all, acc, o_buf, psend, precv, local_sem):
    step = pl.program_id(0)
    f = lax.axis_index("fsdp")
    core = f % 2

    @pl.when(step == 0)
    def _():
        greet([{"fsdp": fsdp_at(s, o)} for s, o in PEERS])

    blocks = down_block(a_ref, idx_ref, g_ref, x_ref, wd_ref, acc, None)
    for tb in range(2):
        o_buf[step, tb] = blocks[tb]

    def send(s, o):
        tb = 1 - core if o else core
        return pltpu.make_async_remote_copy(
            src_ref=o_buf.at[(s + 3) % 4, tb], dst_ref=o_all.at[f], send_sem=psend.at[s, o], recv_sem=precv.at[s, o],
            device_id={"fsdp": fsdp_at(s, o)}, device_id_type=MESH)

    for s in range(1, 4):
        @pl.when(step == s - 1)
        def _(s=s):
            send(s, 0).start()
            send(s, 1).start()

    @pl.when(step == 3)
    def _():
        send(0, 1).start()
        mine = pltpu.make_async_copy(o_buf.at[3, core], o_all.at[f], local_sem)
        mine.start()
        for s, o in PEERS:
            source = fsdp_at((4 - s) % 4, o)
            pltpu.make_async_remote_copy(
                src_ref=o_buf.at[0, 0], dst_ref=o_all.at[source], send_sem=psend.at[s, o], recv_sem=precv.at[s, o],
                device_id={"fsdp": source}, device_id_type=MESH).wait_recv()
        for s, o in PEERS:
            send(s, o).wait_send()
        mine.wait()


def down_proj(a, idx, gates, xs_all, wd, tok_major, last):
    if last:
        block = lambda i: lax.rem(lax.axis_index("fsdp") // 2 + 1 + i, 4)
    else:
        block = lambda i: i
    if tok_major:
        x_spec = pl.BlockSpec((2, 1, 512, TB), lambda i: (block(i), lax.axis_index("fsdp"), 0, 0))
    else:
        x_spec = pl.BlockSpec((1, 2, 512, TB), lambda i: (lax.axis_index("fsdp"), block(i), 0, 0))
    return pl.pallas_call(
        down_last_kernel if last else down_mid_kernel,
        grid=(4,),
        out_shape=jax.ShapeDtypeStruct((8, 512, TB) if last else (8, 8, 512, TB), BF),
        in_specs=[
            pl.BlockSpec((2, K, 8 * FP, TB), lambda i: (block(i), 0, 0, 0)),
            pl.BlockSpec((2, K, TB), lambda i: (block(i), 0, 0)),
            pl.BlockSpec((2, E, TB), lambda i: (block(i), 0, 0)),
            x_spec,
            pl.BlockSpec((E, 512, KP), lambda i: (0, 0, 0)),
        ],
        out_specs=pl.BlockSpec(memory_space=pl.ANY),
        scratch_shapes=[pltpu.VMEM((512, 2 * TB), F32)] + (
            [pltpu.VMEM((4, 2, 512, TB), BF), pltpu.SemaphoreType.DMA((4, 2)), pltpu.SemaphoreType.DMA((4, 2)), pltpu.SemaphoreType.DMA]
            if last else [pltpu.VMEM((8, 512, TB), BF)] + X_SEMS + [pltpu.SemaphoreType.DMA((8,))]),
        compiler_params=pltpu.CompilerParams(vmem_limit_bytes=60 * 1024 * 1024, collective_id=4 if last else 3, has_side_effects=True),
        cost_estimate=pl.CostEstimate(flops=2 * 704 * 16 * 512 * 2048, bytes_accessed=30_000_000, transcendentals=0),
        name="down_last" if last else "down_mid",
    )(a, idx, gates, xs_all, wd)


def solution(mesh):
    tok_spec = P(("rep", "ep", "fsdp"), None)
    idx_spec = P(None, ("rep", "ep", "fsdp"), None)
    in_specs = (tok_spec, P(None, None), P(None, None, None), P(None, "ep", None, "fsdp"), P(None, "ep", None, "fsdp"), P(None, "ep", "fsdp", None), idx_spec)

    def local_program(x, norm_w, router_w, w_gate, w_up, w_down, expert_idx):
        layers = norm_w.shape[0]
        pad = jnp.zeros((FP - 86, D), BF)
        rows = [jnp.concatenate([w_gate[l, 0].T, pad, w_up[l, 0].T, pad], axis=0) for l in range(layers)]
        ups = [lax.all_gather(rows[0], "ep", axis=0, tiled=True)]
        xt = x.T.reshape(8, 512, TB)
        wd = jnp.pad(w_down[:, 0], ((0, 0), (0, FP - 86), (0, 0))).reshape(layers, FP, 8, 512).swapaxes(1, 2)
        xt, idx, wd, _ = lax.optimization_barrier((xt, jnp.swapaxes(expert_idx, 1, 2), wd, rows[0]))
        xs_all, idx_all, wd = first_exchange(xt, idx, wd)
        wd = jnp.swapaxes(wd.reshape(layers, 8 * FP, 512), 1, 2)
        wd = jnp.pad(wd, ((0, 0), (0, 0), (0, KP - 8 * FP)))
        for l in range(1, layers):
            nxt, _ = lax.optimization_barrier((rows[l], idx_all))
            ups.append(lax.all_gather(nxt, "ep", axis=0, tiled=True))
        for l in range(layers):
            nw = jnp.broadcast_to(norm_w[l].reshape(8, 512, 1), (8, 512, 128))
            a, gates, wd_all = up_proj(xs_all, nw, idx_all[:, l], wd[l], ups[l], router_w[l].T, l == 0)
            xs_all = down_proj(a, idx_all[:, l], gates, xs_all, wd_all, l == 0, l == layers - 1)
        return xs_all.reshape(D, TB).T

    return jax.shard_map(local_program, mesh=mesh, in_specs=in_specs, out_specs=tok_spec, check_vma=False)
```

time: 879 us -> 534 us (0.61)
  waiting for transfers between devices: 479 us -> 36.7 us
  Pallas kernels: 215 us -> 448 us
  blocking collectives: 98.2 us -> 0 us
  local copies, waits for them, and re-layouts: 69.3 us -> 34.1 us
    all_gather x8 -> x2, waiting for transfers between devices: 477 us -> 36.7 us  [the longest x1 36.6 us: local_program(): ups = [lax.all_gather(rows[0], 'ep', axis=0, tiled=True)]]
    pallas_call x2 -> x3, Pallas kernels: 69.8 us -> 230 us  [the longest x2 135 us: down_proj(): pl.pallas_call(down_last_kernel if last else down_mid_kernel, grid=(4,),...]
    all_to_all x2 -> x0, blocking collectives: 84.4 us -> none  [the longest x1 54.7 us: local_program(): wd = lax.all_to_all(wd, 'fsdp', split_axis=2, concat_axis=1, tiled=True)]
    pallas_call x2, Pallas kernels: 145 us -> 218 us  [up_proj(): pl.pallas_call(up_kernel, grid=(4,), out_shape=(jax.ShapeDtypeStruct((8,...]
    all_gather x2 -> x0, local copies, waits for them, and re-layouts: 31.2 us -> none  [local_program(): lax.all_gather(wd[l], 'ep', axis=0, tiled=False)]
    all_gather x1 -> x0, blocking collectives: 13.8 us -> none  [local_program(): lax.all_gather(jnp.swapaxes(expert_idx, 1, 2), 'fsdp', axis=0, tiled=False)]
  transfers between devices with their start and end apart: 8 -> 2, of which waited for: 8 -> 1; matrix products, arithmetic and copies ran while one was open for 7% -> 3% of each run, Pallas kernels for 21% -> 57%
where the time goes in v3:
time: 534 us
  Pallas kernels  448 us (84%)
  waiting for transfers between devices  36.7 us (7%)
  local copies, waits for them, and re-layouts  34.1 us (6%)
  between operations  13.6 us (3%)
    pallas_call x2, Pallas kernels, up_proj(): pl.pallas_call(up_kernel, grid=(4,), out_shape=(jax.ShapeDtypeStruct((8,...  218 us
    pallas_call x2, Pallas kernels, down_proj(): pl.pallas_call(down_last_kernel if last else down_mid_kernel, grid=(4,),...  135 us
    pallas_call x1, Pallas kernels, first_exchange(): pl.pallas_call(first_kernel, out_shape=(jax.ShapeDtypeStruct((8, 8, 512,...  94.9 us
    all_gather x1, waiting for transfers between devices, local_program(): ups = [lax.all_gather(rows[0], 'ep', axis=0, tiled=True)]  36.6 us
  transfers between devices with their start and end apart: 2, of which 1 were waited for; matrix products, arithmetic and copies ran while one was open for 3% of the time, Pallas kernels for 57%

profile of v3, /device:TPU:1, one launch (start us, length us, event | category | flops | bytes accessed | tf_op | source)
XLA Modules:
  0.0 534.1 jit_solution(4337167212578380430)
XLA Ops:
  6.5 0.0 copy-start
  6.5 0.0 all-gather.3.cloned.1.call-start
  6.5 5.1 fusion.5
  11.6 0.0 copy-done
  11.6 3.2 fusion.4
  14.8 1.5 copy_bitcast_fusion.1
  16.3 1.5 copy_bitcast_fusion.2
  17.9 1.9 pad_maximum_fusion
  19.8 0.0 copy-start.2
  19.8 0.0 all-gather.3.cloned.1.call-update
  19.8 0.0 all-gather.5.cloned.1.call-start
  19.9 1.3 copy-done.2
  21.1 1.5 pad.8
  22.7 1.2 reshape.18
  23.9 1.9 copy.41
  25.8 4.1 copy.17
  29.9 94.9 %first_exchange.1 = (bf16[8,8,512,256]{3,2,1,0:T(8,128)(2,1)}, s32[8,2,4,256]{3,2,1,0:T(4,128)}, bf16[2,8,88,512]{3,2,1,0:T(8,128)(2,1)}) custom-call(bf16[8,512,256]{2,1,0:T(8,128)(2,1)} %bitcast.48, s32[2,4,256]{2,1,0:T(4,128)} %bitcast.52, bf16[2,8,88,512]{3,2,1,0:T(8,128)(2,1)} %bitcast.50), custom_call_target="tpu_custom_call" | custom-call | flops 70000001024 | bytes 16000000 | tf_op jit(solution)/shard_map/first_exchange/pallas_call | solution.py:165
  124.8 0.0 copy-start.1
  124.8 0.0 all-gather.5.cloned.1.call-update
  124.8 1.3 copy-done.1
  126.1 0.0 copy-start.5
  126.1 0.7 copy.23
  126.8 0.1 copy-done.5
  126.9 0.1 slice_reduce_fusion
  127.0 0.0 copy-start.4
  127.0 0.0 copy-start.3
  127.0 1.3 fusion.3
  128.4 0.0 copy-done.4
  128.4 0.6 slice_bitcast_fusion.2
  129.0 0.0 copy-done.3
  129.0 0.7 slice_bitcast_fusion
  129.7 36.6 %all-gather.3.cloned.1.call-done.w_hbm = bf16[2816,4096]{1,0:T(8,128)(2,1)} async-done(((bf16[176,4096]{1,0:T(8,128)(2,1)}), bf16[2816,4096]{1,0:T(8,128)(2,1)}) %all-gather.3.cloned.1.call-update) | async-done | bytes 23068688 | tf_op jit(solution)/shard_map/all_gather | solution.py:510
  166.4 1.9 broadcast_in_dim.19.nw_ref
  168.3 124.4 %up_proj.2 = (bf16[8,4,704,256]{3,2,1,0:T(8,128)(2,1)}, f32[8,16,256]{2,1,0:T(8,128)}, bf16[16,512,768]{2,1,0:T(8,128)(2,1)}) custom-call(bf16[8,8,512,256]{3,2,1,0:T(8,128)(2,1)} %get-tuple-element.21.x_ref, f32[8,512,128]{2,1,0:T(8,128)} %broadcast_in_dim.19.nw_ref, s32[8,4,256]{2,1,0:T(4,128)} %get-tuple-element.42.idx_ref, ...), custom_call_target="tpu_custom_call" | custom-call | flops 47513075712 | bytes 45000000 | tf_op jit(solution)/shard_map/up_proj/pallas_call | solution.py:336
  292.7 87.5 %down_mid.1.x_ref = bf16[8,8,512,256]{3,2,1,0:T(8,128)(2,1)} custom-call(bf16[8,4,704,256]{3,2,1,0:T(8,128)(2,1)} %get-tuple-element.24.a_ref, s32[8,4,256]{2,1,0:T(4,128)} %get-tuple-element.42.idx_ref, f32[8,16,256]{2,1,0:T(8,128)} %get-tuple-element.25.g_ref, bf16[8,8,512,256]{3,2,1,0:T(8,128)(2,1)} %get-tuple-element.21.x_ref, ...), custom_call_target="tpu_custom_call" | custom-call | flops 23622320128 | bytes 30000000 | tf_op jit(solution)/shard_map/down_mid/pallas_call | solution.py:480
  380.2 0.0 all-gather.5.cloned.1.call-done.w_hbm
  380.2 1.9 broadcast_in_dim.21.nw_ref
  382.2 93.6 %up_proj.3 = (bf16[8,4,704,256]{3,2,1,0:T(8,128)(2,1)}, f32[8,16,256]{2,1,0:T(8,128)}, bf16[16,512,768]{2,1,0:T(8,128)(2,1)}) custom-call(bf16[8,8,512,256]{3,2,1,0:T(8,128)(2,1)} %down_mid.1.x_ref, f32[8,512,128]{2,1,0:T(8,128)} %broadcast_in_dim.21.nw_ref, s32[8,4,256]{2,1,0:T(4,128)} %get-tuple-element.41.idx_ref, ...), custom_call_target="tpu_custom_call" | custom-call | flops 47513075712 | bytes 45000000 | tf_op jit(solution)/shard_map/up_proj/pallas_call | solution.py:336
  475.8 47.4 %down_last.1 = bf16[8,512,256]{2,1,0:T(8,128)(2,1)} custom-call(bf16[8,4,704,256]{3,2,1,0:T(8,128)(2,1)} %get-tuple-element.28.a_ref, s32[8,4,256]{2,1,0:T(4,128)} %get-tuple-element.41.idx_ref, f32[8,16,256]{2,1,0:T(8,128)} %get-tuple-element.29.g_ref, bf16[8,8,512,256]{3,2,1,0:T(8,128)(2,1)} %down_mid.1.x_ref, bf16[16,512,768]{2,1,0:T(8,128)(2,1)} %get-tuple-element.30.wd_ref), custom_call_target="tpu_custom_call" | custom-call | flops 23622320128 | bytes 30000000 | tf_op jit(solution)/shard_map/down_last/pallas_call | solution.py:480
  523.2 4.1 copy.27
  (3 shorter events, 0.0 us)
Async XLA Ops:
  6.5 5.1 copy-start
  6.5 159.8 %all-gather.3.cloned.1.call-start = ((), (), s32[]{:S(2)}) async-start(), calls=%async_computation | async-start | bytes 24510464 | tf_op jit(solution)/shard_map/all_gather | solution.py:510
  19.8 1.4 copy-start.2
  19.8 360.4 %all-gather.5.cloned.1.call-start = ((), (), s32[]{:S(2)}) async-start(), calls=%async_computation.1 | async-start | bytes 24510464 | tf_op jit(solution)/shard_map/all_gather | solution.py:519
  124.8 1.4 copy-start.1
  126.1 0.8 copy-start.5
  127.0 1.4 copy-start.4
  127.0 2.0 copy-start.3
Sparse Core Ops, SparseCore 0:
  19.9 146.4 all-gather.2
  168.5 188.1 all-gather.4

commit v4 on v3

--- a/solution.py
+++ b/solution.py
@@ -194,9 +194,50 @@
     return first, second, near
 
 
+def norm_kernel(x_ref, nw_ref, h_ref):
+    for tb in range(2):
+        def rows(c, tb=tb):
+            if x_ref.shape[0] == 2:
+                return x_ref[tb, c]
+            return x_ref[c, tb]
+
+        def ssq_body(c, acc):
+            xf = rows(c).astype(F32)
+            return acc + jnp.sum(xf * xf, axis=0, keepdims=True)
+
+        ssq = lax.fori_loop(0, 8, ssq_body, jnp.zeros((1, TB), F32))
+        rstd = lax.rsqrt(ssq * (1.0 / D) + NORM_EPS)
+
+        def h_body(c, carry, tb=tb, rstd=rstd):
+            xf = rows(c).astype(F32)
+            nw = nw_ref[c]
+            nw2 = jnp.concatenate([nw, nw], axis=1)
+            h_ref[0, pl.ds(pl.multiple_of(c * 512, 512), 512), tb * TB:(tb + 1) * TB] = (xf * rstd * nw2).astype(BF)
+            return carry
+
+        lax.fori_loop(0, 8, h_body, 0)
+
+
+def norm(x, nw, tok_major):
+    if tok_major:
+        x_spec = pl.BlockSpec((2, 8, 512, TB), lambda i: (i, 0, 0, 0))
+    else:
+        x_spec = pl.BlockSpec((8, 2, 512, TB), lambda i: (0, i, 0, 0))
+    return pl.pallas_call(
+        norm_kernel,
+        grid=(4,),
+        out_shape=jax.ShapeDtypeStruct((4, D, 2 * TB), BF),
+        in_specs=[x_spec, pl.BlockSpec((8, 512, 128), lambda i: (0, 0, 0))],
+        out_specs=pl.BlockSpec((1, D, 2 * TB), lambda i: (i, 0, 0)),
+        compiler_params=pltpu.CompilerParams(vmem_limit_bytes=40 * 1024 * 1024),
+        cost_estimate=pl.CostEstimate(flops=20_000_000_000, bytes_accessed=34_000_000, transcendentals=0),
+        name="norm",
+    )(x, nw)
+
+
 def up_kernel(
-    x_ref, nw_ref, idx_ref, wd_ref, w_hbm, rt_hbm, a_all, g_ref, wd_all,
-    wv, h, slots, logits, a_buf, sems, send_sem, recv_sem, send1, recv1, send2, recv2, local_sem,
+    h_ref, idx_ref, wd_ref, w_hbm, rt_hbm, a_all, g_ref, wd_all,
+    wv, slots, logits, a_buf, sems, send_sem, recv_sem, send1, recv1, send2, recv2, local_sem,
 ):
     step = pl.program_id(0)
     f = lax.axis_index("fsdp")
@@ -219,39 +260,6 @@
             for k in range(2):
                 r.start(k)
 
-    @pl.when(step == 1)
-    def _():
-        for r in first:
-            for k in range(2):
-                r.last(k)
-            r.drain()
-        own_wd.wait()
-        for r in second:
-            for k in range(4):
-                r.start(k)
-
-    for tb in range(2):
-        def rows(c, tb=tb):
-            if x_ref.shape[0] == 2:
-                return x_ref[tb, c]
-            return x_ref[c, tb]
-
-        def ssq_body(c, acc):
-            xf = rows(c).astype(F32)
-            return acc + jnp.sum(xf * xf, axis=0, keepdims=True)
-
-        ssq = lax.fori_loop(0, 8, ssq_body, jnp.zeros((1, TB), F32))
-        rstd = lax.rsqrt(ssq * (1.0 / D) + NORM_EPS)
-
-        def h_body(c, carry, tb=tb, rstd=rstd):
-            xf = rows(c).astype(F32)
-            nw = nw_ref[c]
-            nw2 = jnp.concatenate([nw, nw], axis=1)
-            h[pl.ds(pl.multiple_of(c * 512, 512), 512), tb * TB:(tb + 1) * TB] = (xf * rstd * nw2).astype(BF)
-            return carry
-
-        lax.fori_loop(0, 8, h_body, 0)
-
     slots[...] = jnp.zeros_like(slots)
     idx = jnp.concatenate([idx_ref[0], idx_ref[1]], axis=1)
 
@@ -261,30 +269,37 @@
             pltpu.make_async_copy(w_hbm.at[pl.ds(g * GROWS, GROWS)], wv.at[g, pl.ds(0, GROWS)], sems.at[2 * g]).wait()
             pltpu.make_async_copy(rt_hbm, wv.at[g, pl.ds(GROWS, E)], sems.at[2 * g + 1]).wait()
 
-        @pl.when(jnp.logical_and(step == 0, g == 3))
+        @pl.when(jnp.logical_and(step >= 1, g == 3))
+        def _():
+            for tb in range(2):
+                ring.relay(2 * step - 2 + tb, tb == 1)
+
+        tick = step * GROUPS + g
+
+        @pl.when(tick == 3)
+        def _():
+            for k in range(2):
+                for r in first:
+                    r.relay(k, k % 2 == 1)
+
+        @pl.when(tick == 5)
         def _():
             for r in first:
                 for k in range(2):
+                    r.last(k)
+                r.drain()
+            own_wd.wait()
+            for k in range(4):
+                for r in second:
+                    r.start(k)
+
+        for k, t in enumerate((9, 12, 15)):
+            @pl.when(tick == t)
+            def _(k=k):
+                for r in second:
                     r.relay(k, k % 2 == 1)
 
-        @pl.when(jnp.logical_and(step >= 1, g == 2))
-        def _():
-            for tb in range(2):
-                ring.relay(2 * step - 2 + tb, tb == 1)
-
-        @pl.when(jnp.logical_and(step == 3, g == 1))
-        def _():
-            for r in second:
-                for k in range(2):
-                    r.relay(k, k % 2 == 1)
-
-        @pl.when(jnp.logical_and(step == 3, g == 3))
-        def _():
-            for r in second:
-                for k in range(2, 4):
-                    r.relay(k, k % 2 == 1)
-
-        res = jnp.dot(wv[g], h[...], preferred_element_type=F32)
+        res = jnp.dot(wv[g], h_ref[0], preferred_element_type=F32)
         logits[...] = res[GROWS:]
         for k in range(E // GROUPS):
             u = res[k * 2 * FP:k * 2 * FP + FP]
@@ -315,6 +330,8 @@
 
     @pl.when(step == 3)
     def _():
+        for r in second:
+            r.relay(3, True)
         for k in (6, 7):
             ring.relay(k, k % 2 == 1)
         for k in range(8):
@@ -328,18 +345,13 @@
             r.drain()
 
 
-def up_proj(x, nw, idx, wd, w, rt, tok_major):
-    if tok_major:
-        x_spec = pl.BlockSpec((2, 8, 512, TB), lambda i: (i, 0, 0, 0))
-    else:
-        x_spec = pl.BlockSpec((8, 2, 512, TB), lambda i: (0, i, 0, 0))
+def up_proj(h, idx, wd, w, rt, layer):
     return pl.pallas_call(
         up_kernel,
         grid=(4,),
         out_shape=(jax.ShapeDtypeStruct((8, K, 8 * FP, TB), BF), jax.ShapeDtypeStruct((8, E, TB), F32), jax.ShapeDtypeStruct((E, 512, KP), BF)),
         in_specs=[
-            x_spec,
-            pl.BlockSpec((8, 512, 128), lambda i: (0, 0, 0)),
+            pl.BlockSpec((1, D, 2 * TB), lambda i: (i, 0, 0)),
             pl.BlockSpec((2, K, TB), lambda i: (i, 0, 0)),
             pl.BlockSpec((512, KP), lambda i: (0, 0)),
             pl.BlockSpec(memory_space=pl.ANY),
@@ -348,7 +360,6 @@
         out_specs=(pl.BlockSpec(memory_space=pl.ANY), pl.BlockSpec((2, E, TB), lambda i: (i, 0, 0)), pl.BlockSpec(memory_space=pl.ANY)),
         scratch_shapes=[
             pltpu.VMEM((GROUPS, GROWS + E, D), BF),
-            pltpu.VMEM((D, 2 * TB), BF),
             pltpu.VMEM((K, FP, 2 * TB), F32),
             pltpu.VMEM((E, 2 * TB), F32),
             pltpu.VMEM((8, K, FP, TB), BF),
@@ -359,10 +370,10 @@
             pltpu.SemaphoreType.DMA((9,)),
         ],
         compiler_params=pltpu.CompilerParams(
-            vmem_limit_bytes=60 * 1024 * 1024, collective_id=1 if tok_major else 2, has_side_effects=True),
+            vmem_limit_bytes=60 * 1024 * 1024, collective_id=1, has_side_effects=True),
         cost_estimate=pl.CostEstimate(flops=2 * 2832 * D * 2048, bytes_accessed=45_000_000, transcendentals=3_000_000),
         name="up_proj",
-    )(x, nw, idx, wd, w, rt)
+    )(h, idx, wd, w, rt)
 
 
 def down_block(a_ref, idx_ref, g_ref, x_ref, wd_ref, acc, hook):
@@ -506,20 +517,25 @@
     def local_program(x, norm_w, router_w, w_gate, w_up, w_down, expert_idx):
         layers = norm_w.shape[0]
         pad = jnp.zeros((FP - 86, D), BF)
-        rows = [jnp.concatenate([w_gate[l, 0].T, pad, w_up[l, 0].T, pad], axis=0) for l in range(layers)]
-        ups = [lax.all_gather(rows[0], "ep", axis=0, tiled=True)]
+
+        def pack(gate, up):
+            return jnp.concatenate([gate.T, pad, up.T, pad], axis=0)
+
+        rows = pack(w_gate[0, 0], w_up[0, 0])
+        ups = [lax.all_gather(rows, "ep", axis=0, tiled=True)]
         xt = x.T.reshape(8, 512, TB)
         wd = jnp.pad(w_down[:, 0], ((0, 0), (0, FP - 86), (0, 0))).reshape(layers, FP, 8, 512).swapaxes(1, 2)
-        xt, idx, wd, _ = lax.optimization_barrier((xt, jnp.swapaxes(expert_idx, 1, 2), wd, rows[0]))
+        xt, idx, wd, _ = lax.optimization_barrier((xt, jnp.swapaxes(expert_idx, 1, 2), wd, rows))
         xs_all, idx_all, wd = first_exchange(xt, idx, wd)
         wd = jnp.swapaxes(wd.reshape(layers, 8 * FP, 512), 1, 2)
         wd = jnp.pad(wd, ((0, 0), (0, 0), (0, KP - 8 * FP)))
+        gates_w, ups_w, _ = lax.optimization_barrier((w_gate, w_up, idx_all))
         for l in range(1, layers):
-            nxt, _ = lax.optimization_barrier((rows[l], idx_all))
-            ups.append(lax.all_gather(nxt, "ep", axis=0, tiled=True))
+            ups.append(lax.all_gather(pack(gates_w[l, 0], ups_w[l, 0]), "ep", axis=0, tiled=True))
         for l in range(layers):
             nw = jnp.broadcast_to(norm_w[l].reshape(8, 512, 1), (8, 512, 128))
-            a, gates, wd_all = up_proj(xs_all, nw, idx_all[:, l], wd[l], ups[l], router_w[l].T, l == 0)
+            h = norm(xs_all, nw, l == 0)
+            a, gates, wd_all = up_proj(h, idx_all[:, l], wd[l], ups[l], router_w[l].T, l)
             xs_all = down_proj(a, idx_all[:, l], gates, xs_all, wd_all, l == 0, l == layers - 1)
         return xs_all.reshape(D, TB).T
 

time: 534 us -> 525 us (0.983)
  waiting for transfers between devices: 36.7 us -> 19.6 us
  Pallas kernels: 448 us -> 465 us
  local copies, waits for them, and re-layouts: 34.1 us -> 24 us
    pallas_call x0 -> x2, Pallas kernels: none -> 29.2 us  [norm(): pl.pallas_call(norm_kernel, grid=(4,), out_shape=jax.ShapeDtypeStruct((4,...]
    all_gather x2, waiting for transfers between devices: 36.7 us -> 19.5 us  [the longest x1 19.5 us: local_program(): ups = [lax.all_gather(rows, 'ep', axis=0, tiled=True)]]
    pallas_call x2, Pallas kernels: 218 us -> 204 us  [up_proj(): pl.pallas_call(up_kernel, grid=(4,), out_shape=(jax.ShapeDtypeStruct((8,...]
    slice x2 -> x0, local copies, waits for them, and re-layouts: 8.23 us -> none  [the longest x1 5.08 us: local_program(): w_up[l, 0]]
  transfers between devices with their start and end apart: 2 -> 2, of which waited for: 1 -> 1; matrix products, arithmetic and copies ran while one was open for 3% -> 3% of each run, Pallas kernels for 57% -> 64%
where the time goes in v4:
time: 525 us; the launch traced here: 524 us
  Pallas kernels  465 us (89%)
  local copies, waits for them, and re-layouts  24 us (5%)
  waiting for transfers between devices  19.6 us (4%)
  between operations  13.6 us (3%)
    pallas_call x2, Pallas kernels, up_proj(): pl.pallas_call(up_kernel, grid=(4,), out_shape=(jax.ShapeDtypeStruct((8,...  204 us
    pallas_call x2, Pallas kernels, down_proj(): pl.pallas_call(down_last_kernel if last else down_mid_kernel, grid=(4,),...  137 us
    pallas_call x1, Pallas kernels, first_exchange(): pl.pallas_call(first_kernel, out_shape=(jax.ShapeDtypeStruct((8, 8, 512,...  95 us
    pallas_call x2, Pallas kernels, norm(): pl.pallas_call(norm_kernel, grid=(4,), out_shape=jax.ShapeDtypeStruct((4,...  29.2 us
    all_gather x1, waiting for transfers between devices, local_program(): ups = [lax.all_gather(rows, 'ep', axis=0, tiled=True)]  19.5 us
  transfers between devices with their start and end apart: 2, of which 1 were waited for; matrix products, arithmetic and copies ran while one was open for 3% of the time, Pallas kernels for 64%

profile of v4, /device:TPU:1, one launch (start us, length us, event | category | flops | bytes accessed | tf_op | source)
XLA Modules:
  0.0 524.4 jit_solution(6963306940778060501)
XLA Ops:
  6.5 0.0 all-gather.3.cloned.1.call-start
  6.5 3.3 copy_bitcast_fusion.1
  9.9 0.0 copy-start.3
  9.9 1.3 pad_maximum_fusion.1
  11.2 0.0 all-gather.3.cloned.1.call-update
  11.2 0.0 all-gather.5.cloned.1.call-start
  11.3 0.5 copy-done.3
  11.7 1.5 pad.8
  13.3 1.2 reshape.18
  14.5 1.9 copy.37
  16.5 4.1 copy.17
  20.5 0.0 copy-start
  20.5 95.0 %first_exchange.1 = (bf16[8,8,512,256]{3,2,1,0:T(8,128)(2,1)}, s32[8,2,4,256]{3,2,1,0:T(4,128)}, bf16[2,8,88,512]{3,2,1,0:T(8,128)(2,1)}) custom-call(bf16[8,512,256]{2,1,0:T(8,128)(2,1)} %bitcast.52, s32[2,4,256]{2,1,0:T(4,128)} %bitcast.56, bf16[2,8,88,512]{3,2,1,0:T(8,128)(2,1)} %bitcast.54), custom_call_target="tpu_custom_call" | custom-call | flops 70000001024 | bytes 16000000 | tf_op jit(solution)/shard_map/first_exchange/pallas_call | solution.py:165
  115.5 0.0 copy-start.1
  115.5 0.0 copy-done
  115.6 0.8 copy.26
  116.4 0.5 copy-done.1
  116.9 0.8 copy.25
  117.8 0.0 copy-start.6
  117.8 0.0 copy-start.2
  117.8 1.3 pad_maximum_fusion
  119.1 0.0 all-gather.5.cloned.1.call-update
  119.1 0.0 copy-done.6
  119.1 0.1 slice_reduce_fusion
  119.2 0.5 copy-done.2
  119.7 0.7 copy.23
  120.4 0.0 copy-start.5
  120.4 0.0 copy-start.4
  120.4 1.3 fusion.3
  121.7 0.0 copy-done.5
  121.7 0.6 slice_bitcast_fusion.4
  122.4 0.0 copy-done.4
  122.4 0.7 slice_bitcast_fusion.2
  123.1 0.6 broadcast_in_dim.19.nw_ref
  123.7 14.6 %norm.2.h_ref = bf16[4,4096,512]{2,1,0:T(8,128)(2,1)} custom-call(bf16[8,8,512,256]{3,2,1,0:T(8,128)(2,1)} %get-tuple-element.22.x_ref, f32[8,512,128]{2,1,0:T(8,128)S(1)} %broadcast_in_dim.19.nw_ref), custom_call_target="tpu_custom_call" | custom-call | flops 20000000000 | bytes 34000000 | tf_op jit(solution)/shard_map/norm/pallas_call | solution.py:226
  138.3 19.5 %all-gather.3.cloned.1.call-done.w_hbm = bf16[2816,4096]{1,0:T(8,128)(2,1)} async-done(((bf16[176,4096]{1,0:T(8,128)(2,1)}), bf16[2816,4096]{1,0:T(8,128)(2,1)}) %all-gather.3.cloned.1.call-update) | async-done | bytes 23068688 | tf_op jit(solution)/shard_map/all_gather | solution.py:525
  157.8 121.2 %up_proj.2 = (bf16[8,4,704,256]{3,2,1,0:T(8,128)(2,1)}, f32[8,16,256]{2,1,0:T(8,128)}, bf16[16,512,768]{2,1,0:T(8,128)(2,1)}) custom-call(bf16[4,4096,512]{2,1,0:T(8,128)(2,1)} %norm.2.h_ref, s32[8,4,256]{2,1,0:T(4,128)} %get-tuple-element.40.idx_ref, bf16[512,768]{1,0:T(8,128)(2,1)} %get-tuple-element.36.wd_ref, ...), custom_call_target="tpu_custom_call" | custom-call | flops 47513075712 | bytes 45000000 | tf_op jit(solution)/shard_map/up_proj/pallas_call | solution.py:349
  279.0 89.1 %down_mid.1.x_ref = bf16[8,8,512,256]{3,2,1,0:T(8,128)(2,1)} custom-call(bf16[8,4,704,256]{3,2,1,0:T(8,128)(2,1)} %get-tuple-element.25.a_ref, s32[8,4,256]{2,1,0:T(4,128)} %get-tuple-element.40.idx_ref, f32[8,16,256]{2,1,0:T(8,128)} %get-tuple-element.26.g_ref, bf16[8,8,512,256]{3,2,1,0:T(8,128)(2,1)} %get-tuple-element.22.x_ref, ...), custom_call_target="tpu_custom_call" | custom-call | flops 23622320128 | bytes 30000000 | tf_op jit(solution)/shard_map/down_mid/pallas_call | solution.py:491
  368.2 0.6 broadcast_in_dim.21.nw_ref
  368.8 14.6 %norm.3.h_ref = bf16[4,4096,512]{2,1,0:T(8,128)(2,1)} custom-call(bf16[8,8,512,256]{3,2,1,0:T(8,128)(2,1)} %down_mid.1.x_ref, f32[8,512,128]{2,1,0:T(8,128)S(1)} %broadcast_in_dim.21.nw_ref), custom_call_target="tpu_custom_call" | custom-call | flops 20000000000 | bytes 34000000 | tf_op jit(solution)/shard_map/norm/pallas_call | solution.py:226
  383.3 0.0 all-gather.5.cloned.1.call-done.w_hbm
  383.3 82.4 %up_proj.3 = (bf16[8,4,704,256]{3,2,1,0:T(8,128)(2,1)}, f32[8,16,256]{2,1,0:T(8,128)}, bf16[16,512,768]{2,1,0:T(8,128)(2,1)}) custom-call(bf16[4,4096,512]{2,1,0:T(8,128)(2,1)} %norm.3.h_ref, s32[8,4,256]{2,1,0:T(4,128)} %get-tuple-element.39.idx_ref, bf16[512,768]{1,0:T(8,128)(2,1)} %get-tuple-element.35.wd_ref, ...), custom_call_target="tpu_custom_call" | custom-call | flops 47513075712 | bytes 45000000 | tf_op jit(solution)/shard_map/up_proj/pallas_call | solution.py:349
  465.8 47.7 %down_last.1 = bf16[8,512,256]{2,1,0:T(8,128)(2,1)} custom-call(bf16[8,4,704,256]{3,2,1,0:T(8,128)(2,1)} %get-tuple-element.30.a_ref, s32[8,4,256]{2,1,0:T(4,128)} %get-tuple-element.39.idx_ref, f32[8,16,256]{2,1,0:T(8,128)} %get-tuple-element.31.g_ref, bf16[8,8,512,256]{3,2,1,0:T(8,128)(2,1)} %down_mid.1.x_ref, bf16[16,512,768]{2,1,0:T(8,128)(2,1)} %get-tuple-element.32.wd_ref), custom_call_target="tpu_custom_call" | custom-call | flops 23622320128 | bytes 30000000 | tf_op jit(solution)/shard_map/down_last/pallas_call | solution.py:491
  513.5 4.1 copy.27
  (5 shorter events, 0.1 us)
Async XLA Ops:
  6.5 151.3 %all-gather.3.cloned.1.call-start = ((), (), s32[]{:S(2)}) async-start(), calls=%async_computation | async-start | bytes 24510464 | tf_op jit(solution)/shard_map/all_gather | solution.py:525
  9.9 1.9 copy-start.3
  11.2 372.1 %all-gather.5.cloned.1.call-start = ((), (), s32[]{:S(2)}) async-start(), calls=%async_computation.1 | async-start | bytes 24510464 | tf_op jit(solution)/shard_map/all_gather | solution.py:534
  20.5 95.0 %copy-start = (bf16[2,1,4096,86]{2,0,3,1:T(2,128)(2,1)S(1)}, bf16[2,1,4096,86]{2,0,3,1:T(2,128)(2,1)}, u32[]{:S(2)}) copy-start(bf16[2,1,4096,86]{2,0,3,1:T(2,128)(2,1)} %param.11) | copy-start | bytes 4227076
  115.5 1.4 copy-start.1
  117.8 1.3 copy-start.6
  117.8 1.9 copy-start.2
  120.4 1.4 copy-start.5
  120.4 2.0 copy-start.4
Sparse Core Ops, SparseCore 0:
  11.4 146.4 all-gather.2
  160.0 186.4 all-gather.4

commit v5 on v0

v5 whole, which is shorter than its diff:
```python
import jax
import jax.numpy as jnp
from jax import lax
from jax.experimental import pallas as pl
from jax.experimental.pallas import tpu as pltpu
from jax.sharding import PartitionSpec as P

NORM_EPS = 1e-5
TB = 256
TB2 = 512
NB = 8
D = 4096
DS = 512
F = 86
FP = 88
FA = 48
RA = 96
RB = 80
RE = 176
KP = 768
E = 16
K = 4
STEPS = 4
GE = 4
GROWS = GE * RE
BF = jnp.bfloat16
F32 = jnp.float32
MESH = pl.DeviceIdType.MESH
DMA = pltpu.SemaphoreType.DMA
ANY = pl.BlockSpec(memory_space=pl.ANY)
IN_VMEM = pl.BlockSpec(memory_space=pltpu.VMEM)
PEERS = [(s, o) for s in range(4) for o in range(2) if s + o]


def shape(dims, dtype=BF):
    return jax.ShapeDtypeStruct(dims, dtype)


def params(collective_id):
    return pltpu.CompilerParams(vmem_limit_bytes=62_000_000, collective_id=collective_id, has_side_effects=True)


def cost(micros):
    return pl.CostEstimate(flops=micros * 1_000_000_000, bytes_accessed=10_000_000, transcendentals=0)


def remote(src, dst, send_sem, recv_sem, device):
    return pltpu.make_async_remote_copy(src_ref=src, dst_ref=dst, send_sem=send_sem, recv_sem=recv_sem, device_id=device, device_id_type=MESH)


def fsdp_at(step, other=0):
    f = lax.axis_index("fsdp")
    core = f % 2
    return lax.rem(f // 2 + step, 4) * 2 + (1 - core if other else core)


def greet(devices):
    barrier = pltpu.get_barrier_semaphore()
    for d in devices:
        pl.semaphore_signal(barrier, inc=1, device_id=d, device_id_type=MESH)
    pl.semaphore_wait(barrier, len(devices))


class Ring:
    def __init__(self, pos, dev, own, place, chunks, send_sem, recv_sem, partner=None):
        self.pos, self.dev, self.own, self.place, self.chunks = pos, dev, own, place, chunks
        self.send_sem, self.recv_sem, self.partner = send_sem, recv_sem, partner
        self.right, self.left, self.far = [lax.rem(pos + s, 4) for s in (1, 3, 2)]

    def copy(self, kind, k, src, dst, device):
        return remote(src, dst, self.send_sem.at[kind, k], self.recv_sem.at[kind, k], device)

    def own_copies(self, k):
        mine = self.place(self.pos, k)
        out = [self.copy(0, k, self.own(k), mine, self.dev(self.right)), self.copy(1, k, self.own(k), mine, self.dev(self.left))]
        if self.partner is not None:
            out.append(self.copy(3, k, self.own(k), mine, self.partner))
        return out

    def onward(self, k, odd):
        source, target = (self.right, self.left) if odd else (self.left, self.right)
        ref = self.place(source, k)
        return self.copy(2, k, ref, ref, self.dev(target))

    def across(self, kind, k):
        ref = self.place({4: self.left, 5: self.right, 6: self.far}[kind], k)
        return self.copy(kind, k, ref, ref, self.partner)

    def arrived(self, kind, k, pos, *other):
        ref = self.place(pos, k, *other)
        self.copy(kind, k, ref, ref, self.dev(self.right)).wait_recv()

    def start(self, k):
        for c in self.own_copies(k):
            c.start()

    def relay(self, k, odd):
        for kind, pos, onward in ((0, self.left, not odd), (1, self.right, odd)):
            self.arrived(kind, k, pos)
            if onward:
                self.onward(k, odd).start()
            if self.partner is not None:
                self.across(4 + kind, k).start()

    def last(self, k):
        self.arrived(2, k, self.far)
        if self.partner is not None:
            self.across(6, k).start()

    def from_partner(self, k):
        for kind, pos in ((3, self.pos), (4, self.left), (5, self.right), (6, self.far)):
            self.arrived(kind, k, pos, 1)

    def drain(self):
        for k in range(self.chunks):
            for c in self.own_copies(k):
                c.wait_send()
            self.onward(k, k % 2 == 1).wait_send()
            if self.partner is not None:
                for kind in (4, 5, 6):
                    self.across(kind, k).wait_send()


def x_ring(own, place, send_sem, recv_sem):
    f = lax.axis_index("fsdp")
    core = f % 2

    def where(p, k, other=0):
        return place(p * 2 + (1 - core if other else core), k)

    return Ring(f // 2, lambda p: {"fsdp": p * 2 + core}, own, where, NB, send_sem, recv_sem, {"fsdp": fsdp_at(0, 1)})


X_SEMS = [DMA((7, NB)), DMA((7, NB))]
FIRST_SEMS = [DMA((2, 3, 2)), DMA((2, 3, 2))]
SECOND_SEMS = [DMA((2, 3, 4)), DMA((2, 3, 4))]


def x_neighbours():
    return [{"fsdp": fsdp_at(1)}, {"fsdp": fsdp_at(3)}, {"fsdp": fsdp_at(0, 1)}]


def yz():
    e = lax.axis_index("ep")
    z, y = e // 4, e % 4
    return z, y, (lambda p: {"ep": p * 4 + y}), (lambda p: {"ep": z * 4 + p})


def yz_neighbours():
    z, y, on_z, on_y = yz()
    return [f(lax.rem(p + s, 4)) for f, p in ((on_z, z), (on_y, y)) for s in (1, 3)]


def cut(ref, lanes, half, chunk=None):
    size = ref.shape[1 if lanes else 0] // 2
    span = pl.ds(half * size, size) if chunk is None else pl.ds(half * size + chunk * (size // 2), size // 2)
    return ref.at[:, span] if lanes else ref.at[span]


def first_rings(own, full, lanes, sems):
    z, y, on_z, on_y = yz()
    send, recv = sems
    return [
        Ring(y, on_y, lambda k: cut(own, lanes, 0, k), lambda p, k: cut(full.at[z * 4 + p], lanes, 0, k), 2, send.at[0], recv.at[0]),
        Ring(z, on_z, lambda k: cut(own, lanes, 1, k), lambda p, k: cut(full.at[p * 4 + y], lanes, 1, k), 2, send.at[1], recv.at[1]),
    ]


def second_rings(full, lanes, sems):
    z, y, on_z, on_y = yz()
    send, recv = sems
    by_z = lambda p, k: cut(full.at[p * 4 + k], lanes, 0)
    by_y = lambda p, k: cut(full.at[k * 4 + p], lanes, 1)
    return [
        Ring(z, on_z, lambda k: by_z(z, k), by_z, 4, send.at[0], recv.at[0]),
        Ring(y, on_y, lambda k: by_y(y, k), by_y, 4, send.at[1], recv.at[1]),
    ]


def start(rings):
    for k in range(rings[0].chunks):
        for r in rings:
            r.start(k)


def relay(rings, k):
    for r in rings:
        r.relay(k, k % 2 == 1)


def finish(rings):
    for r in rings:
        for k in range(r.chunks):
            r.last(k)
        r.drain()


def norm_block(view, nw_ref, stage, h_stage, h_out, sems, tok_major):
    load = pltpu.make_async_copy(view, stage, sems.at[0])
    load.start()
    load.wait()
    for tb in range(2):
        def rows(c, tb=tb):
            return (stage[tb, c] if tok_major else stage[c, tb]).astype(F32)

        def ssq_body(c, acc):
            xf = rows(c)
            return acc + jnp.sum(xf * xf, axis=0, keepdims=True)

        ssq = lax.fori_loop(0, NB, ssq_body, jnp.zeros((1, TB), F32))
        rstd = lax.rsqrt(ssq * (1.0 / D) + NORM_EPS)

        def h_body(c, carry, tb=tb, rstd=rstd):
            nw = nw_ref[c]
            nw2 = jnp.concatenate([nw, nw], axis=1)
            h_stage[pl.ds(pl.multiple_of(c * DS, DS), DS), tb * TB:(tb + 1) * TB] = (rows(c) * rstd * nw2).astype(BF)
            return carry

        lax.fori_loop(0, NB, h_body, 0)
    store = pltpu.make_async_copy(h_stage, h_out, sems.at[1])
    store.start()
    store.wait()


def first_kernel(
    x_ref, nw_ref, w_ref, idx_ref, wd_ref, x_all, h_all, w_all, idx_all, wd_all, wd_next,
    stage, h_stage, wd_in, wd_out, local_sem, norm_sem, small_send, small_recv, *sems,
):
    f, e = lax.axis_index("fsdp"), lax.axis_index("ep")
    greet([{"fsdp": fsdp_at(s, o)} for s, o in PEERS] + yz_neighbours())
    ring = x_ring(lambda k: x_ref.at[k], lambda owner, k: x_all.at[owner, k], *sems[:2])
    w_first = first_rings(w_ref, w_all, True, sems[2:4])
    w_second = second_rings(w_all, True, sems[4:6])
    d_first = first_rings(wd_out.at[0], wd_all, False, sems[6:])
    own = [pltpu.make_async_copy(src, dst, local_sem.at[i])
           for i, (src, dst) in enumerate((
               (w_ref, w_all.at[e]), (x_ref, x_all.at[f]), (wd_ref.at[:, f], wd_in.at[:, f]), (idx_ref, idx_all.at[f])))]
    after = [pltpu.make_async_copy(wd_out.at[0], wd_all.at[e], local_sem.at[4]), pltpu.make_async_copy(wd_out.at[1], wd_next, local_sem.at[5])]
    small = []
    for p, (s, o) in enumerate(PEERS):
        peer = fsdp_at(s, o)
        small.append(remote(wd_ref.at[:, peer], wd_in.at[:, f], small_send.at[0, p], small_recv.at[0, p], {"fsdp": peer}))
        small.append(remote(idx_ref, idx_all.at[f], small_send.at[1, p], small_recv.at[1, p], {"fsdp": peer}))
    start(w_first)
    for c in small + own:
        c.start()
    for k in range(NB):
        ring.start(k)
    for p, (s, o) in enumerate(PEERS):
        source = fsdp_at((4 - s) % 4, o)
        remote(wd_ref.at[:, 0], wd_in.at[:, source], small_send.at[0, p], small_recv.at[0, p], {"fsdp": source}).wait_recv()
        remote(idx_ref, idx_all.at[source], small_send.at[1, p], small_recv.at[1, p], {"fsdp": source}).wait_recv()
    for c in own[2:]:
        c.wait()
    for l in range(2):
        wd_out[l, :, :NB * FP] = jnp.swapaxes(wd_in[l].reshape(NB * FP, DS), 0, 1)
        wd_out[l, :, NB * FP:] = jnp.zeros((DS, KP - NB * FP), BF)
    relay(w_first, 0)
    for k in range(NB):
        ring.relay(k, k % 2 == 1)
        if k == 0:
            relay(w_first, 1)
            for c in after:
                c.start()
            start(d_first)
        if k == 3:
            finish(w_first)
            own[0].wait()
            start(w_second)
        if k in (5, 6):
            relay(d_first, k - 5)
    for k in range(NB):
        ring.last(k)
        if k in (0, 4):
            relay(w_second, k // 4)
    for k in range(NB):
        ring.from_partner(k)
    own[1].wait()
    for i in range(STEPS):
        if i < 2:
            relay(w_second, i + 2)
        norm_block(x_all.at[pl.ds(2 * i, 2)], nw_ref, stage, h_stage, h_all.at[i], norm_sem, True)
    finish(d_first)
    for c in after:
        c.wait()
    finish(w_second)
    ring.drain()
    for c in small:
        c.wait_send()


def first_exchange(xt, nw, w, idx, wd):
    return pl.pallas_call(
        first_kernel,
        out_shape=(
            shape((NB, NB, DS, TB)), shape((STEPS, D, TB2)), shape((E,) + w.shape), shape((NB,) + idx.shape, jnp.int32),
            shape((E, DS, KP)), shape((DS, KP))),
        in_specs=[IN_VMEM] * 5,
        out_specs=[ANY] * 6,
        scratch_shapes=[
            pltpu.VMEM((2, NB, DS, TB), BF), pltpu.VMEM((D, TB2), BF), pltpu.VMEM((2, NB, FP, DS), BF), pltpu.VMEM((2, DS, KP), BF),
            DMA((6,)), DMA((2,)), DMA((2, 7)), DMA((2, 7)),
        ] + X_SEMS + FIRST_SEMS + SECOND_SEMS + FIRST_SEMS,
        compiler_params=params(1),
        cost_estimate=cost(120),
        name="first_exchange",
    )(xt, nw, w, idx, wd)


def up_kernel(split, h_ref, idx_ref, rt_hbm, wd_part, *refs):
    w_refs, refs = refs[:1 + split], refs[1 + split:]
    a_all, g_ref, wd_all, wv, slots, logits, a_buf, w_sem, rt_sem, local_sem = refs[:10]
    sems = refs[10:]
    step = pl.program_id(0)
    f = lax.axis_index("fsdp")
    mine = lambda owner: pl.ds(pl.multiple_of(owner * FP, 8), FP)
    ring = x_ring(lambda k: a_buf.at[k], lambda owner, k: a_all.at[k, :, mine(owner)], *sems[:2])
    second = second_rings(wd_all, False, sems[2:])

    def own_a(k):
        return pltpu.make_async_copy(a_buf.at[k], a_all.at[k, :, mine(f)], local_sem.at[k])

    def loads(g):
        out = [pltpu.make_async_copy(rt_hbm, wv.at[g, pl.ds(GROWS, E)], rt_sem.at[g])]
        for i in range(GE):
            at = 0
            for n, w in enumerate(w_refs):
                size = w.shape[1]
                out.append(pltpu.make_async_copy(w.at[g * GE + i], wv.at[g, pl.ds(i * RE + at, size)], w_sem.at[g, n, i]))
                at += size
        return out

    @pl.when(step == 0)
    def _():
        for g in range(STEPS):
            for c in loads(g):
                c.start()
        greet(x_neighbours() + yz_neighbours())
        start(second)

    slots[...] = jnp.zeros_like(slots)
    idx = jnp.concatenate([idx_ref[0], idx_ref[1]], axis=1)

    def group(g, carry):
        tick = step * STEPS + g

        @pl.when(step == 0)
        def _():
            for c in loads(g):
                c.wait()

        @pl.when(jnp.logical_and(step >= 1, g == 3))
        def _():
            for tb in range(2):
                ring.relay(2 * step - 2 + tb, tb == 1)

        for k in range(4):
            @pl.when(tick == 4 + 3 * k)
            def _(k=k):
                relay(second, k)

        res = jnp.dot(wv[g], h_ref[0], preferred_element_type=F32)
        logits[...] = res[GROWS:]
        for i in range(GE):
            at, parts = i * RE, []
            for n in (FA, FP - FA):
                parts.append(jax.nn.silu(res[at:at + n]) * res[at + n:at + 2 * n])
                at += 2 * n
            act = jnp.concatenate(parts, axis=0)
            for j in range(K):
                slots[j] = jnp.where(idx[j:j + 1] == g * GE + i, act, slots[j])
        return carry

    lax.fori_loop(0, STEPS, group, 0)
    for tb in range(2):
        a_buf[2 * step + tb] = slots[:, :, tb * TB:(tb + 1) * TB].astype(BF)
    eids = lax.broadcasted_iota(jnp.int32, (E, TB2), 0)
    chosen = idx[0:1] == eids
    for j in range(1, K):
        chosen = jnp.logical_or(chosen, idx[j:j + 1] == eids)
    lg = jnp.where(chosen, logits[...], -jnp.inf)
    ex = jnp.where(chosen, jnp.exp(lg - jnp.max(lg, axis=0, keepdims=True)), 0.0)
    gates = ex / jnp.sum(ex, axis=0, keepdims=True)
    for tb in range(2):
        g_ref[tb] = gates[:, tb * TB:(tb + 1) * TB]
    for tb in range(2):
        ring.start(2 * step + tb)
        own_a(2 * step + tb).start()

    @pl.when(step == 3)
    def _():
        for k in (6, 7):
            ring.relay(k, k % 2 == 1)
        for k in range(NB):
            ring.last(k)
        for k in range(NB):
            ring.from_partner(k)
            own_a(k).wait()
        ring.drain()
        finish(second)


def pair(*tail):
    return pl.BlockSpec((2,) + tail, lambda i: (i,) + (0,) * len(tail))


def whole(*dims):
    return pl.BlockSpec(dims, lambda i: (0,) * len(dims))


def up_proj(h, idx, rt, wd_part, ws):
    split = len(ws) - 1
    return pl.pallas_call(
        lambda *refs: up_kernel(split, *refs),
        grid=(STEPS,),
        out_shape=(shape((NB, K, NB * FP, TB)), shape((NB, E, TB), F32), shape((E, DS, KP))),
        in_specs=[pl.BlockSpec((1, D, TB2), lambda i: (i, 0, 0)), pair(K, TB), ANY, ANY] + [ANY] * len(ws),
        out_specs=(ANY, pair(E, TB), ANY),
        scratch_shapes=[
            pltpu.VMEM((STEPS, GROWS + E, D), BF),
            pltpu.VMEM((K, FP, TB2), F32),
            pltpu.VMEM((E, TB2), F32),
            pltpu.VMEM((NB, K, FP, TB), BF),
            DMA((STEPS, 2, GE)), DMA((STEPS,)), DMA((NB,)),
        ] + X_SEMS + SECOND_SEMS,
        input_output_aliases={3: 2},
        compiler_params=params(2 + split),
        cost_estimate=cost(70),
        name="up_proj",
    )(h, idx, rt, wd_part, *ws)


def down_block(a_ref, idx_ref, g_ref, wd_ref, acc, hook):
    idx = jnp.concatenate([idx_ref[0], idx_ref[1]], axis=1).astype(F32).astype(BF)
    acc[...] = jnp.zeros_like(acc)

    def group(g, carry):
        hook(g)
        for i in range(GE):
            e = g * GE + i
            ef = e.astype(F32).astype(BF)
            parts = []
            for tb in range(2):
                sel = jnp.zeros((NB * FP, TB), BF)
                for j in range(K):
                    row = idx[j:j + 1, tb * TB:(tb + 1) * TB]
                    sel = jnp.where(row == ef, a_ref[tb, j], sel)
                parts.append(sel)
            out = jnp.dot(wd_ref[e, :, :NB * FP], jnp.concatenate(parts, axis=1), preferred_element_type=F32)
            gate = jnp.concatenate([g_ref[0, pl.ds(e, 1)], g_ref[1, pl.ds(e, 1)]], axis=1)
            acc[...] += gate * out
        return carry

    lax.fori_loop(0, STEPS, group, 0)


def new_x(x, acc, tb):
    return (x.astype(F32) + acc[:, tb * TB:(tb + 1) * TB]).astype(BF)


def down_mid_kernel(
    a_ref, idx_ref, g_ref, x_ref, wd_ref, nw_ref, wd_next, x_all, h_all, wd_all, acc, o_buf, stage, h_stage, local_sem, norm_sem, *sems,
):
    step = pl.program_id(0)
    f = lax.axis_index("fsdp")
    ring = x_ring(lambda k: o_buf.at[k], lambda owner, k: x_all.at[owner, k], *sems[:2])
    d_first = first_rings(wd_next, wd_all, False, sems[2:])
    own_wd = pltpu.make_async_copy(wd_next, wd_all.at[lax.axis_index("ep")], local_sem.at[NB])

    def own_x(k):
        return pltpu.make_async_copy(o_buf.at[k], x_all.at[f, k], local_sem.at[k])

    @pl.when(step == 0)
    def _():
        greet(x_neighbours() + yz_neighbours())
        own_wd.start()
        start(d_first)

    def hook(g):
        @pl.when(jnp.logical_and(step >= 2, g == 2))
        def _():
            for tb in range(2):
                ring.relay(2 * step - 4 + tb, tb == 1)
            for k in range(2):
                @pl.when(step == 2 + k)
                def _(k=k):
                    relay(d_first, k)

    down_block(a_ref, idx_ref, g_ref, wd_ref, acc, hook)
    for tb in range(2):
        o_buf[2 * step + tb] = new_x(x_ref[tb, 0], acc, tb)
    for tb in range(2):
        ring.start(2 * step + tb)
        own_x(2 * step + tb).start()

    @pl.when(step == 3)
    def _():
        for i in range(STEPS):
            for k in (2 * i, 2 * i + 1):
                ring.last(k)
            for k in (2 * i, 2 * i + 1):
                ring.from_partner(k)
                own_x(k).wait()
            norm_block(x_all.at[:, pl.ds(2 * i, 2)], nw_ref, stage, h_stage, h_all.at[i], norm_sem, False)
            if i < 2:
                for k in (2 * i + 4, 2 * i + 5):
                    ring.relay(k, k % 2 == 1)
        ring.drain()
        own_wd.wait()
        finish(d_first)


def down_mid(a, idx, gates, x_all, wd, nw, wd_next):
    return pl.pallas_call(
        down_mid_kernel,
        grid=(STEPS,),
        out_shape=(shape((NB, NB, DS, TB)), shape((STEPS, D, TB2)), shape((E, DS, KP))),
        in_specs=[
            pair(K, NB * FP, TB), pair(K, TB), pair(E, TB),
            pl.BlockSpec((2, 1, DS, TB), lambda i: (i, lax.axis_index("fsdp"), 0, 0)),
            whole(E, DS, KP), whole(NB, DS, 128), whole(DS, KP),
        ],
        out_specs=[ANY] * 3,
        scratch_shapes=[
            pltpu.VMEM((DS, TB2), F32), pltpu.VMEM((NB, DS, TB), BF), pltpu.VMEM((NB, 2, DS, TB), BF), pltpu.VMEM((D, TB2), BF),
            DMA((NB + 1,)), DMA((2,)),
        ] + X_SEMS + FIRST_SEMS,
        compiler_params=params(4),
        cost_estimate=cost(80),
        name="down_mid",
    )(a, idx, gates, x_all, wd, nw, wd_next)


def down_last_kernel(a_ref, idx_ref, g_ref, x_ref, wd_ref, o_all, acc, o_buf, send_sem, recv_sem, local_sem):
    step = pl.program_id(0)
    f = lax.axis_index("fsdp")
    core = f % 2

    @pl.when(step == 0)
    def _():
        greet([{"fsdp": fsdp_at(s, o)} for s, o in PEERS])

    down_block(a_ref, idx_ref, g_ref, wd_ref, acc, lambda g: None)
    for tb in range(2):
        o_buf[step, tb] = new_x(x_ref[0, tb], acc, tb)

    def send(s, o):
        return remote(o_buf.at[(s + 3) % 4, 1 - core if o else core], o_all.at[f], send_sem.at[s, o], recv_sem.at[s, o], {"fsdp": fsdp_at(s, o)})

    for s in range(1, 4):
        @pl.when(step == s - 1)
        def _(s=s):
            send(s, 0).start()
            send(s, 1).start()

    @pl.when(step == 3)
    def _():
        send(0, 1).start()
        mine = pltpu.make_async_copy(o_buf.at[3, core], o_all.at[f], local_sem)
        mine.start()
        for s, o in PEERS:
            source = fsdp_at((4 - s) % 4, o)
            remote(o_buf.at[0, 0], o_all.at[source], send_sem.at[s, o], recv_sem.at[s, o], {"fsdp": source}).wait_recv()
        for s, o in PEERS:
            send(s, o).wait_send()
        mine.wait()


def down_last(a, idx, gates, x_all, wd):
    block = lambda i: lax.rem(lax.axis_index("fsdp") // 2 + 1 + i, 4)

    def turned(*tail):
        return pl.BlockSpec((2,) + tail, lambda i: (block(i),) + (0,) * len(tail))

    return pl.pallas_call(
        down_last_kernel,
        grid=(STEPS,),
        out_shape=shape((NB, DS, TB)),
        in_specs=[
            turned(K, NB * FP, TB), turned(K, TB), turned(E, TB),
            pl.BlockSpec((1, 2, DS, TB), lambda i: (lax.axis_index("fsdp"), block(i), 0, 0)),
            whole(E, DS, KP),
        ],
        out_specs=ANY,
        scratch_shapes=[pltpu.VMEM((DS, TB2), F32), pltpu.VMEM((STEPS, 2, DS, TB), BF), DMA((4, 2)), DMA((4, 2)), DMA],
        compiler_params=params(5),
        cost_estimate=cost(45),
        name="down_last",
    )(a, idx, gates, x_all, wd)


def solution(mesh):
    tok_spec = P(("rep", "ep", "fsdp"), None)
    idx_spec = P(None, ("rep", "ep", "fsdp"), None)
    in_specs = (tok_spec, P(None, None), P(None, None, None), P(None, "ep", None, "fsdp"), P(None, "ep", None, "fsdp"), P(None, "ep", "fsdp", None), idx_spec)

    def local_program(x, norm_w, router_w, w_gate, w_up, w_down, expert_idx):
        pad = jnp.zeros((FP - F, D), BF)
        nws = [jnp.broadcast_to(n.reshape(NB, DS, 1), (NB, DS, 128)) for n in norm_w]
        routers = [r.T for r in router_w]

        def pack(gate, up):
            gate, up = gate.T, up.T
            return [gate[:FA], up[:FA]], [gate[FA:], pad, up[FA:], pad]

        part_a, part_b = [jnp.concatenate(p, axis=0) for p in pack(w_gate[0, 0], w_up[0, 0])]
        w_a = lax.all_gather(part_a, "ep", axis=0, tiled=False)
        gate1, up1, _ = lax.optimization_barrier((w_gate, w_up, part_a))
        one, two = pack(gate1[1, 0], up1[1, 0])
        rows = jnp.concatenate(one + two, axis=0)
        wd = jnp.pad(w_down[:, 0], ((0, 0), (0, FP - F), (0, 0))).reshape(2, FP, NB, DS).swapaxes(1, 2)
        xt = x.T.reshape(NB, DS, TB)
        xt, idx, wd, part_b, rows = lax.optimization_barrier((xt, jnp.swapaxes(expert_idx, 1, 2), wd, part_b, rows))
        x_all, h, w_b, idx, wd_part, wd_next = first_exchange(xt, nws[0], part_b, idx, wd)
        rows, _ = lax.optimization_barrier((rows, idx))
        w_next = lax.all_gather(rows, "ep", axis=0, tiled=False)
        a, gates, wd_all = up_proj(h, idx[:, 0], routers[0], wd_part, (w_a, w_b))
        x_all, h, wd_part = down_mid(a, idx[:, 0], gates, x_all, wd_all, nws[1], wd_next)
        a, gates, wd_all = up_proj(h, idx[:, 1], routers[1], wd_part, (w_next,))
        return down_last(a, idx[:, 1], gates, x_all, wd_all).reshape(D, TB).T

    return jax.shard_map(local_program, mesh=mesh, in_specs=in_specs, out_specs=tok_spec, check_vma=False)
```

time: 3470 us -> 502 us (0.14)
  waiting for transfers between devices: 2330 us -> 0.06 us
  local copies, waits for them, and re-layouts: 679 us -> 35.4 us
  Pallas kernels: 310 us -> 450 us
  other arithmetic: 112 us -> 1.95 us
    all_gather x12 -> x2, waiting for transfers between devices: 2330 us -> 0.02 us  [the longest x1 0.02 us: local_program(): w_next = lax.all_gather(rows, 'ep', axis=0, tiled=False)]
    all_gather x10 -> x0, local copies, waits for them, and re-layouts: 537 us -> none  [the longest x2 229 us: local_program(): lax.all_gather(lax.all_gather(w_up[layer_num], 'fsdp', axis=2, tiled=True...]
    pallas_call x0 -> x5, Pallas kernels: none -> 450 us  [the longest x2 175 us: up_proj(): pl.pallas_call(lambda *refs: up_kernel(split, *refs), grid=(STEPS,), out_...]
    another operation x6 -> x0, Pallas kernels: 307 us -> none
    gather x10 -> x0, local copies, waits for them, and re-layouts: 74.5 us -> none  [the longest x2 40.8 us: routed_ffn(): jnp.take(sorted_out, slot_pos, axis=0).reshape(tok_count, top_k, -1)]
    select_n x6 -> x0, other arithmetic: 39.6 us -> none  [the longest x2 24 us: routed_ffn(): jnp.take(sorted_out, slot_pos, axis=0).reshape(tok_count, top_k, -1)]
  transfers between devices with their start and end apart: 12 -> 2, of which waited for: 12 -> 0; matrix products, arithmetic and copies ran while one was open for 21% -> 5% of each run, Pallas kernels for 7% -> 64%
where the time goes in v5:
time: 502 us; the launch traced here: 501 us
  Pallas kernels  450 us (90%)
  local copies, waits for them, and re-layouts  35.4 us (7%)
  between operations  13.6 us (3%)
    pallas_call x2, Pallas kernels, up_proj(): pl.pallas_call(lambda *refs: up_kernel(split, *refs), grid=(STEPS,), out_...  175 us
    pallas_call x1, Pallas kernels, first_exchange(): pl.pallas_call(first_kernel, out_shape=(shape((NB, NB, DS, TB)), shape((S...  130 us
    pallas_call x1, Pallas kernels, down_mid(): pl.pallas_call(down_mid_kernel, grid=(STEPS,), out_shape=(shape((NB, NB,...  97.3 us
    pallas_call x1, Pallas kernels, down_last(): pl.pallas_call(down_last_kernel, grid=(STEPS,), out_shape=shape((NB, DS,...  48.3 us
  transfers between devices with their start and end apart: 2, of which 0 were waited for; matrix products, arithmetic and copies ran while one was open for 5% of the time, Pallas kernels for 64%

profile of v5, /device:TPU:1, one launch (start us, length us, event | category | flops | bytes accessed | tf_op | source)
XLA Modules:
  0.0 501.4 jit_solution(14974934766078719629)
XLA Ops:
  6.5 0.0 copy-start.1
  6.5 0.0 all-gather.5.cloned.1.call-start
  6.5 2.2 copy.38
  8.8 0.0 copy-done.1
  8.8 0.8 copy.37
  9.6 0.0 copy-start.2
  9.6 0.8 copy-done.2
  10.5 0.0 copy-start
  10.5 1.0 pad_maximum_fusion
  11.5 0.0 all-gather.5.cloned.1.call-update
  11.6 0.0 all-gather.7.cloned.1.call-start
  11.6 0.5 copy-done
  12.1 0.8 copy.22
  12.9 0.0 copy-start.3
  13.0 0.9 copy-done.3
  13.8 0.8 copy.23
  14.7 0.0 copy-start.4
  14.7 0.0 copy-start.6
  14.7 0.8 slice.58
  15.5 1.7 slice.59
  17.2 0.0 copy-done.4
  17.2 0.0 copy-done.6
  17.2 1.5 pad.4
  18.8 1.2 reshape.16
  20.0 0.0 copy-start.5
  20.0 1.9 copy.36
  21.9 0.0 copy-done.5
  21.9 0.0 slice-start
  21.9 0.0 slice-start.1
  21.9 0.0 slice-start.2
  21.9 0.0 slice-start.3
  21.9 2.5 copy.17
  24.4 0.0 copy-start.7
  24.4 0.0 copy-start.8
  24.4 0.0 slice-done
  24.4 0.0 slice-done.1
  24.4 0.0 slice-done.2
  24.5 0.0 slice-done.3
  24.5 0.0 copy-start.10
  24.5 8.6 %concatenate.11 = bf16[176,4096]{1,0:T(8,128)(2,1)} concatenate(bf16[48,4096]{1,0:T(8,128)(2,1)S(1)} %slice-done, bf16[48,4096]{1,0:T(8,128)(2,1)S(1)} %slice-done.2, bf16[38,4096]{1,0:T(8,128)(2,1)S(1)} %slice-done.1, bf16[2,4096]{1,0:T(2,128)(2,1)S(1)} %broadcast_in_dim.17, bf16[38,4096]{1,0:T(8,128)(2,1)S(1)} %slice-done.3, bf16[2,4096]{1,0:T(2,128)(2,1)S(1)} %broadcast_in_dim.17), dimensions={0} | concatenate | bytes 2883584 | tf_op jit(solution)/shard_map/concatenate | solution.py:610
  33.1 0.0 copy-done.7
  33.1 0.0 copy-done.8
  33.1 0.9 pad_maximum_fusion.1.w_ref
  34.0 0.0 copy-done.10
  34.0 0.1 slice_reduce_fusion
  34.1 1.9 broadcast_in_dim.19.nw_ref
  36.0 130.1 %first_exchange.1 = (bf16[8,8,512,256]{3,2,1,0:T(8,128)(2,1)}, bf16[4,4096,512]{2,1,0:T(8,128)(2,1)}, bf16[16,80,4096]{2,1,0:T(8,128)(2,1)}, s32[8,2,4,256]{3,2,...) custom-call(bf16[8,512,256]{2,1,0:T(8,128)(2,1)} %bitcast.52, ...), custom_call_target="tpu_custom_call" | custom-call | flops 120000004096 | bytes 10000000 | tf_op jit(solution)/shard_map/first_exchange/pallas_call | solution.py:293
  166.2 0.0 copy-start.9
  166.2 0.0 all-gather.7.cloned.1.call-update
  166.2 1.4 slice_bitcast_fusion.4
  167.7 0.0 copy-done.9
  167.7 0.7 slice_bitcast_fusion.2
  168.4 0.0 all-gather.5.cloned.1.call-done
  168.4 94.5 %up_proj.2 = (bf16[8,4,704,256]{3,2,1,0:T(8,128)(2,1)}, f32[8,16,256]{2,1,0:T(8,128)}, bf16[16,512,768]{2,1,0:T(8,128)(2,1)}) custom-call(bf16[4,4096,512]{2,1,0:T(8,128)(2,1)} %get-tuple-element.34.refs_0_, s32[8,4,256]{2,1,0:T(4,128)} %get-tuple-element.56.refs_1_.idx_ref, ...), custom_call_target="tpu_custom_call", output_to_operand_aliasing={{2}: (3, {})} | custom-call | flops 70000001024 | bytes 10000000 | tf_op jit(solution)/shard_map/up_proj/pallas_call | solution.py:413
  262.9 1.9 broadcast_in_dim.21.nw_ref
  264.8 97.3 %down_mid.1 = (bf16[8,8,512,256]{3,2,1,0:T(8,128)(2,1)}, bf16[4,4096,512]{2,1,0:T(8,128)(2,1)}, bf16[16,512,768]{2,1,0:T(8,128)(2,1)}) custom-call(bf16[8,4,704,256]{3,2,1,0:T(8,128)(2,1)} %get-tuple-element.38.a_ref, s32[8,4,256]{2,1,0:T(4,128)} %get-tuple-element.56.refs_1_.idx_ref, f32[8,16,256]{2,1,0:T(8,128)} %get-tuple-element.39.g_ref, ...), custom_call_target="tpu_custom_call" | custom-call | flops 80000000000 | bytes 10000000 | tf_op jit(solution)/shard_map/down_mid/pallas_call | solution.py:514
  362.1 0.0 all-gather.7.cloned.1.call-done
  362.1 80.1 %up_proj.3 = (bf16[8,4,704,256]{3,2,1,0:T(8,128)(2,1)}, f32[8,16,256]{2,1,0:T(8,128)}, bf16[16,512,768]{2,1,0:T(8,128)(2,1)}) custom-call(bf16[4,4096,512]{2,1,0:T(8,128)(2,1)} %get-tuple-element.43.refs_0_, s32[8,4,256]{2,1,0:T(4,128)} %get-tuple-element.55.refs_1_.idx_ref, ...), custom_call_target="tpu_custom_call", output_to_operand_aliasing={{2}: (3, {})} | custom-call | flops 70000001024 | bytes 10000000 | tf_op jit(solution)/shard_map/up_proj/pallas_call | solution.py:413
  442.2 48.3 %down_last.1 = bf16[8,512,256]{2,1,0:T(8,128)(2,1)} custom-call(bf16[8,4,704,256]{3,2,1,0:T(8,128)(2,1)} %get-tuple-element.47.a_ref, s32[8,4,256]{2,1,0:T(4,128)} %get-tuple-element.55.refs_1_.idx_ref, f32[8,16,256]{2,1,0:T(8,128)} %get-tuple-element.48.g_ref, bf16[8,8,512,256]{3,2,1,0:T(8,128)(2,1)} %get-tuple-element.49.x_ref, ...), custom_call_target="tpu_custom_call" | custom-call | flops 44999999488 | bytes 10000000 | tf_op jit(solution)/shard_map/down_last/pallas_call | solution.py:575
  490.5 4.1 copy.26
  (7 shorter events, 0.2 us)
Async XLA Ops:
  6.5 2.3 copy-start.1
  6.5 161.8 %all-gather.5.cloned.1.call-start = ((), (), s32[]{:S(2)}) async-start(), calls=%async_computation | async-start | bytes 13369344 | tf_op jit(solution)/shard_map/all_gather | solution.py:607
  9.6 0.9 copy-start.2
  10.5 1.6 copy-start
  11.6 350.6 %all-gather.7.cloned.1.call-start = ((), (), s32[]{:S(2)}) async-start(), calls=%async_computation.1 | async-start | bytes 24510464 | tf_op jit(solution)/shard_map/all_gather | solution.py:616
  12.9 0.9 copy-start.3
  14.7 2.5 copy-start.4
  14.7 2.5 copy-start.6
  20.0 1.9 copy-start.5
  21.9 2.5 slice-start
  21.9 2.5 slice-start.1
  21.9 2.5 slice-start.2
  21.9 2.5 slice-start.3
  24.4 8.7 %copy-start.7 = (bf16[38,4096]{1,0:T(8,128)(2,1)S(1)}, bf16[38,4096]{1,0:T(8,128)(2,1)}, u32[]{:S(2)}) copy-start(bf16[38,4096]{1,0:T(8,128)(2,1)} %slice.58) | copy-start | bytes 933892
  24.4 8.7 %copy-start.8 = (bf16[38,4096]{1,0:T(8,128)(2,1)S(1)}, bf16[38,4096]{1,0:T(8,128)(2,1)}, u32[]{:S(2)}) copy-start(bf16[38,4096]{1,0:T(8,128)(2,1)} %slice.59) | copy-start | bytes 933892
  24.5 9.5 %copy-start.10 = (f32[2,4096]{1,0:T(2,128)S(1)}, f32[2,4096]{1,0:T(2,128)}, u32[]{:S(2)}) copy-start(f32[2,4096]{1,0:T(2,128)} %param.8) | copy-start | bytes 98308
  166.2 1.5 copy-start.9
Sparse Core Ops, SparseCore 0:
  11.7 131.2 all-gather.4
  166.3 188.8 all-gather.6

commit v6 on v5

--- a/solution.py
+++ b/solution.py
@@ -37,7 +37,7 @@
 
 
 def params(collective_id):
-    return pltpu.CompilerParams(vmem_limit_bytes=62_000_000, collective_id=collective_id, has_side_effects=True)
+    return pltpu.CompilerParams(vmem_limit_bytes=67_000_000, collective_id=collective_id, has_side_effects=True)
 
 
 def cost(micros):
@@ -307,81 +307,93 @@
     )(xt, nw, w, idx, wd)
 
 
-def up_kernel(split, h_ref, idx_ref, rt_hbm, wd_part, *refs):
-    w_refs, refs = refs[:1 + split], refs[1 + split:]
-    a_all, g_ref, wd_all, wv, slots, logits, a_buf, w_sem, rt_sem, local_sem = refs[:10]
-    sems = refs[10:]
-    step = pl.program_id(0)
-    f = lax.axis_index("fsdp")
-    mine = lambda owner: pl.ds(pl.multiple_of(owner * FP, 8), FP)
-    ring = x_ring(lambda k: a_buf.at[k], lambda owner, k: a_all.at[k, :, mine(owner)], *sems[:2])
-    second = second_rings(wd_all, False, sems[2:])
-
-    def own_a(k):
-        return pltpu.make_async_copy(a_buf.at[k], a_all.at[k, :, mine(f)], local_sem.at[k])
-
-    def loads(g):
-        out = [pltpu.make_async_copy(rt_hbm, wv.at[g, pl.ds(GROWS, E)], rt_sem.at[g])]
-        for i in range(GE):
-            at = 0
-            for n, w in enumerate(w_refs):
-                size = w.shape[1]
-                out.append(pltpu.make_async_copy(w.at[g * GE + i], wv.at[g, pl.ds(i * RE + at, size)], w_sem.at[g, n, i]))
-                at += size
-        return out
-
-    @pl.when(step == 0)
-    def _():
-        for g in range(STEPS):
-            for c in loads(g):
-                c.start()
-        greet(x_neighbours() + yz_neighbours())
-        start(second)
-
+def weight_loads(g, w_refs, rt_hbm, wv, w_sem, rt_sem):
+    out = [pltpu.make_async_copy(rt_hbm, wv.at[g, pl.ds(GROWS, E)], rt_sem.at[g])]
+    for i in range(GE):
+        at = 0
+        for n, w in enumerate(w_refs):
+            size = w.shape[1]
+            out.append(pltpu.make_async_copy(w.at[g * GE + i], wv.at[g, pl.ds(i * RE + at, size)], w_sem.at[g, n, i]))
+            at += size
+    return out
+
+
+def up_block(h_ref, idx, wv, slots, logits, split, hook):
     slots[...] = jnp.zeros_like(slots)
-    idx = jnp.concatenate([idx_ref[0], idx_ref[1]], axis=1)
 
     def group(g, carry):
-        tick = step * STEPS + g
-
-        @pl.when(step == 0)
-        def _():
-            for c in loads(g):
-                c.wait()
-
-        @pl.when(jnp.logical_and(step >= 1, g == 3))
-        def _():
-            for tb in range(2):
-                ring.relay(2 * step - 2 + tb, tb == 1)
-
-        for k in range(4):
-            @pl.when(tick == 4 + 3 * k)
-            def _(k=k):
-                relay(second, k)
-
+        hook(g)
         res = jnp.dot(wv[g], h_ref[0], preferred_element_type=F32)
         logits[...] = res[GROWS:]
         for i in range(GE):
             at, parts = i * RE, []
-            for n in (FA, FP - FA):
+            for n in (FA, FP - FA) if split else (FP,):
                 parts.append(jax.nn.silu(res[at:at + n]) * res[at + n:at + 2 * n])
                 at += 2 * n
-            act = jnp.concatenate(parts, axis=0)
+            act = jnp.concatenate(parts, axis=0) if split else parts[0]
             for j in range(K):
                 slots[j] = jnp.where(idx[j:j + 1] == g * GE + i, act, slots[j])
         return carry
 
     lax.fori_loop(0, STEPS, group, 0)
-    for tb in range(2):
-        a_buf[2 * step + tb] = slots[:, :, tb * TB:(tb + 1) * TB].astype(BF)
     eids = lax.broadcasted_iota(jnp.int32, (E, TB2), 0)
     chosen = idx[0:1] == eids
     for j in range(1, K):
         chosen = jnp.logical_or(chosen, idx[j:j + 1] == eids)
     lg = jnp.where(chosen, logits[...], -jnp.inf)
     ex = jnp.where(chosen, jnp.exp(lg - jnp.max(lg, axis=0, keepdims=True)), 0.0)
-    gates = ex / jnp.sum(ex, axis=0, keepdims=True)
+    return ex / jnp.sum(ex, axis=0, keepdims=True)
+
+
+def both(ref):
+    return jnp.concatenate([ref[0], ref[1]], axis=1)
+
+
+def when_all(*conditions):
+    out = conditions[0]
+    for c in conditions[1:]:
+        out = jnp.logical_and(out, c)
+    return pl.when(out)
+
+
+def up_kernel(h_ref, idx_ref, rt_hbm, wd_part, w_a, w_b, a_all, g_ref, wd_all, wv, slots, logits, a_buf, w_sem, rt_sem, local_sem, *sems):
+    step = pl.program_id(0)
+    f = lax.axis_index("fsdp")
+    mine = lambda owner: pl.ds(pl.multiple_of(owner * FP, 8), FP)
+    ring = x_ring(lambda k: a_buf.at[k], lambda owner, k: a_all.at[k, :, mine(owner)], *sems[:2])
+    second = second_rings(wd_all, False, sems[2:])
+    loads = lambda g: weight_loads(g, (w_a, w_b), rt_hbm, wv, w_sem, rt_sem)
+
+    def own_a(k):
+        return pltpu.make_async_copy(a_buf.at[k], a_all.at[k, :, mine(f)], local_sem.at[k])
+
+    @pl.when(step == 0)
+    def _():
+        for g in range(STEPS):
+            for c in loads(g):
+                c.start()
+        greet(x_neighbours() + yz_neighbours())
+        start(second)
+
+    def hook(g):
+        @pl.when(step == 0)
+        def _():
+            for c in loads(g):
+                c.wait()
+
+        @when_all(step >= 1, g == 3)
+        def _():
+            for tb in range(2):
+                ring.relay(2 * step - 2 + tb, tb == 1)
+
+        for k in range(4):
+            @pl.when(step * STEPS + g == 4 + 3 * k)
+            def _(k=k):
+                relay(second, k)
+
+    gates = up_block(h_ref, both(idx_ref), wv, slots, logits, True, hook)
     for tb in range(2):
+        a_buf[2 * step + tb] = slots[:, :, tb * TB:(tb + 1) * TB].astype(BF)
         g_ref[tb] = gates[:, tb * TB:(tb + 1) * TB]
     for tb in range(2):
         ring.start(2 * step + tb)
@@ -408,30 +420,32 @@
     return pl.BlockSpec(dims, lambda i: (0,) * len(dims))
 
 
-def up_proj(h, idx, rt, wd_part, ws):
-    split = len(ws) - 1
+UP_SCRATCH = [
+    pltpu.VMEM((STEPS, GROWS + E, D), BF),
+    pltpu.VMEM((K, FP, TB2), F32),
+    pltpu.VMEM((E, TB2), F32),
+    pltpu.VMEM((NB, K, FP, TB), BF),
+    DMA((STEPS, 2, GE)), DMA((STEPS,)), DMA((NB,)),
+]
+
+
+def up_proj(h, idx, rt, wd_part, w_a, w_b):
     return pl.pallas_call(
-        lambda *refs: up_kernel(split, *refs),
+        up_kernel,
         grid=(STEPS,),
         out_shape=(shape((NB, K, NB * FP, TB)), shape((NB, E, TB), F32), shape((E, DS, KP))),
-        in_specs=[pl.BlockSpec((1, D, TB2), lambda i: (i, 0, 0)), pair(K, TB), ANY, ANY] + [ANY] * len(ws),
+        in_specs=[pl.BlockSpec((1, D, TB2), lambda i: (i, 0, 0)), pair(K, TB)] + [ANY] * 4,
         out_specs=(ANY, pair(E, TB), ANY),
-        scratch_shapes=[
-            pltpu.VMEM((STEPS, GROWS + E, D), BF),
-            pltpu.VMEM((K, FP, TB2), F32),
-            pltpu.VMEM((E, TB2), F32),
-            pltpu.VMEM((NB, K, FP, TB), BF),
-            DMA((STEPS, 2, GE)), DMA((STEPS,)), DMA((NB,)),
-        ] + X_SEMS + SECOND_SEMS,
+        scratch_shapes=UP_SCRATCH + X_SEMS + SECOND_SEMS,
         input_output_aliases={3: 2},
-        compiler_params=params(2 + split),
+        compiler_params=params(2),
         cost_estimate=cost(70),
         name="up_proj",
-    )(h, idx, rt, wd_part, *ws)
+    )(h, idx, rt, wd_part, w_a, w_b)
 
 
 def down_block(a_ref, idx_ref, g_ref, wd_ref, acc, hook):
-    idx = jnp.concatenate([idx_ref[0], idx_ref[1]], axis=1).astype(F32).astype(BF)
+    idx = both(idx_ref).astype(F32).astype(BF)
     acc[...] = jnp.zeros_like(acc)
 
     def group(g, carry):
@@ -531,62 +545,183 @@
     )(a, idx, gates, x_all, wd, nw, wd_next)
 
 
-def down_last_kernel(a_ref, idx_ref, g_ref, x_ref, wd_ref, o_all, acc, o_buf, send_sem, recv_sem, local_sem):
+CODES = (17, 74, 191, 228)
+
+
+def turn(n):
+    ring = lax.axis_index("fsdp") // 2
+    place = (1 + 3 * (ring % 2)) * (1 + 15 * (ring // 2))
+    out = 0
+    for i in range(STEPS):
+        out = out + jnp.where(n == i, (CODES[i] // place) % 4, 0)
+    return out
+
+
+def last_kernel(
+    h_ref, idx_ref, rt_hbm, wd_part, w, x_ref, o_all, a_all, wd_all, wv, slots, logits, a_buf, w_sem, rt_sem, local_sem,
+    g_v, wd_v, a_v, acc, o_buf, wd_sem, a_sem, out_send, out_recv, *sems,
+):
     step = pl.program_id(0)
     f = lax.axis_index("fsdp")
     core = f % 2
+    mine = lambda owner: pl.ds(pl.multiple_of(owner * FP, 8), FP)
+    ring = x_ring(lambda k: a_buf.at[k], lambda owner, k: a_all.at[k, :, mine(owner)], *sems[:2])
+    second = second_rings(wd_all, False, sems[2:])
+    loads = lambda g: weight_loads(g, (w,), rt_hbm, wv, w_sem, rt_sem)
+
+    def own_a(k):
+        return pltpu.make_async_copy(a_buf.at[k], a_all.at[k, :, mine(f)], local_sem.at[k])
+
+    def wd_load(g):
+        return pltpu.make_async_copy(wd_all.at[pl.ds(g * GE, GE)], wd_v.at[pl.ds(g * GE, GE)], wd_sem.at[g])
+
+    def a_load(n):
+        return pltpu.make_async_copy(a_all.at[pl.ds(2 * turn(n), 2)], a_v.at[n % 2], a_sem.at[n % 2])
+
+    def complete(chunks):
+        for k in chunks:
+            ring.from_partner(k)
+            own_a(k).wait()
 
     @pl.when(step == 0)
     def _():
-        greet([{"fsdp": fsdp_at(s, o)} for s, o in PEERS])
-
-    down_block(a_ref, idx_ref, g_ref, wd_ref, acc, lambda g: None)
-    for tb in range(2):
-        o_buf[step, tb] = new_x(x_ref[0, tb], acc, tb)
-
-    def send(s, o):
-        return remote(o_buf.at[(s + 3) % 4, 1 - core if o else core], o_all.at[f], send_sem.at[s, o], recv_sem.at[s, o], {"fsdp": fsdp_at(s, o)})
-
-    for s in range(1, 4):
-        @pl.when(step == s - 1)
-        def _(s=s):
-            send(s, 0).start()
-            send(s, 1).start()
-
-    @pl.when(step == 3)
-    def _():
-        send(0, 1).start()
-        mine = pltpu.make_async_copy(o_buf.at[3, core], o_all.at[f], local_sem)
-        mine.start()
+        for g in range(STEPS):
+            for c in loads(g):
+                c.start()
+        greet([{"fsdp": fsdp_at(s, o)} for s, o in PEERS] + yz_neighbours())
+        start(second)
+
+    def up_hook(g):
+        @pl.when(step == 0)
+        def _():
+            for c in loads(g):
+                c.wait()
+
+        @when_all(step >= 1, g == 3)
+        def _():
+            for tb in range(2):
+                ring.relay(2 * step - 2 + tb, tb == 1)
+
+        for k in range(4):
+            @pl.when(step * STEPS + g == 4 + 3 * k)
+            def _(k=k):
+                relay(second, k)
+
+        @when_all(step == 3, g == 1)
+        def _():
+            for k in range(4):
+                ring.last(k)
+
+        @when_all(step == 3, g == 2)
+        def _():
+            complete(range(4))
+            a_load(0).start()
+
+    @pl.when(step < STEPS)
+    def _():
+        gates = up_block(h_ref, both(idx_ref.at[pl.ds(2 * step, 2)]), wv, slots, logits, False, up_hook)
+        for tb in range(2):
+            a_buf[2 * step + tb] = slots[:, :, tb * TB:(tb + 1) * TB].astype(BF)
+            g_v[2 * step + tb] = gates[:, tb * TB:(tb + 1) * TB]
+        for tb in range(2):
+            ring.start(2 * step + tb)
+            own_a(2 * step + tb).start()
+
+    n = step - STEPS
+
+    @pl.when(n == 0)
+    def _():
+        finish(second)
+        for g in range(STEPS):
+            wd_load(g).start()
+
+    def down_hook(g):
+        @pl.when(n == 0)
+        def _():
+            wd_load(g).wait()
+
+        @when_all(n == 0, g == 1)
+        def _():
+            for k in (4, 5):
+                ring.last(k)
+
+        @when_all(n == 0, g == 2)
+        def _():
+            complete((4, 5))
+            a_load(1).start()
+
+        @when_all(n == 1, g == 0)
+        def _():
+            for k in (6, 7):
+                ring.relay(k, k % 2 == 1)
+
+        @when_all(n == 1, g == 3)
+        def _():
+            for k in (6, 7):
+                ring.last(k)
+
+        @when_all(n == 2, g == 0)
+        def _():
+            a_load(3).start()
+
+    def send(i, other):
+        return remote(
+            o_buf.at[i, 1 - core if other else core], o_all.at[f], out_send.at[i, other], out_recv.at[f],
+            {"fsdp": 2 * turn(i) + (1 - core if other else core)})
+
+    @pl.when(n >= 0)
+    def _():
+        now = 2 * turn(n)
+        a_load(n).wait()
+        down_block(a_v.at[n % 2], idx_ref.at[pl.ds(now, 2)], g_v.at[pl.ds(now, 2)], wd_v, acc, down_hook)
+        for tb in range(2):
+            o_buf[n, tb] = new_x(x_ref[0, now + tb], acc, tb)
+        send(n, 1).start()
+
+        @pl.when(n < 3)
+        def _():
+            send(n, 0).start()
+
+        @pl.when(n == 1)
+        def _():
+            complete((6, 7))
+            a_load(2).start()
+
+    @pl.when(n == 3)
+    def _():
+        own = pltpu.make_async_copy(o_buf.at[3, core], o_all.at[f], a_sem.at[0])
+        own.start()
+        ring.drain()
         for s, o in PEERS:
-            source = fsdp_at((4 - s) % 4, o)
-            remote(o_buf.at[0, 0], o_all.at[source], send_sem.at[s, o], recv_sem.at[s, o], {"fsdp": source}).wait_recv()
-        for s, o in PEERS:
-            send(s, o).wait_send()
-        mine.wait()
-
-
-def down_last(a, idx, gates, x_all, wd):
-    block = lambda i: lax.rem(lax.axis_index("fsdp") // 2 + 1 + i, 4)
-
-    def turned(*tail):
-        return pl.BlockSpec((2,) + tail, lambda i: (block(i),) + (0,) * len(tail))
-
+            source = fsdp_at(s, o)
+            remote(o_buf.at[0, 0], o_all.at[source], out_send.at[0, 0], out_recv.at[source], {"fsdp": source}).wait_recv()
+        for i in range(STEPS):
+            send(i, 1).wait_send()
+            if i < 3:
+                send(i, 0).wait_send()
+        own.wait()
+
+
+def last_layer(h, idx, rt, wd_part, w, x_all):
     return pl.pallas_call(
-        down_last_kernel,
-        grid=(STEPS,),
-        out_shape=shape((NB, DS, TB)),
+        last_kernel,
+        grid=(2 * STEPS,),
+        out_shape=(shape((NB, DS, TB)), shape((NB, K, NB * FP, TB)), shape((E, DS, KP))),
         in_specs=[
-            turned(K, NB * FP, TB), turned(K, TB), turned(E, TB),
-            pl.BlockSpec((1, 2, DS, TB), lambda i: (lax.axis_index("fsdp"), block(i), 0, 0)),
-            whole(E, DS, KP),
+            pl.BlockSpec((1, D, TB2), lambda i: (jnp.minimum(i, STEPS - 1), 0, 0)), whole(NB, K, TB), ANY, ANY, ANY,
+            pl.BlockSpec((1, NB, DS, TB), lambda i: (lax.axis_index("fsdp"), 0, 0, 0), pipeline_mode=pl.Buffered(1)),
         ],
-        out_specs=ANY,
-        scratch_shapes=[pltpu.VMEM((DS, TB2), F32), pltpu.VMEM((STEPS, 2, DS, TB), BF), DMA((4, 2)), DMA((4, 2)), DMA],
-        compiler_params=params(5),
-        cost_estimate=cost(45),
-        name="down_last",
-    )(a, idx, gates, x_all, wd)
+        out_specs=[ANY] * 3,
+        scratch_shapes=UP_SCRATCH + [
+            pltpu.VMEM((NB, E, TB), F32), pltpu.VMEM((E, DS, KP), BF), pltpu.VMEM((2, 2, K, NB * FP, TB), BF),
+            pltpu.VMEM((DS, TB2), F32), pltpu.VMEM((STEPS, 2, DS, TB), BF),
+            DMA((STEPS,)), DMA((2,)), DMA((4, 2)), DMA((NB,)),
+        ] + X_SEMS + SECOND_SEMS,
+        input_output_aliases={3: 2},
+        compiler_params=params(3),
+        cost_estimate=cost(110),
+        name="last_layer",
+    )(h, idx, rt, wd_part, w, x_all)
 
 
 def solution(mesh):
@@ -606,17 +741,15 @@
         part_a, part_b = [jnp.concatenate(p, axis=0) for p in pack(w_gate[0, 0], w_up[0, 0])]
         w_a = lax.all_gather(part_a, "ep", axis=0, tiled=False)
         gate1, up1, _ = lax.optimization_barrier((w_gate, w_up, part_a))
-        one, two = pack(gate1[1, 0], up1[1, 0])
-        rows = jnp.concatenate(one + two, axis=0)
+        rows = jnp.concatenate([gate1[1, 0].T, pad, up1[1, 0].T, pad], axis=0)
         wd = jnp.pad(w_down[:, 0], ((0, 0), (0, FP - F), (0, 0))).reshape(2, FP, NB, DS).swapaxes(1, 2)
         xt = x.T.reshape(NB, DS, TB)
         xt, idx, wd, part_b, rows = lax.optimization_barrier((xt, jnp.swapaxes(expert_idx, 1, 2), wd, part_b, rows))
         x_all, h, w_b, idx, wd_part, wd_next = first_exchange(xt, nws[0], part_b, idx, wd)
         rows, _ = lax.optimization_barrier((rows, idx))
         w_next = lax.all_gather(rows, "ep", axis=0, tiled=False)
-        a, gates, wd_all = up_proj(h, idx[:, 0], routers[0], wd_part, (w_a, w_b))
+        a, gates, wd_all = up_proj(h, idx[:, 0], routers[0], wd_part, w_a, w_b)
         x_all, h, wd_part = down_mid(a, idx[:, 0], gates, x_all, wd_all, nws[1], wd_next)
-        a, gates, wd_all = up_proj(h, idx[:, 1], routers[1], wd_part, (w_next,))
-        return down_last(a, idx[:, 1], gates, x_all, wd_all).reshape(D, TB).T
+        return last_layer(h, idx[:, 1], routers[1], wd_part, w_next, x_all)[0].reshape(D, TB).T
 
     return jax.shard_map(local_program, mesh=mesh, in_specs=in_specs, out_specs=tok_spec, check_vma=False)

time: 502 us -> 513 us (1.022)
  Pallas kernels: 450 us -> 465 us
    pallas_call x3 -> x2, Pallas kernels: 223 us -> 233 us  [the longest x1 136 us: last_layer(): pl.pallas_call(last_kernel, grid=(2 * STEPS,), out_shape=(shape((NB, DS,...]
    concatenate x1 -> x0, local copies, waits for them, and re-layouts: 8.59 us -> none  [local_program(): rows = jnp.concatenate(one + two, axis=0)]
where the time goes in v6:
time: 513 us
  Pallas kernels  465 us (91%)
  local copies, waits for them, and re-layouts  30.4 us (6%)
  between operations  13.6 us (3%)
    pallas_call x1, Pallas kernels, last_layer(): pl.pallas_call(last_kernel, grid=(2 * STEPS,), out_shape=(shape((NB, DS,...  136 us
    pallas_call x1, Pallas kernels, first_exchange(): pl.pallas_call(first_kernel, out_shape=(shape((NB, NB, DS, TB)), shape((S...  135 us
    pallas_call x1, Pallas kernels, down_mid(): pl.pallas_call(down_mid_kernel, grid=(STEPS,), out_shape=(shape((NB, NB,...  97.3 us
    pallas_call x1, Pallas kernels, up_proj(): pl.pallas_call(up_kernel, grid=(STEPS,), out_shape=(shape((NB, K, NB * FP...  96.8 us
  transfers between devices with their start and end apart: 2, of which 0 were waited for; matrix products, arithmetic and copies ran while one was open for 5% of the time, Pallas kernels for 64%

profile of v6, /device:TPU:1, one launch (start us, length us, event | category | flops | bytes accessed | tf_op | source)
XLA Modules:
  0.0 512.5 jit_solution(1517175685542059410)
XLA Ops:
  6.5 0.0 copy-start.1
  6.5 0.0 all-gather.5.cloned.1.call-start
  6.5 2.2 copy.38
  8.8 0.0 copy-done.1
  8.8 0.8 copy.37
  9.6 0.0 copy-start.4
  9.6 0.8 copy-done.4
  10.5 0.0 copy-start
  10.5 1.0 pad_maximum_fusion.1
  11.5 0.0 all-gather.5.cloned.1.call-update
  11.5 0.0 all-gather.7.cloned.1.call-start
  11.6 0.7 slice.41
  12.3 1.7 slice.42
  14.1 0.0 copy-done
  14.1 1.9 copy.22
  16.0 0.0 copy-start.5
  16.0 1.9 copy.23
  17.8 0.0 copy-done.5
  17.8 1.5 pad.4
  19.4 1.2 reshape.16
  20.6 1.9 copy.36
  22.5 0.0 copy-start.6
  22.5 0.0 copy-start.7
  22.5 0.0 copy-start.2
  22.5 0.0 copy-start.3
  22.6 4.2 copy.17
  26.8 0.0 copy-done.6
  26.8 0.0 copy-done.7
  26.8 0.9 pad_maximum_fusion.2.w_ref
  27.8 0.0 copy-done.2
  27.8 0.0 copy-done.3
  27.8 0.1 slice_bitcast_fusion
  27.9 0.0 copy-start.8
  27.9 1.3 pad_maximum_fusion
  29.1 0.0 copy-done.8
  29.1 0.1 slice_reduce_fusion
  29.2 2.0 broadcast_in_dim.19.nw_ref
  31.2 135.0 %first_exchange.1 = (bf16[8,8,512,256]{3,2,1,0:T(8,128)(2,1)}, bf16[4,4096,512]{2,1,0:T(8,128)(2,1)}, bf16[16,80,4096]{2,1,0:T(8,128)(2,1)}, s32[8,2,4,256]{3,2,...) custom-call(bf16[8,512,256]{2,1,0:T(8,128)(2,1)} %bitcast.52, ...), custom_call_target="tpu_custom_call" | custom-call | flops 120000004096 | bytes 10000000 | tf_op jit(solution)/shard_map/first_exchange/pallas_call | solution.py:293
  166.2 0.0 all-gather.7.cloned.1.call-update
  166.3 1.4 slice_bitcast_fusion.4
  167.7 1.7 slice_bitcast_fusion.2
  169.3 0.0 all-gather.5.cloned.1.call-done
  169.3 96.8 %up_proj.1 = (bf16[8,4,704,256]{3,2,1,0:T(8,128)(2,1)}, f32[8,16,256]{2,1,0:T(8,128)}, bf16[16,512,768]{2,1,0:T(8,128)(2,1)}) custom-call(bf16[4,4096,512]{2,1,0:T(8,128)(2,1)} %get-tuple-element.32.h_ref, s32[8,4,256]{2,1,0:T(4,128)} %get-tuple-element.52.idx_ref, bf16[16,4096]{1,0:T(8,128)(2,1)} %get-tuple-element.50.rt_hbm, ...), custom_call_target="tpu_custom_call", output_to_operand_aliasing={{2}: (3, {})} | custom-call | flops 70000001024 | bytes 10000000 | tf_op jit(solution)/shard_map/up_proj/pallas_call | solution.py:433
  266.2 1.9 broadcast_in_dim.21.nw_ref
  268.1 97.3 %down_mid.1 = (bf16[8,8,512,256]{3,2,1,0:T(8,128)(2,1)}, bf16[4,4096,512]{2,1,0:T(8,128)(2,1)}, bf16[16,512,768]{2,1,0:T(8,128)(2,1)}) custom-call(bf16[8,4,704,256]{3,2,1,0:T(8,128)(2,1)} %get-tuple-element.36.a_ref, s32[8,4,256]{2,1,0:T(4,128)} %get-tuple-element.52.idx_ref, f32[8,16,256]{2,1,0:T(8,128)} %get-tuple-element.37.g_ref, ...), custom_call_target="tpu_custom_call" | custom-call | flops 80000000000 | bytes 10000000 | tf_op jit(solution)/shard_map/down_mid/pallas_call | solution.py:528
  365.4 0.0 all-gather.7.cloned.1.call-done
  365.4 136.2 %last_layer.1 = (bf16[8,512,256]{2,1,0:T(8,128)(2,1)}, bf16[8,4,704,256]{3,2,1,0:T(8,128)(2,1)}, bf16[16,512,768]{2,1,0:T(8,128)(2,1)}) custom-call(bf16[4,4096,512]{2,1,0:T(8,128)(2,1)} %get-tuple-element.41.h_ref, s32[8,4,256]{2,1,0:T(4,128)} %get-tuple-element.51.idx_ref, ...), custom_call_target="tpu_custom_call", output_to_operand_aliasing={{2}: (3, {})} | custom-call | flops 109999996928 | bytes 10000000 | tf_op jit(solution)/shard_map/last_layer/pallas_call | solution.py:706
  501.6 4.1 copy.26
  (5 shorter events, 0.1 us)
Async XLA Ops:
  6.5 2.3 copy-start.1
  6.5 162.8 %all-gather.5.cloned.1.call-start = ((), (), s32[]{:S(2)}) async-start(), calls=%async_computation | async-start | bytes 13369344 | tf_op jit(solution)/shard_map/all_gather | solution.py:742
  9.6 0.9 copy-start.4
  10.5 3.6 copy-start
  11.5 353.8 %all-gather.7.cloned.1.call-start = ((), (), s32[]{:S(2)}) async-start(), calls=%async_computation.1 | async-start | bytes 24510464 | tf_op jit(solution)/shard_map/all_gather | solution.py:750
  16.0 1.9 copy-start.5
  22.5 4.3 copy-start.6
  22.5 4.3 copy-start.7
  22.5 5.2 %copy-start.2 = (bf16[2,1,4096,86]{2,3,1,0:T(8,128)(2,1)S(1)}, bf16[2,1,4096,86]{2,3,1,0:T(8,128)(2,1)}, u32[]{:S(2)}) copy-start(bf16[2,1,4096,86]{2,3,1,0:T(8,128)(2,1)} %copy.22) | copy-start | bytes 4227076
  22.5 5.2 %copy-start.3 = (bf16[2,1,4096,86]{2,3,1,0:T(8,128)(2,1)S(1)}, bf16[2,1,4096,86]{2,3,1,0:T(8,128)(2,1)}, u32[]{:S(2)}) copy-start(bf16[2,1,4096,86]{2,3,1,0:T(8,128)(2,1)} %copy.23) | copy-start | bytes 4227076
  27.9 1.3 copy-start.8
Sparse Core Ops, SparseCore 0:
  11.7 135.7 all-gather.4
  166.4 190.7 all-gather.6

commit v7 on v6

--- a/solution.py
+++ b/solution.py
@@ -14,8 +14,6 @@
 F = 86
 FP = 88
 FA = 48
-RA = 96
-RB = 80
 RE = 176
 KP = 768
 E = 16
@@ -29,6 +27,8 @@
 DMA = pltpu.SemaphoreType.DMA
 ANY = pl.BlockSpec(memory_space=pl.ANY)
 IN_VMEM = pl.BlockSpec(memory_space=pltpu.VMEM)
+LATE = (6, 7)
+MIDDLE = (4, 5)
 PEERS = [(s, o) for s in range(4) for o in range(2) if s + o]
 
 
@@ -356,6 +356,23 @@
     return pl.when(out)
 
 
+def up_hook(step, g, loads, ring, second):
+    @pl.when(step == 0)
+    def _():
+        for c in loads(g):
+            c.wait()
+
+    @when_all(step >= 1, g == 3)
+    def _():
+        for tb in range(2):
+            ring.relay(2 * step - 2 + tb, tb == 1)
+
+    for k in range(4):
+        @pl.when(step * STEPS + g == 4 + 3 * k)
+        def _(k=k):
+            relay(second, k)
+
+
 def up_kernel(h_ref, idx_ref, rt_hbm, wd_part, w_a, w_b, a_all, g_ref, wd_all, wv, slots, logits, a_buf, w_sem, rt_sem, local_sem, *sems):
     step = pl.program_id(0)
     f = lax.axis_index("fsdp")
@@ -375,22 +392,7 @@
         greet(x_neighbours() + yz_neighbours())
         start(second)
 
-    def hook(g):
-        @pl.when(step == 0)
-        def _():
-            for c in loads(g):
-                c.wait()
-
-        @when_all(step >= 1, g == 3)
-        def _():
-            for tb in range(2):
-                ring.relay(2 * step - 2 + tb, tb == 1)
-
-        for k in range(4):
-            @pl.when(step * STEPS + g == 4 + 3 * k)
-            def _(k=k):
-                relay(second, k)
-
+    hook = lambda g: up_hook(step, g, loads, ring, second)
     gates = up_block(h_ref, both(idx_ref), wv, slots, logits, True, hook)
     for tb in range(2):
         a_buf[2 * step + tb] = slots[:, :, tb * TB:(tb + 1) * TB].astype(BF)
@@ -401,7 +403,7 @@
 
     @pl.when(step == 3)
     def _():
-        for k in (6, 7):
+        for k in LATE:
             ring.relay(k, k % 2 == 1)
         for k in range(NB):
             ring.last(k)
@@ -416,6 +418,10 @@
     return pl.BlockSpec((2,) + tail, lambda i: (i,) + (0,) * len(tail))
 
 
+def routing(layer):
+    return pl.BlockSpec((NB if layer else 2, None, K, TB), lambda i: (0 if layer else i, layer, 0, 0))
+
+
 def whole(*dims):
     return pl.BlockSpec(dims, lambda i: (0,) * len(dims))
 
@@ -434,7 +440,7 @@
         up_kernel,
         grid=(STEPS,),
         out_shape=(shape((NB, K, NB * FP, TB)), shape((NB, E, TB), F32), shape((E, DS, KP))),
-        in_specs=[pl.BlockSpec((1, D, TB2), lambda i: (i, 0, 0)), pair(K, TB)] + [ANY] * 4,
+        in_specs=[pl.BlockSpec((1, D, TB2), lambda i: (i, 0, 0)), routing(0)] + [ANY] * 4,
         out_specs=(ANY, pair(E, TB), ANY),
         scratch_shapes=UP_SCRATCH + X_SEMS + SECOND_SEMS,
         input_output_aliases={3: 2},
@@ -473,7 +479,8 @@
 
 
 def down_mid_kernel(
-    a_ref, idx_ref, g_ref, x_ref, wd_ref, nw_ref, wd_next, x_all, h_all, wd_all, acc, o_buf, stage, h_stage, local_sem, norm_sem, *sems,
+    a_ref, idx_ref, g_ref, x_ref, wd_hbm, nw_ref, wd_next, x_all, h_all, wd_all,
+    acc, o_buf, stage, h_stage, wd_v, wd_sem, local_sem, norm_sem, *sems,
 ):
     step = pl.program_id(0)
     f = lax.axis_index("fsdp")
@@ -484,13 +491,22 @@
     def own_x(k):
         return pltpu.make_async_copy(o_buf.at[k], x_all.at[f, k], local_sem.at[k])
 
+    def wd_load(g):
+        return pltpu.make_async_copy(wd_hbm.at[pl.ds(g * GE, GE)], wd_v.at[pl.ds(g * GE, GE)], wd_sem.at[g])
+
     @pl.when(step == 0)
     def _():
+        for g in range(STEPS):
+            wd_load(g).start()
         greet(x_neighbours() + yz_neighbours())
         own_wd.start()
         start(d_first)
 
     def hook(g):
+        @pl.when(step == 0)
+        def _():
+            wd_load(g).wait()
+
         @pl.when(jnp.logical_and(step >= 2, g == 2))
         def _():
             for tb in range(2):
@@ -500,7 +516,7 @@
                 def _(k=k):
                     relay(d_first, k)
 
-    down_block(a_ref, idx_ref, g_ref, wd_ref, acc, hook)
+    down_block(a_ref, idx_ref, g_ref, wd_v, acc, hook)
     for tb in range(2):
         o_buf[2 * step + tb] = new_x(x_ref[tb, 0], acc, tb)
     for tb in range(2):
@@ -530,14 +546,14 @@
         grid=(STEPS,),
         out_shape=(shape((NB, NB, DS, TB)), shape((STEPS, D, TB2)), shape((E, DS, KP))),
         in_specs=[
-            pair(K, NB * FP, TB), pair(K, TB), pair(E, TB),
+            pair(K, NB * FP, TB), routing(0), pair(E, TB),
             pl.BlockSpec((2, 1, DS, TB), lambda i: (i, lax.axis_index("fsdp"), 0, 0)),
-            whole(E, DS, KP), whole(NB, DS, 128), whole(DS, KP),
+            ANY, whole(NB, DS, 128), whole(DS, KP),
         ],
         out_specs=[ANY] * 3,
         scratch_shapes=[
             pltpu.VMEM((DS, TB2), F32), pltpu.VMEM((NB, DS, TB), BF), pltpu.VMEM((NB, 2, DS, TB), BF), pltpu.VMEM((D, TB2), BF),
-            DMA((NB + 1,)), DMA((2,)),
+            pltpu.VMEM((E, DS, KP), BF), DMA((STEPS,)), DMA((NB + 1,)), DMA((2,)),
         ] + X_SEMS + FIRST_SEMS,
         compiler_params=params(4),
         cost_estimate=cost(80),
@@ -559,7 +575,7 @@
 
 def last_kernel(
     h_ref, idx_ref, rt_hbm, wd_part, w, x_ref, o_all, a_all, wd_all, wv, slots, logits, a_buf, w_sem, rt_sem, local_sem,
-    g_v, wd_v, a_v, acc, o_buf, wd_sem, a_sem, out_send, out_recv, *sems,
+    g_v, wd_v, a_v, acc, o_buf, passing, wd_sem, a_sem, out_send, out_recv, pass_send, pass_recv, *sems,
 ):
     step = pl.program_id(0)
     f = lax.axis_index("fsdp")
@@ -591,21 +607,8 @@
         greet([{"fsdp": fsdp_at(s, o)} for s, o in PEERS] + yz_neighbours())
         start(second)
 
-    def up_hook(g):
-        @pl.when(step == 0)
-        def _():
-            for c in loads(g):
-                c.wait()
-
-        @when_all(step >= 1, g == 3)
-        def _():
-            for tb in range(2):
-                ring.relay(2 * step - 2 + tb, tb == 1)
-
-        for k in range(4):
-            @pl.when(step * STEPS + g == 4 + 3 * k)
-            def _(k=k):
-                relay(second, k)
+    def hook(g):
+        up_hook(step, g, loads, ring, second)
 
         @when_all(step == 3, g == 1)
         def _():
@@ -619,7 +622,7 @@
 
     @pl.when(step < STEPS)
     def _():
-        gates = up_block(h_ref, both(idx_ref.at[pl.ds(2 * step, 2)]), wv, slots, logits, False, up_hook)
+        gates = up_block(h_ref, both(idx_ref.at[pl.ds(2 * step, 2)]), wv, slots, logits, False, hook)
         for tb in range(2):
             a_buf[2 * step + tb] = slots[:, :, tb * TB:(tb + 1) * TB].astype(BF)
             g_v[2 * step + tb] = gates[:, tb * TB:(tb + 1) * TB]
@@ -642,32 +645,46 @@
 
         @when_all(n == 0, g == 1)
         def _():
-            for k in (4, 5):
+            for k in MIDDLE:
                 ring.last(k)
 
         @when_all(n == 0, g == 2)
         def _():
-            complete((4, 5))
+            complete(MIDDLE)
             a_load(1).start()
 
         @when_all(n == 1, g == 0)
         def _():
-            for k in (6, 7):
+            for k in LATE:
                 ring.relay(k, k % 2 == 1)
 
         @when_all(n == 1, g == 3)
         def _():
-            for k in (6, 7):
+            for k in LATE:
                 ring.last(k)
 
         @when_all(n == 2, g == 0)
         def _():
             a_load(3).start()
 
+        @when_all(n == 3, g == 3)
+        def _():
+            for other in range(2):
+                send_by(0, other).wait_recv()
+                passed(other).start()
+
     def send(i, other):
+        part = 1 - core if other else core
+        return remote(o_buf.at[i, part], o_all.at[f], out_send.at[i, other], out_recv.at[f], {"fsdp": 2 * turn(i) + part})
+
+    def send_by(i, other):
+        near = {"fsdp": fsdp_at(3 if other else 1)}
+        return remote(o_buf.at[i, 1 - core if other else core], passing.at[other], out_send.at[i, other], pass_recv.at[other], near)
+
+    def passed(other):
+        source = fsdp_at(1 if other else 3)
         return remote(
-            o_buf.at[i, 1 - core if other else core], o_all.at[f], out_send.at[i, other], out_recv.at[f],
-            {"fsdp": 2 * turn(i) + (1 - core if other else core)})
+            passing.at[other], o_all.at[source], pass_send.at[other], out_recv.at[source], {"fsdp": fsdp_at(3 if other else 1, other)})
 
     @pl.when(n >= 0)
     def _():
@@ -676,15 +693,24 @@
         down_block(a_v.at[n % 2], idx_ref.at[pl.ds(now, 2)], g_v.at[pl.ds(now, 2)], wd_v, acc, down_hook)
         for tb in range(2):
             o_buf[n, tb] = new_x(x_ref[0, now + tb], acc, tb)
-        send(n, 1).start()
-
-        @pl.when(n < 3)
+        away = lax.rem(turn(n) + 4 - f // 2, 4)
+
+        @pl.when(away == 2)
+        def _():
+            for other in range(2):
+                send_by(n, other).start()
+
+        @pl.when(away != 2)
+        def _():
+            send(n, 1).start()
+
+        @pl.when(away % 2 == 1)
         def _():
             send(n, 0).start()
 
         @pl.when(n == 1)
         def _():
-            complete((6, 7))
+            complete(LATE)
             a_load(2).start()
 
     @pl.when(n == 3)
@@ -696,9 +722,11 @@
             source = fsdp_at(s, o)
             remote(o_buf.at[0, 0], o_all.at[source], out_send.at[0, 0], out_recv.at[source], {"fsdp": source}).wait_recv()
         for i in range(STEPS):
-            send(i, 1).wait_send()
+            send_by(i, 1).wait_send()
             if i < 3:
-                send(i, 0).wait_send()
+                send_by(i, 0).wait_send()
+        for other in range(2):
+            passed(other).wait_send()
         own.wait()
 
 
@@ -708,14 +736,14 @@
         grid=(2 * STEPS,),
         out_shape=(shape((NB, DS, TB)), shape((NB, K, NB * FP, TB)), shape((E, DS, KP))),
         in_specs=[
-            pl.BlockSpec((1, D, TB2), lambda i: (jnp.minimum(i, STEPS - 1), 0, 0)), whole(NB, K, TB), ANY, ANY, ANY,
+            pl.BlockSpec((1, D, TB2), lambda i: (jnp.minimum(i, STEPS - 1), 0, 0)), routing(1), ANY, ANY, ANY,
             pl.BlockSpec((1, NB, DS, TB), lambda i: (lax.axis_index("fsdp"), 0, 0, 0), pipeline_mode=pl.Buffered(1)),
         ],
         out_specs=[ANY] * 3,
         scratch_shapes=UP_SCRATCH + [
             pltpu.VMEM((NB, E, TB), F32), pltpu.VMEM((E, DS, KP), BF), pltpu.VMEM((2, 2, K, NB * FP, TB), BF),
             pltpu.VMEM((DS, TB2), F32), pltpu.VMEM((STEPS, 2, DS, TB), BF),
-            DMA((STEPS,)), DMA((2,)), DMA((4, 2)), DMA((NB,)),
+            pltpu.VMEM((2, DS, TB), BF), DMA((STEPS,)), DMA((2,)), DMA((4, 2)), DMA((NB,)), DMA((2,)), DMA((2,)),
         ] + X_SEMS + SECOND_SEMS,
         input_output_aliases={3: 2},
         compiler_params=params(3),
@@ -744,12 +772,12 @@
         rows = jnp.concatenate([gate1[1, 0].T, pad, up1[1, 0].T, pad], axis=0)
         wd = jnp.pad(w_down[:, 0], ((0, 0), (0, FP - F), (0, 0))).reshape(2, FP, NB, DS).swapaxes(1, 2)
         xt = x.T.reshape(NB, DS, TB)
-        xt, idx, wd, part_b, rows = lax.optimization_barrier((xt, jnp.swapaxes(expert_idx, 1, 2), wd, part_b, rows))
+        xt, idx, wd, part_b, rows, nws, routers = lax.optimization_barrier((xt, jnp.swapaxes(expert_idx, 1, 2), wd, part_b, rows, nws, routers))
         x_all, h, w_b, idx, wd_part, wd_next = first_exchange(xt, nws[0], part_b, idx, wd)
         rows, _ = lax.optimization_barrier((rows, idx))
         w_next = lax.all_gather(rows, "ep", axis=0, tiled=False)
-        a, gates, wd_all = up_proj(h, idx[:, 0], routers[0], wd_part, w_a, w_b)
-        x_all, h, wd_part = down_mid(a, idx[:, 0], gates, x_all, wd_all, nws[1], wd_next)
-        return last_layer(h, idx[:, 1], routers[1], wd_part, w_next, x_all)[0].reshape(D, TB).T
+        a, gates, wd_all = up_proj(h, idx, routers[0], wd_part, w_a, w_b)
+        x_all, h, wd_part = down_mid(a, idx, gates, x_all, wd_all, nws[1], wd_next)
+        return last_layer(h, idx, routers[1], wd_part, w_next, x_all)[0].reshape(D, TB).T
 
     return jax.shard_map(local_program, mesh=mesh, in_specs=in_specs, out_specs=tok_spec, check_vma=False)

time: 513 us -> 487 us (0.949)
  Pallas kernels: 465 us -> 439 us
    pallas_call x1, Pallas kernels: 136 us -> 120 us  [last_layer(): pl.pallas_call(last_kernel, grid=(2 * STEPS,), out_shape=(shape((NB, DS,...]
  transfers between devices with their start and end apart: 2 -> 2, of which waited for: 0 -> 0; matrix products, arithmetic and copies ran while one was open for 5% -> 5% of each run, Pallas kernels for 64% -> 66%
where the time goes in v7:
time: 487 us; the launch traced here: 486 us
  Pallas kernels  439 us (90%)
  local copies, waits for them, and re-layouts  30 us (6%)
  between operations  13.6 us (3%)
    pallas_call x1, Pallas kernels, first_exchange(): pl.pallas_call(first_kernel, out_shape=(shape((NB, NB, DS, TB)), shape((S...  130 us
    pallas_call x1, Pallas kernels, last_layer(): pl.pallas_call(last_kernel, grid=(2 * STEPS,), out_shape=(shape((NB, DS,...  120 us
    pallas_call x1, Pallas kernels, down_mid(): pl.pallas_call(down_mid_kernel, grid=(STEPS,), out_shape=(shape((NB, NB,...  94.5 us
    pallas_call x1, Pallas kernels, up_proj(): pl.pallas_call(up_kernel, grid=(STEPS,), out_shape=(shape((NB, K, NB * FP...  94.1 us
  transfers between devices with their start and end apart: 2, of which 0 were waited for; matrix products, arithmetic and copies ran while one was open for 5% of the time, Pallas kernels for 66%

profile of v7, /device:TPU:1, one launch (start us, length us, event | category | flops | bytes accessed | tf_op | source)
XLA Modules:
  0.0 485.7 jit_solution(10979975916027780367)
XLA Ops:
  6.5 0.0 copy-start.1
  6.5 0.0 all-gather.5.cloned.1.call-start
  6.5 2.2 copy.32
  8.8 0.0 copy-done.1
  8.8 0.8 copy.31
  9.6 0.0 copy-start.4
  9.6 0.8 copy-done.4
  10.5 0.0 copy-start
  10.5 1.0 pad_maximum_fusion.1
  11.5 0.0 all-gather.5.cloned.1.call-update
  11.5 0.0 all-gather.7.cloned.1.call-start
  11.6 0.7 slice.32
  12.3 1.7 slice.33
  14.1 0.0 copy-done
  14.1 1.9 copy.20
  16.0 0.0 copy-start.9
  16.0 1.9 copy.21
  17.8 0.0 copy-done.9
  17.8 0.1 slice_reduce_fusion
  17.9 0.6 broadcast_in_dim.20
  18.5 2.9 pad.4
  21.5 1.2 reshape.16
  22.7 1.9 copy.30
  24.6 0.0 copy-start.5
  24.6 0.0 copy-start.6
  24.6 0.0 copy-start.2
  24.6 0.0 copy-start.3
  24.6 4.2 copy.15
  28.9 0.0 copy-done.5
  28.9 0.0 copy-done.6
  28.9 0.9 pad_maximum_fusion.2.w_ref
  29.8 0.0 copy-done.2
  29.8 0.0 copy-done.3
  29.8 0.1 slice_bitcast_fusion
  29.9 0.0 copy-start.7
  30.0 0.0 copy-start.8
  30.0 1.3 pad_maximum_fusion
  31.2 0.0 copy-done.7
  31.2 0.7 slice_bitcast_fusion.2
  31.9 2.0 broadcast_in_dim.19.nw_ref
  33.9 0.0 copy-done.8
  33.9 1.9 broadcast_in_dim.21.nw_ref
  35.8 130.1 %first_exchange.1 = (bf16[8,8,512,256]{3,2,1,0:T(8,128)(2,1)}, bf16[4,4096,512]{2,1,0:T(8,128)(2,1)}, bf16[16,80,4096]{2,1,0:T(8,128)(2,1)}, s32[8,2,4,256]{3,2,...) custom-call(bf16[8,512,256]{2,1,0:T(8,128)(2,1)} %bitcast.48, ...), custom_call_target="tpu_custom_call" | custom-call | flops 120000004096 | bytes 10000000 | tf_op jit(solution)/shard_map/first_exchange/pallas_call | solution.py:293
  166.0 0.0 all-gather.7.cloned.1.call-update
  166.0 0.0 all-gather.5.cloned.1.call-done
  166.0 94.1 %up_proj.1 = (bf16[8,4,704,256]{3,2,1,0:T(8,128)(2,1)}, f32[8,16,256]{2,1,0:T(8,128)}, bf16[16,512,768]{2,1,0:T(8,128)(2,1)}) custom-call(bf16[4,4096,512]{2,1,0:T(8,128)(2,1)} %get-tuple-element.37.h_ref, s32[8,2,4,256]{3,2,1,0:T(4,128)} %get-tuple-element.38.idx_ref, bf16[16,4096]{1,0:T(8,128)(2,1)} %get-tuple-element.39.rt_hbm, ...), custom_call_target="tpu_custom_call", output_to_operand_aliasing={{2}: (3, {})} | custom-call | flops 70000001024 | bytes 10000000 | tf_op jit(solution)/shard_map/up_proj/pallas_call | solution.py:439
  260.2 94.5 %down_mid.1 = (bf16[8,8,512,256]{3,2,1,0:T(8,128)(2,1)}, bf16[4,4096,512]{2,1,0:T(8,128)(2,1)}, bf16[16,512,768]{2,1,0:T(8,128)(2,1)}) custom-call(bf16[8,4,704,256]{3,2,1,0:T(8,128)(2,1)} %get-tuple-element.42.a_ref, s32[8,2,4,256]{3,2,1,0:T(4,128)} %get-tuple-element.38.idx_ref, f32[8,16,256]{2,1,0:T(8,128)} %get-tuple-element.43.g_ref, ...), custom_call_target="tpu_custom_call" | custom-call | flops 80000000000 | bytes 10000000 | tf_op jit(solution)/shard_map/down_mid/pallas_call | solution.py:544
  354.7 0.0 all-gather.7.cloned.1.call-done
  354.7 120.1 %last_layer.1 = (bf16[8,512,256]{2,1,0:T(8,128)(2,1)}, bf16[8,4,704,256]{3,2,1,0:T(8,128)(2,1)}, bf16[16,512,768]{2,1,0:T(8,128)(2,1)}) custom-call(bf16[4,4096,512]{2,1,0:T(8,128)(2,1)} %get-tuple-element.48.h_ref, s32[8,2,4,256]{3,2,1,0:T(4,128)} %get-tuple-element.38.idx_ref, ...), custom_call_target="tpu_custom_call", output_to_operand_aliasing={{2}: (3, {})} | custom-call | flops 109999996928 | bytes 10000000 | tf_op jit(solution)/shard_map/last_layer/pallas_call | solution.py:734
  474.8 4.1 copy.22
  (4 shorter events, 0.1 us)
Async XLA Ops:
  6.5 2.3 copy-start.1
  6.5 159.5 %all-gather.5.cloned.1.call-start = ((), (), s32[]{:S(2)}) async-start(), calls=%async_computation | async-start | bytes 13369344 | tf_op jit(solution)/shard_map/all_gather | solution.py:770
  9.6 0.9 copy-start.4
  10.5 3.6 copy-start
  11.5 343.2 %all-gather.7.cloned.1.call-start = ((), (), s32[]{:S(2)}) async-start(), calls=%async_computation.1 | async-start | bytes 24510464 | tf_op jit(solution)/shard_map/all_gather | solution.py:778
  16.0 1.9 copy-start.9
  24.6 4.3 copy-start.5
  24.6 4.3 copy-start.6
  24.6 5.2 %copy-start.2 = (bf16[2,1,4096,86]{2,3,1,0:T(8,128)(2,1)S(1)}, bf16[2,1,4096,86]{2,3,1,0:T(8,128)(2,1)}, u32[]{:S(2)}) copy-start(bf16[2,1,4096,86]{2,3,1,0:T(8,128)(2,1)} %copy.20) | copy-start | bytes 4227076
  24.6 5.2 %copy-start.3 = (bf16[2,1,4096,86]{2,3,1,0:T(8,128)(2,1)S(1)}, bf16[2,1,4096,86]{2,3,1,0:T(8,128)(2,1)}, u32[]{:S(2)}) copy-start(bf16[2,1,4096,86]{2,3,1,0:T(8,128)(2,1)} %copy.21) | copy-start | bytes 4227076
  29.9 1.3 copy-start.7
  30.0 4.0 copy-start.8
Sparse Core Ops, SparseCore 0:
  11.7 131.0 all-gather.4
  166.1 186.8 all-gather.6
